TPU v7x, 32 devices: a whole 2x2x4 slice. The times are simulated.
32 devices in a mesh: surf: 32 (over z, y, x, core).
Axes of the slice: x: 2, y: 2, z: 4, core: 2. Of those that a mesh axis runs over, the one named last changes fastest.
Arguments:
- excitation: float32 [2, 16384, 256], P(None, 'surf'), may hold values from -6 to 6
- leaf_basis: bfloat16 [2, 8192, 512], P(None, 'surf'), may hold values from -0.1875 to 0.1875
- self_transfer: bfloat16 [3, 2, 8192, 256], P(None, None, 'surf'), may hold values from -0.1875 to 0.1875
- cross_transfer: bfloat16 [3, 2, 8192, 256], P(None, None, 'surf'), may hold values from -0.1875 to 0.1875
- out_basis: bfloat16 [2, 16384, 256], P(None, 'surf'), may hold values from -0.25 to 0.25
- near_tiles: bfloat16 [192, 2, 128, 128], P('surf'), may hold values from -0.375 to 0.375
- near_list: int32 [32, 6, 3], replicated, may hold values from -1 to 31, as said below
Outputs:
- response: float32 [2, 16384, 256], P(None, 'surf')
Inputs may be any that keep to these rules, and one draw needn't show every extreme that they name: `near_list`: row i lists patch i's near tiles as (owner, row tile, column tile). An owner is i - 1, i or i + 1 modulo 32, or -1 for an empty slot; empty slots come last and hold 0 for both tiles. Every patch has at least one tile and some patch fills all 6 slots. From one neighbouring patch a patch lists at most 2 distinct column tiles, and some patch reaches 2.
All inputs are finite; a program needn't handle non-finite values.
Results may differ from a plain program's by a relative error of at most 0.0051.
Values may be sent and summed in bfloat16 or wider, within the bound.
No kernel may reach another device: no remote copies, remote signals or barrier semaphores. Data moves between devices by JAX's collectives and lax.ppermute only.
A program may use at most 64 MiB of HBM per device.

v0:
```python
import jax
import jax.numpy as jnp
from jax import lax
from jax.sharding import PartitionSpec as P


def from_partner(x, axis, apart):
    return lax.ppermute(x, axis, [(i, i ^ 1 << apart) for i in range(lax.axis_size(axis))])


def extended(block, sides, width):
    for axis, dim in sides:
        count = lax.axis_size(axis)
        forward = [(i, i + 1) for i in range(count - 1)]
        forward.append((count - 1, 0))
        backward = [(target, source) for source, target in forward]
        low = lax.ppermute(
            lax.slice_in_dim(block, block.shape[dim] - width, None, axis=dim), axis, forward
        )
        high = lax.ppermute(lax.slice_in_dim(block, 0, width, axis=dim), axis, backward)
        block = jnp.concatenate([low, block, high], axis=dim)
    return block


def cmat(matrix, vector):
    real = jnp.dot(matrix[0], vector[0], preferred_element_type=jnp.float32) - jnp.dot(
        matrix[1], vector[1], preferred_element_type=jnp.float32
    )
    imag = jnp.dot(matrix[0], vector[1], preferred_element_type=jnp.float32) + jnp.dot(
        matrix[1], vector[0], preferred_element_type=jnp.float32
    )
    return jnp.stack([real, imag])


def per_device(
    excitation, leaf_basis, self_transfer, cross_transfer, out_basis, near_tiles, near_list
):
    xb = excitation.astype(jnp.bfloat16)
    rows = xb.shape[1]
    width = xb.shape[2]
    tile = near_tiles.shape[2]
    blocks = rows // tile
    coef = cmat(leaf_basis, xb).astype(jnp.bfloat16)
    for level in range(self_transfer.shape[0]):
        exchange_partner = from_partner(coef, "surf", level)
        coef = (
            cmat(self_transfer[level], coef) + cmat(cross_transfer[level], exchange_partner)
        ).astype(jnp.bfloat16)
    far = cmat(out_basis, coef)
    tile_count = lax.axis_size("surf")
    here = lax.axis_index("surf")
    mine = lax.dynamic_index_in_dim(near_list, here, 0, keepdims=False)
    owner = mine[:, 0]
    row_tile = mine[:, 1]
    column = mine[:, 2]
    valid = (owner >= 0).astype(jnp.float32)
    side = jnp.where(owner >= 0, (owner - here + 1) % tile_count, 1)
    wide = extended(xb, (("surf", 1),), rows)
    window = wide.reshape(2, 3 * blocks, tile, width)
    place = side * blocks + column
    block_ids = jnp.arange(blocks, dtype=jnp.int32)
    near = jnp.zeros((2, blocks, tile, width), jnp.float32)
    for slot in range(near_tiles.shape[0]):
        block = lax.dynamic_index_in_dim(window, place[slot], 1, keepdims=False)
        term = cmat(near_tiles[slot], block) * valid[slot]
        hit = (block_ids == row_tile[slot]).astype(jnp.float32)
        near = near + term[:, None] * hit[None, :, None, None]
    return far + near.reshape(2, rows, width)


def solution(mesh):
    placed = (
        P(None, "surf", None),
        P(None, "surf", None),
        P(None, None, "surf", None),
        P(None, None, "surf", None),
        P(None, "surf", None),
        P("surf", None, None, None),
        P(),
    )
    return jax.shard_map(
        per_device, mesh=mesh, in_specs=placed, out_specs=P(None, "surf", None), check_vma=False
    )
```

profile of v0, /device:TPU:0, one launch (start us, length us, event | category | flops | bytes accessed | tf_op | source)
XLA Modules:
  0.0 84.4 jit_solution(15669492883442702821)
XLA Ops:
  0.0 1.3 %convert_element_type.58 = bf16[2,512,256]{2,1,0:T(8,128)(2,1)S(1)} convert(f32[2,512,256]{2,1,0:T(8,128)} %param.7) | non-fusion elementwise | flops 262144 | bytes 1572864 | tf_op jit(solution)/shard_map/convert_element_type | solution.py:38
  1.9 6.0 %collective-permute-start.4 = (bf16[2,512,256]{2,1,0:T(8,128)(2,1)S(1)}, bf16[2,512,256]{2,1,0:T(8,128)(2,1)}, u32[]{:S(2)}, u32[]{:S(2)}) collective-permute-start(bf16[2,512,256]{2,1,0:T(8,128)(2,1)S(1)} %convert_element_type.58), channel_id=1, source_target_pairs={{1,0},{2,1},{3,2},{4,3},{5,4},{6,5},{7,6},{8,7},{9,8},{10,9},{11,1... | collective-permute-start | bytes 1572872 | tf_op jit(solution)/shard_map/ppermute | solution.py:20
  9.7 0.7 fusion.196
  10.4 0.7 fusion.198
  11.0 0.7 fusion.197
  15.3 0.7 broadcast_bitcast_fusion
  15.9 0.7 broadcast_bitcast_fusion.2
  16.6 0.7 compare_convert_fusion.5
  28.3 0.7 broadcast_bitcast_fusion.4
  31.0 1.4 %pad_maximum_fusion = bf16[2,1536,256]{2,1,0:T(8,128)(2,1)S(1)} fusion(bf16[2,512,256]{2,1,0:T(8,128)(2,1)} %collective-permute-done.4, bf16[2,512,256]{2,1,0:T(8,128)(2,1)S(1)} %convert_element_type.58, bf16[2,512,256]{2,1,0:T(8,128)(2,1)} %collective-permute-done.3), kind=kLoop, calls=%fused_computation | loop fusion | flops 4718592 | bytes 3145728 | tf_op jit(solution)/shard_map/concatenate | solution.py:21
  33.0 0.9 %fusion.118 = f32[256,128]{1,0:T(8,128)} fusion(bf16[2,12,128,256]{3,2,1,0:T(8,128)(2,1)S(1)} %bitcast.412, s32[]{:T(128)S(6)} %add.198, s32[]{:T(128)S(6)} %select_n.38, bf16[6,2,128,128]{3,2,1,0:T(8,128)(2,1)S(1)} %copy-done.12), kind=kOutput, calls=%fused_computation.184 | convolution fusion | flops 8388608 | bytes 229384 | tf_op jit(solution)/shard_map/dot_general | solution.py:26
  33.8 0.8 fusion.113
  34.7 0.8 fusion.119
  35.5 0.8 fusion.114
  36.3 0.8 fusion.120
  37.2 0.8 fusion.115
  38.0 0.8 fusion.121
  38.9 0.9 %fusion.116 = f32[256,128]{1,0:T(8,128)} fusion(bf16[2,12,128,256]{3,2,1,0:T(8,128)(2,1)S(1)} %bitcast.419, s32[]{:T(128)S(6)} %select_n.42, bf16[6,2,128,128]{3,2,1,0:T(8,128)(2,1)S(1)} %copy-done.12), kind=kOutput, calls=%fused_computation.182 | convolution fusion | flops 8388608 | bytes 229380 | tf_op jit(solution)/shard_map/dot_general | solution.py:29
  41.0 0.9 %fusion.61 = f32[256,256]{1,0:T(8,128)} fusion(bf16[2,256,256]{1,2,0:T(8,128)(2,1)S(1)} %fusion.29, bf16[3,2,256,256]{3,2,1,0:T(8,128)(2,1)S(1)} %copy-done.6), kind=kOutput, calls=%fused_computation.115 | convolution fusion | flops 33554432 | bytes 524288 | tf_op jit(solution)/shard_map/dot_general | solution.py:26
  42.0 0.9 %fusion.59 = f32[256,256]{1,0:T(8,128)} fusion(bf16[2,256,256]{1,2,0:T(8,128)(2,1)S(1)} %fusion.29, bf16[3,2,256,256]{3,2,1,0:T(8,128)(2,1)S(1)} %copy-done.6), kind=kOutput, calls=%fused_computation.113 | convolution fusion | flops 33554432 | bytes 524288 | tf_op jit(solution)/shard_map/dot_general | solution.py:29
  43.3 0.7 maximum_multiply_fusion
  44.0 1.2 %mul.186 = f32[2,4,128,256]{2,1,3,0:T(4,128)} broadcast(f32[2,128,256]{1,2,0:T(8,128)S(1)} %maximum_multiply_fusion), dimensions={0,2,3} | broadcast | bytes 1310720 | tf_op jit(solution)/shard_map/mul | solution.py:67
  45.2 1.6 %mul.187 = f32[2,512,256]{1,2,0:T(8,128)S(1)} reshape(f32[2,4,128,256]{2,1,3,0:T(4,128)} %mul.186) | data formatting | bytes 2097152 | tf_op jit(solution)/shard_map/mul | solution.py:67
  47.0 1.1 %fusion.25 = f32[1,128,256]{1,2,0:T(8,128)S(1)} fusion(f32[256,128]{1,0:T(8,128)} %fusion.118, bf16[2,12,128,256]{3,2,1,0:T(8,128)(2,1)S(1)} %bitcast.424, s32[]{:T(128)S(6)} %select_n.38, bf16[6,2,128,128]{3,2,1,0:T(8,128)(2,1)S(1)} %copy-done.13), kind=kOutput, calls=%fused_computation.52 | convolution fusion | flops 8421376 | bytes 360452 | tf_op jit(solution)/shard_map/dot_general | solution.py:26
  48.1 0.7 maximum_multiply_fusion.1
  48.8 1.2 %mul.194 = f32[2,4,128,256]{2,1,3,0:T(4,128)} broadcast(f32[2,128,256]{1,2,0:T(8,128)S(1)} %maximum_multiply_fusion.1), dimensions={0,2,3} | broadcast | bytes 1310720 | tf_op jit(solution)/shard_map/mul | solution.py:67
  49.9 2.6 %mul.195 = f32[2,512,256]{1,2,0:T(8,128)} reshape(f32[2,4,128,256]{2,1,3,0:T(4,128)} %mul.194) | data formatting | bytes 2097152 | tf_op jit(solution)/shard_map/mul | solution.py:67
  52.8 1.1 %fusion.23 = f32[1,128,256]{1,2,0:T(8,128)S(1)} fusion(f32[256,128]{1,0:T(8,128)} %fusion.119, bf16[2,12,128,256]{3,2,1,0:T(8,128)(2,1)S(1)} %bitcast.426, s32[]{:T(128)S(6)} %select_n.39, bf16[6,2,128,128]{3,2,1,0:T(8,128)(2,1)S(1)} %copy-done.13), kind=kOutput, calls=%fused_computation.48 | convolution fusion | flops 8421376 | bytes 360452 | tf_op jit(solution)/shard_map/dot_general | solution.py:26
  53.9 0.7 maximum_multiply_fusion.2
  54.5 1.2 %mul.202 = f32[2,4,128,256]{2,1,3,0:T(4,128)} broadcast(f32[2,128,256]{1,2,0:T(8,128)S(1)} %maximum_multiply_fusion.2), dimensions={0,2,3} | broadcast | bytes 1310720 | tf_op jit(solution)/shard_map/mul | solution.py:67
  55.7 2.6 %mul.203 = f32[2,512,256]{1,2,0:T(8,128)} reshape(f32[2,4,128,256]{2,1,3,0:T(4,128)} %mul.202) | data formatting | bytes 2097152 | tf_op jit(solution)/shard_map/mul | solution.py:67
  58.5 1.1 %fusion.21 = f32[1,128,256]{1,2,0:T(8,128)S(1)} fusion(f32[256,128]{1,0:T(8,128)} %fusion.120, bf16[2,12,128,256]{3,2,1,0:T(8,128)(2,1)S(1)} %bitcast.428, s32[]{:T(128)S(6)} %select_n.40, bf16[6,2,128,128]{3,2,1,0:T(8,128)(2,1)S(1)} %copy-done.13), kind=kOutput, calls=%fused_computation.44 | convolution fusion | flops 8421376 | bytes 360452 | tf_op jit(solution)/shard_map/dot_general | solution.py:26
  59.6 0.7 maximum_multiply_fusion.3
  60.3 1.2 %mul.210 = f32[2,4,128,256]{2,1,3,0:T(4,128)} broadcast(f32[2,128,256]{1,2,0:T(8,128)S(1)} %maximum_multiply_fusion.3), dimensions={0,2,3} | broadcast | bytes 1310720 | tf_op jit(solution)/shard_map/mul | solution.py:67
  61.4 2.6 %mul.211 = f32[2,512,256]{1,2,0:T(8,128)} reshape(f32[2,4,128,256]{2,1,3,0:T(4,128)} %mul.210) | data formatting | bytes 2097152 | tf_op jit(solution)/shard_map/mul | solution.py:67
  64.3 1.1 %fusion.19 = f32[1,128,256]{1,2,0:T(8,128)S(1)} fusion(f32[256,128]{1,0:T(8,128)} %fusion.121, bf16[2,12,128,256]{3,2,1,0:T(8,128)(2,1)S(1)} %bitcast.430, s32[]{:T(128)S(6)} %select_n.41, bf16[6,2,128,128]{3,2,1,0:T(8,128)(2,1)S(1)} %copy-done.13), kind=kOutput, calls=%fused_computation.40 | convolution fusion | flops 8421376 | bytes 360452 | tf_op jit(solution)/shard_map/dot_general | solution.py:26
  65.4 0.7 maximum_multiply_fusion.4
  66.0 1.2 %mul.218 = f32[2,4,128,256]{2,1,3,0:T(4,128)} broadcast(f32[2,128,256]{1,2,0:T(8,128)S(1)} %maximum_multiply_fusion.4), dimensions={0,2,3} | broadcast | bytes 1310720 | tf_op jit(solution)/shard_map/mul | solution.py:67
  67.2 2.6 %mul.219 = f32[2,512,256]{1,2,0:T(8,128)} reshape(f32[2,4,128,256]{2,1,3,0:T(4,128)} %mul.218) | data formatting | bytes 2097152 | tf_op jit(solution)/shard_map/mul | solution.py:67
  71.0 1.4 %mul.227 = f32[2,512,256]{1,2,0:T(8,128)} reshape(f32[2,4,128,256]{2,1,3,0:T(4,128)S(1)} %mul.226) | data formatting | bytes 2097152 | tf_op jit(solution)/shard_map/mul | solution.py:67
  72.4 1.2 %fusion.5 = f32[1,256,256]{1,2,0:T(8,128)S(1)} fusion(f32[256,256]{1,0:T(8,128)} %fusion.61, bf16[2,256,256]{1,2,0:T(8,128)(2,1)S(1)} %fusion.29, bf16[3,2,256,256]{3,2,1,0:T(8,128)(2,1)} %param.9), kind=kOutput, calls=%fused_computation.12 | convolution fusion | flops 33619968 | bytes 786432 | tf_op jit(solution)/shard_map/dot_general | solution.py:26
  73.7 1.2 %fusion.4 = f32[1,256,256]{1,2,0:T(8,128)S(1)} fusion(f32[256,256]{1,0:T(8,128)} %fusion.59, bf16[2,256,256]{1,2,0:T(8,128)(2,1)S(1)} %fusion.29, bf16[3,2,256,256]{3,2,1,0:T(8,128)(2,1)} %param.9), kind=kOutput, calls=%fused_computation.10 | convolution fusion | flops 33619968 | bytes 786432 | tf_op jit(solution)/shard_map/dot_general | solution.py:29
  75.0 1.1 %fusion.53 = f32[256,256]{1,0:T(8,128)S(1)} fusion(bf16[2,256,256]{1,2,0:T(8,128)(2,1)} %collective-permute-done.2, bf16[3,2,256,256]{3,2,1,0:T(8,128)(2,1)S(1)} %copy-done.9), kind=kOutput, calls=%fused_computation.107 | convolution fusion | flops 33554432 | bytes 524288 | tf_op jit(solution)/shard_map/dot_general | solution.py:26
  76.1 1.2 %fusion.51 = f32[256,256]{1,0:T(8,128)S(1)} fusion(bf16[2,256,256]{1,2,0:T(8,128)(2,1)} %collective-permute-done.2, bf16[3,2,256,256]{3,2,1,0:T(8,128)(2,1)S(1)} %copy-done.9), kind=kOutput, calls=%fused_computation.105 | convolution fusion | flops 33554432 | bytes 524288 | tf_op jit(solution)/shard_map/dot_general | solution.py:29
  77.3 1.1 %fusion.3 = f32[1,256,256]{1,2,0:T(8,128)S(1)} fusion(f32[256,256]{1,0:T(8,128)S(1)} %fusion.53, bf16[2,256,256]{1,2,0:T(8,128)(2,1)} %collective-permute-done.2, bf16[3,2,256,256]{3,2,1,0:T(8,128)(2,1)S(1)} %copy-done.9), kind=kOutput, calls=%fused_computation.8 | convolution fusion | flops 33619968 | bytes 786432 | tf_op jit(solution)/shard_map/dot_general | solution.py:26
  78.4 1.1 %fusion.2 = f32[1,256,256]{1,2,0:T(8,128)S(1)} fusion(f32[256,256]{1,0:T(8,128)S(1)} %fusion.51, bf16[2,256,256]{1,2,0:T(8,128)(2,1)} %collective-permute-done.2, bf16[3,2,256,256]{3,2,1,0:T(8,128)(2,1)S(1)} %copy-done.9), kind=kOutput, calls=%fused_computation.6 | convolution fusion | flops 33619968 | bytes 786432 | tf_op jit(solution)/shard_map/dot_general | solution.py:29
  82.2 0.9 %maximum_add_fusion = f32[2,512,256]{1,2,0:T(8,128)S(1)} fusion(f32[1,512,256]{1,2,0:T(8,128)S(1)} %fusion, f32[1,512,256]{1,2,0:T(8,128)S(1)} %fusion.1, f32[2,512,256]{1,2,0:T(8,128)S(1)} %copy-done.5, f32[2,512,256]{1,2,0:T(8,128)S(1)} %copy-done.4, f32[2,512,256]{1,2,0:T(8,128)S(1)} %copy-done.3, f32[2,512,256]{1,2,0:T(8,128)S(1)} %copy-done.2, ...), kind=kLoop, calls=%fused_computation.57 | loop fusion | flops 3407872 | bytes 8400896 | tf_op jit(solution)/shard_map/add | solution.py:68
  83.1 1.3 %copy.9 = f32[2,512,256]{2,1,0:T(8,128)} copy(f32[2,512,256]{1,2,0:T(8,128)S(1)} %maximum_add_fusion) | data formatting | bytes 2097152 | tf_op jit(solution)/shard_map/add | solution.py:68
  (106 shorter events, 14.5 us)
Async XLA Ops:
  0.0 8.9 %copy-start = (s32[32,6,3]{0,2,1:T(4,128)S(1)}, s32[32,6,3]{0,2,1:T(4,128)}, u32[]{:S(2)}) copy-start(s32[32,6,3]{0,2,1:T(4,128)} %param.13) | copy-start | bytes 6916
  0.0 7.9 %copy-start.10 = (bf16[2,256,512]{2,1,0:T(8,128)(2,1)S(1)}, bf16[2,256,512]{2,1,0:T(8,128)(2,1)}, u32[]{:S(2)}) copy-start(bf16[2,256,512]{2,1,0:T(8,128)(2,1)} %param.8) | copy-start | bytes 1572868
  1.3 29.6 %collective-permute-start.3 = (bf16[2,512,256]{2,1,0:T(8,128)(2,1)S(1)}, bf16[2,512,256]{2,1,0:T(8,128)(2,1)}, u32[]{:S(2)}, u32[]{:S(2)}) collective-permute-start(bf16[2,512,256]{2,1,0:T(8,128)(2,1)S(1)} %convert_element_type.58), channel_id=1, source_target_pairs={{0,1},{1,2},{2,3},{3,4},{4,5},{5,6},{6,7},{7,8},{8,9},{9,10},{10,1... | collective-permute-start | bytes 1572872 | tf_op jit(solution)/shard_map/ppermute | solution.py:17
  1.9 29.1 %collective-permute-start.4 = (bf16[2,512,256]{2,1,0:T(8,128)(2,1)S(1)}, bf16[2,512,256]{2,1,0:T(8,128)(2,1)}, u32[]{:S(2)}, u32[]{:S(2)}) collective-permute-start(bf16[2,512,256]{2,1,0:T(8,128)(2,1)S(1)} %convert_element_type.58), channel_id=1, source_target_pairs={{1,0},{2,1},{3,2},{4,3},{5,4},{6,5},{7,6},{8,7},{9,8},{10,9},{11,1... | collective-permute-start | bytes 1572872 | tf_op jit(solution)/shard_map/ppermute | solution.py:20
  8.1 1.1 %copy-start.6 = (bf16[3,2,256,256]{3,2,1,0:T(8,128)(2,1)S(1)}, bf16[3,2,256,256]{3,2,1,0:T(8,128)(2,1)}, u32[]{:S(2)}) copy-start(bf16[3,2,256,256]{3,2,1,0:T(8,128)(2,1)} %param.9) | copy-start | bytes 2359300
  8.8 20.1 %copy-start.7 = (bf16[3,2,256,256]{3,2,1,0:T(8,128)(2,1)S(1)}, bf16[3,2,256,256]{3,2,1,0:T(8,128)(2,1)}, u32[]{:S(2)}) copy-start(bf16[3,2,256,256]{3,2,1,0:T(8,128)(2,1)} %param.10) | copy-start | bytes 2359300
  8.9 20.1 %collective-permute-start = (bf16[2,256,256]{2,1,0:T(8,128)(2,1)S(1)}, bf16[2,256,256]{2,1,0:T(8,128)(2,1)S(1)}, u32[]{:S(2)}, u32[]{:S(2)}) collective-permute-start(bf16[2,256,256]{2,1,0:T(8,128)(2,1)S(1)} %pad_maximum_fusion.1), channel_id=1, source_target_pairs={{0,1},{1,0},{2,3},{3,2},{4,5},{5,4},{6,7},{7,6},{8,9},{9,8},{10,11... | collective-permute-start | bytes 786440 | tf_op jit(solution)/shard_map/ppermute | solution.py:8
  30.0 10.0 %collective-permute-start.1 = (bf16[2,256,256]{1,2,0:T(8,128)(2,1)S(1)}, bf16[2,256,256]{1,2,0:T(8,128)(2,1)S(1)}, u32[]{:S(2)}, u32[]{:S(2)}) collective-permute-start(bf16[2,256,256]{1,2,0:T(8,128)(2,1)S(1)} %fusion.28), channel_id=1, source_target_pairs={{0,2},{1,3},{2,0},{3,1},{4,6},{5,7},{6,4},{7,5},{8,10},{9,11},{10,... | collective-permute-start | bytes 786440 | tf_op jit(solution)/shard_map/ppermute | solution.py:8
  30.9 1.4 %copy-start.12 = (bf16[6,2,128,128]{3,2,1,0:T(8,128)(2,1)S(1)}, bf16[6,2,128,128]{3,2,1,0:T(8,128)(2,1)}, u32[]{:S(2)}) copy-start(bf16[6,2,128,128]{3,2,1,0:T(8,128)(2,1)} %param.12) | copy-start | bytes 1179652
  32.3 7.6 %copy-start.8 = (bf16[3,2,256,256]{3,2,1,0:T(8,128)(2,1)S(1)}, bf16[3,2,256,256]{3,2,1,0:T(8,128)(2,1)}, u32[]{:S(2)}) copy-start(bf16[3,2,256,256]{3,2,1,0:T(8,128)(2,1)} %param.10) | copy-start | bytes 2359300
  40.9 34.0 %collective-permute-start.2 = (bf16[2,256,256]{1,2,0:T(8,128)(2,1)S(1)}, bf16[2,256,256]{1,2,0:T(8,128)(2,1)}, u32[]{:S(2)}, u32[]{:S(2)}) collective-permute-start(bf16[2,256,256]{1,2,0:T(8,128)(2,1)S(1)} %fusion.29), channel_id=1, source_target_pairs={{0,4},{1,5},{2,6},{3,7},{4,0},{5,1},{6,2},{7,3},{8,12},{9,13},{10,... | collective-permute-start | bytes 786440 | tf_op jit(solution)/shard_map/ppermute | solution.py:8
  44.0 2.8 %copy-start.13 = (bf16[6,2,128,128]{3,2,1,0:T(8,128)(2,1)S(1)}, bf16[6,2,128,128]{3,2,1,0:T(8,128)(2,1)}, u32[]{:S(2)}) copy-start(bf16[6,2,128,128]{3,2,1,0:T(8,128)(2,1)} %param.12) | copy-start | bytes 1179652
  48.8 3.8 %copy-start.17 = (f32[256,128]{1,0:T(8,128)S(1)}, f32[256,128]{1,0:T(8,128)}, u32[]{:S(2)}) copy-start(f32[256,128]{1,0:T(8,128)} %fusion.113) | copy-start | bytes 393220
  54.5 3.8 %copy-start.16 = (f32[256,128]{1,0:T(8,128)S(1)}, f32[256,128]{1,0:T(8,128)}, u32[]{:S(2)}) copy-start(f32[256,128]{1,0:T(8,128)} %fusion.114) | copy-start | bytes 393220
  60.3 3.8 %copy-start.15 = (f32[256,128]{1,0:T(8,128)S(1)}, f32[256,128]{1,0:T(8,128)}, u32[]{:S(2)}) copy-start(f32[256,128]{1,0:T(8,128)} %fusion.115) | copy-start | bytes 393220
  66.0 3.8 %copy-start.14 = (f32[256,128]{1,0:T(8,128)S(1)}, f32[256,128]{1,0:T(8,128)}, u32[]{:S(2)}) copy-start(f32[256,128]{1,0:T(8,128)} %fusion.116) | copy-start | bytes 393220
  71.0 3.9 %copy-start.9 = (bf16[3,2,256,256]{3,2,1,0:T(8,128)(2,1)S(1)}, bf16[3,2,256,256]{3,2,1,0:T(8,128)(2,1)}, u32[]{:S(2)}) copy-start(bf16[3,2,256,256]{3,2,1,0:T(8,128)(2,1)} %param.10) | copy-start | bytes 2359300
  76.1 3.6 %copy-start.11 = (bf16[2,512,256]{2,1,0:T(8,128)(2,1)S(1)}, bf16[2,512,256]{2,1,0:T(8,128)(2,1)}, u32[]{:S(2)}) copy-start(bf16[2,512,256]{2,1,0:T(8,128)(2,1)} %param.11) | copy-start | bytes 1572868
  79.5 1.3 %copy-start.5 = (f32[2,512,256]{1,2,0:T(8,128)S(1)}, f32[2,512,256]{1,2,0:T(8,128)}, u32[]{:S(2)}) copy-start(f32[2,512,256]{1,2,0:T(8,128)} %mul.227) | copy-start | bytes 3145732
  79.6 1.5 %copy-start.4 = (f32[2,512,256]{1,2,0:T(8,128)S(1)}, f32[2,512,256]{1,2,0:T(8,128)}, u32[]{:S(2)}) copy-start(f32[2,512,256]{1,2,0:T(8,128)} %mul.219) | copy-start | bytes 3145732
  79.9 1.6 %copy-start.3 = (f32[2,512,256]{1,2,0:T(8,128)S(1)}, f32[2,512,256]{1,2,0:T(8,128)}, u32[]{:S(2)}) copy-start(f32[2,512,256]{1,2,0:T(8,128)} %mul.211) | copy-start | bytes 3145732
  80.2 1.7 %copy-start.1 = (f32[2,512,256]{1,2,0:T(8,128)S(1)}, f32[2,512,256]{1,2,0:T(8,128)}, u32[]{:S(2)}) copy-start(f32[2,512,256]{1,2,0:T(8,128)} %mul.195) | copy-start | bytes 3145732
  80.2 2.0 %copy-start.2 = (f32[2,512,256]{1,2,0:T(8,128)S(1)}, f32[2,512,256]{1,2,0:T(8,128)}, u32[]{:S(2)}) copy-start(f32[2,512,256]{1,2,0:T(8,128)} %mul.203) | copy-start | bytes 3145732
  80.2 2.0 %copy-start.18 = (f32[512]{0:T(512)S(1)}, f32[512]{0:T(512)}, u32[]{:S(2)}) copy-start(f32[512]{0:T(512)} %get-tuple-element.24) | copy-start | bytes 6148
  80.2 2.0 %copy-start.19 = (f32[512]{0:T(512)S(1)}, f32[512]{0:T(512)}, u32[]{:S(2)}) copy-start(f32[512]{0:T(512)} %get-tuple-element.25) | copy-start | bytes 6148
  80.2 2.0 %copy-start.20 = (f32[512]{0:T(512)S(1)}, f32[512]{0:T(512)}, u32[]{:S(2)}) copy-start(f32[512]{0:T(512)} %get-tuple-element.26) | copy-start | bytes 6148
  80.2 2.0 %copy-start.21 = (f32[512]{0:T(512)S(1)}, f32[512]{0:T(512)}, u32[]{:S(2)}) copy-start(f32[512]{0:T(512)} %get-tuple-element.27) | copy-start | bytes 6148
  80.3 1.9 %copy-start.22 = (f32[512]{0:T(512)S(1)}, f32[512]{0:T(512)}, u32[]{:S(2)}) copy-start(f32[512]{0:T(512)} %get-tuple-element.28) | copy-start | bytes 6148
where the time goes:
time: 85.3 us; the launch traced here: 84.4 us
  matrix products  27.9 us (33%)
  local copies, waits for them, and re-layouts  26.4 us (31%)
  other arithmetic  11.7 us (14%)
  between operations  11.7 us (14%)
  starting transfers between devices  6.73 us (8%)
    mul x15, local copies, waits for them, and re-layouts, per_device(): near = near + term[:, None] * hit[None, :, None, None]  21.4 us
    dot_general x14, matrix products, cmat(): jnp.dot(matrix[0], vector[0], preferred_element_type=jnp.float32)  8.23 us
    dot_general x14, matrix products, cmat(): jnp.dot(matrix[1], vector[0], preferred_element_type=jnp.float32)  7.57 us
    dot_general x14, matrix products, cmat(): jnp.dot(matrix[1], vector[1], preferred_element_type=jnp.float32)  7.5 us
    ppermute x1, starting transfers between devices, extended(): lax.ppermute(lax.slice_in_dim(block, 0, width, axis=dim), axis, backward)  5.97 us
    dot_general x14, matrix products, cmat(): jnp.dot(matrix[0], vector[1], preferred_element_type=jnp.float32)  4.6 us
    mul x6, other arithmetic, per_device(): term = cmat(near_tiles[slot], block) * valid[slot]  4.01 us
    convert_element_type x6, other arithmetic, per_device(): hit = (block_ids == row_tile[slot]).astype(jnp.float32)  3.76 us
  transfers between devices with their start and end apart: 5, of which 0 were waited for; matrix products, arithmetic and copies ran while one was open for 64% of the time, Pallas kernels for 0%

commit v1 on v0

v1 whole, which is shorter than its diff:
```python
import functools

import jax
import jax.numpy as jnp
from jax import lax
from jax.experimental import pallas as pl
from jax.experimental.pallas import tpu as pltpu
from jax.sharding import PartitionSpec as P

CHUNKS = 2
VMEM_LIMIT = 12 * 1024 * 1024

ON_CHIP = pl.BlockSpec(memory_space=pltpu.VMEM)
SCALARS = pl.BlockSpec(memory_space=pltpu.SMEM)


def call(body, name, outs, ins, args, flops, nbytes, scratch=()):
    return pl.pallas_call(
        body,
        name=name,
        out_shape=outs,
        in_specs=ins,
        out_specs=[ON_CHIP] * len(outs),
        scratch_shapes=list(scratch),
        cost_estimate=pl.CostEstimate(
            flops=flops, bytes_accessed=nbytes, transcendentals=0
        ),
        compiler_params=pltpu.CompilerParams(vmem_limit_bytes=VMEM_LIMIT),
    )(*args)


def dot(a, b):
    return jnp.dot(a, b, preferred_element_type=jnp.float32)


def complex_dot(m0, m1, v0, v1):
    return dot(m0, v0) - dot(m1, v1), dot(m0, v1) + dot(m1, v0)


def leaf_body(x_ref, leaf_ref, xb_ref, *coef_refs):
    xb_ref[...] = x_ref[...].astype(jnp.bfloat16)
    width = coef_refs[0].shape[2]
    for c, ref in enumerate(coef_refs):
        cols = slice(c * width, (c + 1) * width)
        real, imag = complex_dot(
            leaf_ref[0], leaf_ref[1], xb_ref[0, :, cols], xb_ref[1, :, cols]
        )
        ref[0] = real.astype(ref.dtype)
        ref[1] = imag.astype(ref.dtype)


def span(list_ref, reader, owner, blocks):
    low = jnp.int32(blocks - 1)
    high = jnp.int32(0)
    for slot in range(list_ref.shape[0]):
        mine = list_ref[slot, 0, reader] == owner
        column = list_ref[slot, 2, reader]
        low = jnp.minimum(low, jnp.where(mine, column, low))
        high = jnp.maximum(high, jnp.where(mine, column, high))
    return low, high


def pick_body(axis, count, list_ref, xb_ref, up_ref, down_ref):
    tile = up_ref.shape[2]
    blocks = xb_ref.shape[1] // tile
    here = lax.axis_index(axis)
    for step, ref in ((1, up_ref), (count - 1, down_ref)):
        reader = lax.rem(here + step, count)
        for k, column in enumerate(span(list_ref, reader, here, blocks)):
            rows = pl.ds(pl.multiple_of(column * tile, tile), tile)
            ref[k] = xb_ref[:, rows, :]


def own_body(level, coef_ref, self_ref, out_ref):
    real, imag = complex_dot(
        self_ref[level, 0], self_ref[level, 1], coef_ref[0], coef_ref[1]
    )
    out_ref[0] = real
    out_ref[1] = imag


def cross_body(level, own_ref, partner_ref, cross_ref, out_ref):
    real, imag = complex_dot(
        cross_ref[level, 0], cross_ref[level, 1], partner_ref[0], partner_ref[1]
    )
    out_ref[0] = (own_ref[0] + real).astype(out_ref.dtype)
    out_ref[1] = (own_ref[1] + imag).astype(out_ref.dtype)


def near_body(axis, count, list_ref, tiles_ref, xb_ref, low_ref, high_ref, near_ref):
    tile = tiles_ref.shape[2]
    blocks = xb_ref.shape[1] // tile
    here = lax.axis_index(axis)
    before = lax.rem(here + count - 1, count)
    after = lax.rem(here + 1, count)
    low_first, _ = span(list_ref, here, before, blocks)
    high_first, _ = span(list_ref, here, after, blocks)
    near_ref[...] = jnp.zeros_like(near_ref)

    def add(slot, row, v0, v1):
        real, imag = complex_dot(tiles_ref[slot, 0], tiles_ref[slot, 1], v0, v1)
        rows = pl.ds(pl.multiple_of(row * tile, tile), tile)
        near_ref[0, rows, :] += real
        near_ref[1, rows, :] += imag

    for slot in range(tiles_ref.shape[0]):
        owner = list_ref[slot, 0, here]
        row = list_ref[slot, 1, here]
        column = list_ref[slot, 2, here]

        @pl.when(owner == here)
        def _():
            rows = pl.ds(pl.multiple_of(column * tile, tile), tile)
            add(slot, row, xb_ref[0, rows, :], xb_ref[1, rows, :])

        @pl.when(jnp.logical_and(owner >= 0, owner != here))
        def _():
            below = owner == before
            first = jnp.where(below, low_first, high_first)
            k = jnp.where(column == first, 0, 1)

            @pl.when(below)
            def _():
                add(slot, row, low_ref[k, 0], low_ref[k, 1])

            @pl.when(jnp.logical_not(below))
            def _():
                add(slot, row, high_ref[k, 0], high_ref[k, 1])


def last_body(level, *refs):
    *chunks, cross_ref, out_basis_ref, near_ref, out_ref = refs
    pieces = len(chunks) // 2
    for c in range(pieces):
        own_ref, partner_ref = chunks[c], chunks[pieces + c]
        width = partner_ref.shape[2]
        real, imag = complex_dot(
            cross_ref[level, 0], cross_ref[level, 1], partner_ref[0], partner_ref[1]
        )
        v0 = (own_ref[0] + real).astype(jnp.bfloat16)
        v1 = (own_ref[1] + imag).astype(jnp.bfloat16)
        real, imag = complex_dot(out_basis_ref[0], out_basis_ref[1], v0, v1)
        cols = slice(c * width, (c + 1) * width)
        out_ref[0, :, cols] = real + near_ref[0, :, cols]
        out_ref[1, :, cols] = imag + near_ref[1, :, cols]


def per_device(
    excitation, leaf_basis, self_transfer, cross_transfer, out_basis, near_tiles, near_list
):
    axis = "surf"
    count = lax.axis_size(axis)
    rows, width = excitation.shape[1:]
    rank = leaf_basis.shape[1]
    tile = near_tiles.shape[2]
    levels = self_transfer.shape[0]
    part = width // CHUNKS
    listing = near_list.transpose(1, 2, 0)
    up = [(i, (i + 1) % count) for i in range(count)]
    down = [(i, (i - 1) % count) for i in range(count)]
    piece = pltpu.VMEM((2, rank, part), jnp.bfloat16)
    total = pltpu.VMEM((2, rank, part), jnp.float32)

    xb, *coef = call(
        leaf_body,
        "leaf",
        [pltpu.VMEM(excitation.shape, jnp.bfloat16)] + [piece] * CHUNKS,
        [ON_CHIP, ON_CHIP],
        (excitation, leaf_basis),
        8 * rank * rows * width,
        8 * rows * width,
    )
    near = None
    for level in range(levels):
        swap = [(i, i ^ (1 << level)) for i in range(count)]
        partner = [lax.ppermute(c, axis, swap) for c in coef]
        if level == 0:
            sent = pltpu.VMEM((2, 2, tile, width), jnp.bfloat16)
            to_up, to_down = call(
                functools.partial(pick_body, axis, count),
                "pick",
                [sent, sent],
                [SCALARS, ON_CHIP],
                (listing, xb),
                0,
                8 * tile * width,
            )
            low = lax.ppermute(to_up, axis, up)
            high = lax.ppermute(to_down, axis, down)
        own = [
            call(
                functools.partial(own_body, level),
                "own",
                [total],
                [ON_CHIP, ON_CHIP],
                (c, self_transfer),
                8 * rank * rank * part,
                2 * rank * rank,
            )[0]
            for c in coef
        ]
        if level == levels - 1:
            (near,) = call(
                functools.partial(near_body, axis, count),
                "near",
                [pltpu.VMEM((2, rows, width), jnp.float32)],
                [SCALARS] + [ON_CHIP] * 4,
                (listing, near_tiles, xb, low, high),
                8 * near_tiles.shape[0] * tile * tile * width,
                8 * rows * width,
            )
            break
        coef = [
            call(
                functools.partial(cross_body, level),
                "cross",
                [piece],
                [ON_CHIP] * 3,
                (own[c], partner[c], cross_transfer),
                8 * rank * rank * part,
                2 * rank * rank,
            )[0]
            for c in range(CHUNKS)
        ]
    return call(
        functools.partial(last_body, levels - 1),
        "last",
        [jax.ShapeDtypeStruct((2, rows, width), jnp.float32)],
        [ON_CHIP] * (2 * CHUNKS + 3),
        (*own, *partner, cross_transfer, out_basis, near),
        8 * rank * (rank + rows) * width,
        8 * rows * width,
    )[0]


def solution(mesh):
    placed = (
        P(None, "surf", None),
        P(None, "surf", None),
        P(None, None, "surf", None),
        P(None, None, "surf", None),
        P(None, "surf", None),
        P("surf", None, None, None),
        P(),
    )
    return jax.shard_map(
        per_device, mesh=mesh, in_specs=placed, out_specs=P(None, "surf", None), check_vma=False
    )
```

time: 85.3 us -> 30.2 us (0.35)
  matrix products: 27.9 us -> 0 us
  local copies, waits for them, and re-layouts: 26.4 us -> 3.85 us
  other arithmetic: 11.7 us -> 0 us
  between operations: 11.7 us -> 0.16 us
  Pallas kernels: 0 us -> 8.75 us
  starting transfers between devices: 6.73 us -> 13.4 us
  waiting for transfers between devices: 0.01 us -> 3.87 us
    dot_general x56 -> x0, matrix products: 27.9 us -> none  [the longest x14 8.23 us: cmat(): jnp.dot(matrix[0], vector[0], preferred_element_type=jnp.float32)]
    mul x15 -> x0, local copies, waits for them, and re-layouts: 21.4 us -> none  [per_device(): near = near + term[:, None] * hit[None, :, None, None]]
    pallas_call x0 -> x14, Pallas kernels: none -> 8.75 us  [call(): pl.pallas_call(body, name=name, out_shape=outs, in_specs=ins, out_specs=[...]
    ppermute x5 -> x8, starting transfers between devices: 6.73 us -> 13.4 us  [the longest x6 6.69 us: per_device(): partner = [lax.ppermute(c, axis, swap) for c in coef]]
    convert_element_type x11 -> x0, other arithmetic: 5.34 us -> none  [the longest x6 3.76 us: per_device(): hit = (block_ids == row_tile[slot]).astype(jnp.float32)]
    mul x6 -> x0, other arithmetic: 4.01 us -> none  [per_device(): term = cmat(near_tiles[slot], block) * valid[slot]]
    ppermute x5 -> x8, waiting for transfers between devices: 0.01 us -> 3.87 us  [the longest x6 3.86 us: per_device(): partner = [lax.ppermute(c, axis, swap) for c in coef]]
    unnamed x46 -> x14, local copies, waits for them, and re-layouts: 1.53 us -> 3.85 us
  transfers between devices with their start and end apart: 5 -> 8, of which waited for: 0 -> 2; matrix products, arithmetic and copies ran while one was open for 64% -> 0% of each run, Pallas kernels for 0% -> 19%
where the time goes in v1:
time: 30.2 us; the launch traced here: 30 us
  starting transfers between devices  13.4 us (44%)
  Pallas kernels  8.75 us (29%)
  waiting for transfers between devices  3.87 us (13%)
  local copies, waits for them, and re-layouts  3.85 us (13%)
    pallas_call x14, Pallas kernels, call(): pl.pallas_call(body, name=name, out_shape=outs, in_specs=ins, out_specs=[...  8.75 us
    ppermute x6, starting transfers between devices, per_device(): partner = [lax.ppermute(c, axis, swap) for c in coef]  6.69 us
    ppermute x1, starting transfers between devices, per_device(): high = lax.ppermute(to_down, axis, down)  6.22 us
    ppermute x6, waiting for transfers between devices, per_device(): partner = [lax.ppermute(c, axis, swap) for c in coef]  3.86 us
    unnamed x14, local copies, waits for them, and re-layouts  3.85 us
  transfers between devices with their start and end apart: 8, of which 2 were waited for; matrix products, arithmetic and copies ran while one was open for 0% of the time, Pallas kernels for 19%

profile of v1, /device:TPU:0, one launch (start us, length us, event | category | flops | bytes accessed | tf_op | source)
XLA Modules:
  0.0 30.0 jit_solution(810064495983008388)
XLA Ops:
  0.0 0.0 copy-start
  0.0 0.0 copy-start.2
  0.0 1.3 %copy-done.2 = f32[2,512,256]{2,1,0:T(8,128)S(1)} copy-done((f32[2,512,256]{2,1,0:T(8,128)S(1)}, f32[2,512,256]{2,1,0:T(8,128)}, u32[]{:S(2)}) %copy-start.2) | copy-done | bytes 1048600
  1.3 0.0 copy-start.3
  1.3 1.0 %copy-done.3 = bf16[2,256,512]{2,1,0:T(8,128)(2,1)S(1)} copy-done((bf16[2,256,512]{2,1,0:T(8,128)(2,1)S(1)}, bf16[2,256,512]{2,1,0:T(8,128)(2,1)}, u32[]{:S(2)}) %copy-start.3) | copy-done | bytes 524312
  2.3 0.0 copy-start.6
  2.3 0.7 %leaf.1 = (bf16[2,512,256]{2,1,0:T(8,128)(2,1)S(1)}, bf16[2,256,128]{2,1,0:T(8,128)(2,1)S(1)}, bf16[2,256,128]{2,1,0:T(8,128)(2,1)S(1)}) custom-call(f32[2,512,256]{2,1,0:T(8,128)S(1)} %copy-done.2, bf16[2,256,512]{2,1,0:T(8,128)(2,1)S(1)} %copy-done.3), custom_call_target="tpu_custom_call" | custom-call | flops 268435456 | bytes 1048576 | tf_op jit(solution)/shard_map/leaf/pallas_call | solution.py:18
  3.1 0.6 %collective-permute-start = (bf16[2,256,128]{2,1,0:T(8,128)(2,1)S(1)}, bf16[2,256,128]{2,1,0:T(8,128)(2,1)S(1)}, u32[]{:S(2)}, u32[]{:S(2)}) collective-permute-start(bf16[2,256,128]{2,1,0:T(8,128)(2,1)S(1)} %get-tuple-element.10.coef_ref), channel_id=1, source_target_pairs={{0,1},{1,0},{2,3},{3,2},{4,5},{5,4},{6,7},{7,6},{8,9},{9,8},{10,11... | collective-permute-start | bytes 393224 | tf_op jit(solution)/shard_map/ppermute | solution.py:176
  3.7 0.1 collective-permute-start.2
  3.7 0.0 copy-done.6
  3.7 0.8 %pick.1 = (bf16[2,2,128,256]{3,2,1,0:T(8,128)(2,1)S(1)}, bf16[2,2,128,256]{3,2,1,0:T(8,128)(2,1)S(1)}) custom-call(s32[6,3,32]{2,1,0:T(4,128)S(1)} %bitcast.1, bf16[2,512,256]{2,1,0:T(8,128)(2,1)S(1)} %get-tuple-element.12.xb_ref), custom_call_target="tpu_custom_call" | custom-call | bytes 262144 | tf_op jit(solution)/shard_map/pick/pallas_call | solution.py:18
  4.5 0.5 %collective-permute-start.6 = (bf16[2,2,128,256]{3,2,1,0:T(8,128)(2,1)S(1)}, bf16[2,2,128,256]{3,2,1,0:T(8,128)(2,1)S(1)}, u32[]{:S(2)}, u32[]{:S(2)}) collective-permute-start(bf16[2,2,128,256]{3,2,1,0:T(8,128)(2,1)S(1)} %get-tuple-element.13), channel_id=1, source_target_pairs={{0,1},{1,2},{2,3},{3,4},{4,5},{5,6},{6,7},{7,8},{8,9},{9,10},{10,1... | collective-permute-start | bytes 786440 | tf_op jit(solution)/shard_map/ppermute | solution.py:188
  5.0 6.2 %collective-permute-start.7 = (bf16[2,2,128,256]{3,2,1,0:T(8,128)(2,1)S(1)}, bf16[2,2,128,256]{3,2,1,0:T(8,128)(2,1)S(1)}, u32[]{:S(2)}, u32[]{:S(2)}) collective-permute-start(bf16[2,2,128,256]{3,2,1,0:T(8,128)(2,1)S(1)} %get-tuple-element.14), channel_id=1, source_target_pairs={{0,31},{1,0},{2,1},{3,2},{4,3},{5,4},{6,5},{7,6},{8,7},{9,8},{10,9... | collective-permute-start | bytes 786440 | tf_op jit(solution)/shard_map/ppermute | solution.py:189
  11.3 0.0 copy-done
  11.3 0.3 own.6.own_ref
  11.5 0.0 copy-start.1
  11.6 0.3 own.9.own_ref
  11.8 0.0 collective-permute-done.partner_ref
  11.9 0.8 %copy-done.1 = bf16[3,2,256,256]{3,2,1,0:T(8,128)(2,1)S(1)} copy-done((bf16[3,2,256,256]{3,2,1,0:T(8,128)(2,1)S(1)}, bf16[3,2,256,256]{3,2,1,0:T(8,128)(2,1)}, u32[]{:S(2)}) %copy-start.1) | copy-done | bytes 786456
  12.7 0.3 cross.4.coef_ref
  13.0 0.1 collective-permute-start.1
  13.0 0.0 collective-permute-done.2.partner_ref
  13.1 0.3 cross.6.coef_ref
  13.3 2.1 %collective-permute-start.3 = (bf16[2,256,128]{2,1,0:T(8,128)(2,1)S(1)}, bf16[2,256,128]{2,1,0:T(8,128)(2,1)S(1)}, u32[]{:S(2)}, u32[]{:S(2)}) collective-permute-start(bf16[2,256,128]{2,1,0:T(8,128)(2,1)S(1)} %cross.6.coef_ref), channel_id=1, source_target_pairs={{0,2},{1,3},{2,0},{3,1},{4,6},{5,7},{6,4},{7,5},{8,10},{9,11},{10,... | collective-permute-start | bytes 393224 | tf_op jit(solution)/shard_map/ppermute | solution.py:176
  15.4 0.3 own.7.own_ref
  15.7 0.3 own.10.own_ref
  16.0 3.4 %collective-permute-done.1.partner_ref = bf16[2,256,128]{2,1,0:T(8,128)(2,1)S(1)} collective-permute-done((bf16[2,256,128]{2,1,0:T(8,128)(2,1)S(1)}, bf16[2,256,128]{2,1,0:T(8,128)(2,1)S(1)}, u32[]{:S(2)}, u32[]{:S(2)}) %collective-permute-start.1) | collective-permute-done | bytes 131104 | tf_op jit(solution)/shard_map/ppermute | solution.py:176
  19.4 0.3 cross.5.coef_ref
  19.7 2.8 %collective-permute-start.4 = (bf16[2,256,128]{2,1,0:T(8,128)(2,1)S(1)}, bf16[2,256,128]{2,1,0:T(8,128)(2,1)S(1)}, u32[]{:S(2)}, u32[]{:S(2)}) collective-permute-start(bf16[2,256,128]{2,1,0:T(8,128)(2,1)S(1)} %cross.5.coef_ref), channel_id=1, source_target_pairs={{0,4},{1,5},{2,6},{3,7},{4,0},{5,1},{6,2},{7,3},{8,12},{9,13},{10,... | collective-permute-start | bytes 393224 | tf_op jit(solution)/shard_map/ppermute | solution.py:176
  22.5 0.0 collective-permute-done.3.partner_ref
  22.5 0.3 cross.7.coef_ref
  22.8 1.1 %collective-permute-start.5 = (bf16[2,256,128]{2,1,0:T(8,128)(2,1)S(1)}, bf16[2,256,128]{2,1,0:T(8,128)(2,1)S(1)}, u32[]{:S(2)}, u32[]{:S(2)}) collective-permute-start(bf16[2,256,128]{2,1,0:T(8,128)(2,1)S(1)} %cross.7.coef_ref), channel_id=1, source_target_pairs={{0,4},{1,5},{2,6},{3,7},{4,0},{5,1},{6,2},{7,3},{8,12},{9,13},{10,... | collective-permute-start | bytes 393224 | tf_op jit(solution)/shard_map/ppermute | solution.py:176
  23.9 0.3 own.8.refs_0_
  24.2 0.0 copy-start.5
  24.2 0.3 own.11.refs_1_
  24.5 0.0 copy-start.4
  24.5 0.0 collective-permute-done.6.low_ref
  24.5 0.0 collective-permute-done.7.high_ref
  24.5 0.7 %copy-done.5 = bf16[6,2,128,128]{3,2,1,0:T(8,128)(2,1)S(1)} copy-done((bf16[6,2,128,128]{3,2,1,0:T(8,128)(2,1)S(1)}, bf16[6,2,128,128]{3,2,1,0:T(8,128)(2,1)}, u32[]{:S(2)}) %copy-start.5) | copy-done | bytes 393240
  25.2 2.2 %near.1.refs_6_ = f32[2,512,256]{2,1,0:T(8,128)S(1)} custom-call(s32[6,3,32]{2,1,0:T(4,128)S(1)} %bitcast.2, bf16[6,2,128,128]{3,2,1,0:T(8,128)(2,1)S(1)} %copy-done.5, bf16[2,512,256]{2,1,0:T(8,128)(2,1)S(1)} %get-tuple-element.12.xb_ref, bf16[2,2,128,256]{3,2,1,0:T(8,128)(2,1)S(1)} %collective-permute-done.6.low_ref, ...), custom_call_target="tpu_custom_call" | custom-call | flops 201326592 | bytes 1048576 | tf_op jit(solution)/shard_map/near/pallas_call | solution.py:18
  27.4 0.0 collective-permute-done.4.refs_2_
  27.4 0.4 %collective-permute-done.5.refs_3_ = bf16[2,256,128]{2,1,0:T(8,128)(2,1)S(1)} collective-permute-done((bf16[2,256,128]{2,1,0:T(8,128)(2,1)S(1)}, bf16[2,256,128]{2,1,0:T(8,128)(2,1)S(1)}, u32[]{:S(2)}, u32[]{:S(2)}) %collective-permute-start.5) | collective-permute-done | bytes 131104 | tf_op jit(solution)/shard_map/ppermute | solution.py:176
  27.8 0.0 copy-done.4
  27.8 2.2 %last.1 = f32[2,512,256]{2,1,0:T(8,128)} custom-call(f32[2,256,128]{2,1,0:T(8,128)S(1)} %own.8.refs_0_, f32[2,256,128]{2,1,0:T(8,128)S(1)} %own.11.refs_1_, bf16[2,256,128]{2,1,0:T(8,128)(2,1)S(1)} %collective-permute-done.4.refs_2_, bf16[2,256,128]{2,1,0:T(8,128)(2,1)S(1)} %collective-permute-done.5.refs_3_, bf16[3,2,256,256]{3,2,1,0:T(8,128)(2,1)S(1)} %copy-done.1, ...), custom_call_target="tpu_custom_call" | custom-call | flops 402653184 | bytes 1048576 | tf_op jit(solution)/shard_map/last/pallas_call | solution.py:18
Async XLA Ops:
  0.0 11.3 %copy-start = (bf16[3,2,256,256]{3,2,1,0:T(8,128)(2,1)S(1)}, bf16[3,2,256,256]{3,2,1,0:T(8,128)(2,1)}, u32[]{:S(2)}) copy-start(bf16[3,2,256,256]{3,2,1,0:T(8,128)(2,1)} %self_ref.11) | copy-start | bytes 2359300
  0.0 1.3 %copy-start.2 = (f32[2,512,256]{2,1,0:T(8,128)S(1)}, f32[2,512,256]{2,1,0:T(8,128)}, u32[]{:S(2)}) copy-start(f32[2,512,256]{2,1,0:T(8,128)} %x_ref.1) | copy-start | bytes 3145732
  1.3 1.0 %copy-start.3 = (bf16[2,256,512]{2,1,0:T(8,128)(2,1)S(1)}, bf16[2,256,512]{2,1,0:T(8,128)(2,1)}, u32[]{:S(2)}) copy-start(bf16[2,256,512]{2,1,0:T(8,128)(2,1)} %leaf_ref.1) | copy-start | bytes 1572868
  2.3 1.4 %copy-start.6 = (s32[32,6,3]{0,2,1:T(4,128)S(1)}, s32[32,6,3]{0,2,1:T(4,128)}, u32[]{:S(2)}) copy-start(s32[32,6,3]{0,2,1:T(4,128)} %param.13) | copy-start | bytes 6916
  3.1 8.8 %collective-permute-start = (bf16[2,256,128]{2,1,0:T(8,128)(2,1)S(1)}, bf16[2,256,128]{2,1,0:T(8,128)(2,1)S(1)}, u32[]{:S(2)}, u32[]{:S(2)}) collective-permute-start(bf16[2,256,128]{2,1,0:T(8,128)(2,1)S(1)} %get-tuple-element.10.coef_ref), channel_id=1, source_target_pairs={{0,1},{1,0},{2,3},{3,2},{4,5},{5,4},{6,7},{7,6},{8,9},{9,8},{10,11... | collective-permute-start | bytes 393224 | tf_op jit(solution)/shard_map/ppermute | solution.py:176
  3.7 9.4 %collective-permute-start.2 = (bf16[2,256,128]{2,1,0:T(8,128)(2,1)S(1)}, bf16[2,256,128]{2,1,0:T(8,128)(2,1)S(1)}, u32[]{:S(2)}, u32[]{:S(2)}) collective-permute-start(bf16[2,256,128]{2,1,0:T(8,128)(2,1)S(1)} %get-tuple-element.11.coef_ref), channel_id=1, source_target_pairs={{0,1},{1,0},{2,3},{3,2},{4,5},{5,4},{6,7},{7,6},{8,9},{9,8},{10,11... | collective-permute-start | bytes 393224 | tf_op jit(solution)/shard_map/ppermute | solution.py:176
  4.5 20.0 %collective-permute-start.6 = (bf16[2,2,128,256]{3,2,1,0:T(8,128)(2,1)S(1)}, bf16[2,2,128,256]{3,2,1,0:T(8,128)(2,1)S(1)}, u32[]{:S(2)}, u32[]{:S(2)}) collective-permute-start(bf16[2,2,128,256]{3,2,1,0:T(8,128)(2,1)S(1)} %get-tuple-element.13), channel_id=1, source_target_pairs={{0,1},{1,2},{2,3},{3,4},{4,5},{5,6},{6,7},{7,8},{8,9},{9,10},{10,1... | collective-permute-start | bytes 786440 | tf_op jit(solution)/shard_map/ppermute | solution.py:188
  5.0 19.5 %collective-permute-start.7 = (bf16[2,2,128,256]{3,2,1,0:T(8,128)(2,1)S(1)}, bf16[2,2,128,256]{3,2,1,0:T(8,128)(2,1)S(1)}, u32[]{:S(2)}, u32[]{:S(2)}) collective-permute-start(bf16[2,2,128,256]{3,2,1,0:T(8,128)(2,1)S(1)} %get-tuple-element.14), channel_id=1, source_target_pairs={{0,31},{1,0},{2,1},{3,2},{4,3},{5,4},{6,5},{7,6},{8,7},{9,8},{10,9... | collective-permute-start | bytes 786440 | tf_op jit(solution)/shard_map/ppermute | solution.py:189
  11.5 1.1 %copy-start.1 = (bf16[3,2,256,256]{3,2,1,0:T(8,128)(2,1)S(1)}, bf16[3,2,256,256]{3,2,1,0:T(8,128)(2,1)}, u32[]{:S(2)}) copy-start(bf16[3,2,256,256]{3,2,1,0:T(8,128)(2,1)} %refs_4_.1) | copy-start | bytes 2359300
  13.0 6.4 %collective-permute-start.1 = (bf16[2,256,128]{2,1,0:T(8,128)(2,1)S(1)}, bf16[2,256,128]{2,1,0:T(8,128)(2,1)S(1)}, u32[]{:S(2)}, u32[]{:S(2)}) collective-permute-start(bf16[2,256,128]{2,1,0:T(8,128)(2,1)S(1)} %cross.4.coef_ref), channel_id=1, source_target_pairs={{0,2},{1,3},{2,0},{3,1},{4,6},{5,7},{6,4},{7,5},{8,10},{9,11},{10,... | collective-permute-start | bytes 393224 | tf_op jit(solution)/shard_map/ppermute | solution.py:176
  13.3 9.2 %collective-permute-start.3 = (bf16[2,256,128]{2,1,0:T(8,128)(2,1)S(1)}, bf16[2,256,128]{2,1,0:T(8,128)(2,1)S(1)}, u32[]{:S(2)}, u32[]{:S(2)}) collective-permute-start(bf16[2,256,128]{2,1,0:T(8,128)(2,1)S(1)} %cross.6.coef_ref), channel_id=1, source_target_pairs={{0,2},{1,3},{2,0},{3,1},{4,6},{5,7},{6,4},{7,5},{8,10},{9,11},{10,... | collective-permute-start | bytes 393224 | tf_op jit(solution)/shard_map/ppermute | solution.py:176
  19.7 7.7 %collective-permute-start.4 = (bf16[2,256,128]{2,1,0:T(8,128)(2,1)S(1)}, bf16[2,256,128]{2,1,0:T(8,128)(2,1)S(1)}, u32[]{:S(2)}, u32[]{:S(2)}) collective-permute-start(bf16[2,256,128]{2,1,0:T(8,128)(2,1)S(1)} %cross.5.coef_ref), channel_id=1, source_target_pairs={{0,4},{1,5},{2,6},{3,7},{4,0},{5,1},{6,2},{7,3},{8,12},{9,13},{10,... | collective-permute-start | bytes 393224 | tf_op jit(solution)/shard_map/ppermute | solution.py:176
  22.8 5.0 %collective-permute-start.5 = (bf16[2,256,128]{2,1,0:T(8,128)(2,1)S(1)}, bf16[2,256,128]{2,1,0:T(8,128)(2,1)S(1)}, u32[]{:S(2)}, u32[]{:S(2)}) collective-permute-start(bf16[2,256,128]{2,1,0:T(8,128)(2,1)S(1)} %cross.7.coef_ref), channel_id=1, source_target_pairs={{0,4},{1,5},{2,6},{3,7},{4,0},{5,1},{6,2},{7,3},{8,12},{9,13},{10,... | collective-permute-start | bytes 393224 | tf_op jit(solution)/shard_map/ppermute | solution.py:176
  24.2 1.0 %copy-start.5 = (bf16[6,2,128,128]{3,2,1,0:T(8,128)(2,1)S(1)}, bf16[6,2,128,128]{3,2,1,0:T(8,128)(2,1)}, u32[]{:S(2)}) copy-start(bf16[6,2,128,128]{3,2,1,0:T(8,128)(2,1)} %tiles_ref.1) | copy-start | bytes 1179652
  24.5 3.3 %copy-start.4 = (bf16[2,512,256]{2,1,0:T(8,128)(2,1)S(1)}, bf16[2,512,256]{2,1,0:T(8,128)(2,1)}, u32[]{:S(2)}) copy-start(bf16[2,512,256]{2,1,0:T(8,128)(2,1)} %refs_5_.1) | copy-start | bytes 1572868

commit v2 on v0

v2 whole, which is shorter than its diff:
```python
import functools

import jax
import jax.numpy as jnp
from jax import lax
from jax.experimental import pallas as pl
from jax.experimental.pallas import tpu as pltpu
from jax.sharding import PartitionSpec as P


CHUNKS = 2
VMEM_LIMIT = 12 * 1024 * 1024

ON_CHIP = pl.BlockSpec(memory_space=pltpu.VMEM)
OFF_CHIP = pl.BlockSpec(memory_space=pltpu.HBM)
SCALARS = pl.BlockSpec(memory_space=pltpu.SMEM)


def call(body, outs, ins, args, flops, nbytes, scratch=(), outs_at=None, aliases=None):
    return pl.pallas_call(
        body,
        out_shape=outs,
        in_specs=ins,
        out_specs=outs_at or [ON_CHIP] * len(outs),
        scratch_shapes=list(scratch),
        input_output_aliases=aliases or {},
        cost_estimate=pl.CostEstimate(
            flops=flops, bytes_accessed=nbytes, transcendentals=0
        ),
        compiler_params=pltpu.CompilerParams(vmem_limit_bytes=VMEM_LIMIT),
    )(*args)


def dot(a, b):
    return jnp.dot(a, b, preferred_element_type=jnp.float32)


def turned(v):
    half = v.shape[1] // 2
    return jnp.concatenate([-v[:, half:], v[:, :half]], axis=1)


def stacked(v):
    return jnp.concatenate([v, turned(v)], axis=0)


def both_sides(axis, count):
    here = lax.axis_index(axis)
    odd = lax.rem(here, 2)
    pair = here + 1 - 2 * odd
    other = lax.rem(here + count - 1 + 2 * odd, count)
    return here, pair, other


def span(list_ref, reader, owner, blocks):
    low = jnp.int32(blocks - 1)
    high = jnp.int32(0)
    for slot in range(list_ref.shape[0]):
        mine = list_ref[slot, 0, reader] == owner
        column = list_ref[slot, 2, reader]
        low = jnp.minimum(low, jnp.where(mine, column, low))
        high = jnp.maximum(high, jnp.where(mine, column, high))
    return low, high


def first_body(axis, count, *refs):
    x_hbm, leaf_hbm, self_hbm, cross_hbm, basis_hbm, tiles_hbm, list_hbm = refs[:7]
    coef_refs = refs[7 : 7 + CHUNKS]
    xb_ref, pair_ref, other_ref, self_ref, cross_ref, basis_ref, tiles_ref = refs[
        7 + CHUNKS : 14 + CHUNKS
    ]
    x_ref, leaf_ref, list_ref, sems = refs[14 + CHUNKS :]
    started = 0

    def fetch(source, target):
        nonlocal started
        copy = pltpu.make_async_copy(source, target, sems.at[started])
        started += 1
        copy.start()
        return copy

    def fetch_side_by_side(source, target):
        n = source.shape[-1]
        return [fetch(source.at[c], target.at[:, c * n : (c + 1) * n]) for c in range(2)]

    listing = fetch(list_hbm, list_ref)
    excitation = [fetch(x_hbm.at[c], x_ref.at[c]) for c in range(2)]
    leaf = fetch_side_by_side(leaf_hbm, leaf_ref)
    later = []
    for level in range(self_hbm.shape[0]):
        later += fetch_side_by_side(self_hbm.at[level], self_ref.at[level])
        later += fetch_side_by_side(cross_hbm.at[level], cross_ref.at[level])
    later += fetch_side_by_side(basis_hbm, basis_ref)
    later.append(fetch(tiles_hbm, tiles_ref))

    part = x_ref.shape[2] // CHUNKS
    for copy in excitation:
        copy.wait()
    for c in range(CHUNKS):
        for k in range(2):
            at = (2 * c + k) * part
            xb_ref[:, at : at + part] = x_ref[k, :, c * part : (c + 1) * part].astype(
                jnp.bfloat16
            )
    listing.wait()
    tile = pair_ref.shape[1]
    blocks = xb_ref.shape[0] // tile
    here, pair, other = both_sides(axis, count)
    for reader, ref in ((pair, pair_ref), (other, other_ref)):
        for k, column in enumerate(span(list_ref, reader, here, blocks)):
            rows = pl.ds(pl.multiple_of(column * tile, tile), tile)
            ref[k] = xb_ref[rows, :]
    for copy in leaf:
        copy.wait()
    for c, ref in enumerate(coef_refs):
        v = xb_ref[:, 2 * c * part : 2 * (c + 1) * part]
        ref[...] = dot(leaf_ref[...], stacked(v)).astype(ref.dtype)
    for copy in later:
        copy.wait()


def own_body(level, *refs):
    coef_refs, self_ref, out_refs = refs[:CHUNKS], refs[CHUNKS], refs[CHUNKS + 1 :]
    for coef_ref, out_ref in zip(coef_refs, out_refs):
        out_ref[...] = dot(self_ref[level], stacked(coef_ref[...]))


def cross_body(level, own_ref, partner_ref, cross_ref, out_ref):
    out_ref[...] = (
        own_ref[...] + dot(cross_ref[level], stacked(partner_ref[...]))
    ).astype(out_ref.dtype)


def near_body(axis, count, list_ref, tiles_ref, xb_ref, pair_ref, other_ref, near_ref, block_ref):
    tile = tiles_ref.shape[2]
    blocks = xb_ref.shape[0] // tile
    here, pair, other = both_sides(axis, count)
    pair_first, _ = span(list_ref, here, pair, blocks)
    other_first, _ = span(list_ref, here, other, blocks)
    near_ref[...] = jnp.zeros_like(near_ref)
    slots = tiles_ref.shape[0]
    for slot in range(slots):
        owner = list_ref[slot, 0, here]
        column = list_ref[slot, 2, here]

        @pl.when(owner == here)
        def _():
            rows = pl.ds(pl.multiple_of(column * tile, tile), tile)
            block_ref[slot] = xb_ref[rows, :]

        @pl.when(owner == pair)
        def _():
            block_ref[slot] = pair_ref[jnp.where(column == pair_first, 0, 1)]

        @pl.when(jnp.logical_and(owner == other, owner != pair))
        def _():
            block_ref[slot] = other_ref[jnp.where(column == other_first, 0, 1)]

        @pl.when(owner < 0)
        def _():
            block_ref[slot] = jnp.zeros(block_ref.shape[1:], block_ref.dtype)

    wide = 2 * xb_ref.shape[1] // (2 * CHUNKS)
    for slot in range(slots):
        row = list_ref[slot, 1, here]
        rows = pl.ds(pl.multiple_of(row * tile, tile), tile)
        for c in range(CHUNKS):
            v = block_ref[slot, :, c * wide : (c + 1) * wide]
            term = dot(tiles_ref[slot, 0], v) + dot(tiles_ref[slot, 1], turned(v))
            near_ref[rows, c * wide : (c + 1) * wide] += term


def last_body(level, c, *refs):
    own_ref, partner_ref, cross_ref, basis_ref, near_ref = refs[:5]
    out_hbm, result_ref, sems = refs[-3:]
    v = own_ref[...] + dot(cross_ref[level], stacked(partner_ref[...]))
    v = stacked(v.astype(jnp.bfloat16))
    part = v.shape[1] // 2
    rows = basis_ref.shape[0]
    step = rows // (sems.shape[0] // 2)
    copies = []
    for r in range(0, rows, step):
        result_ref[r : r + step, :] = (
            dot(basis_ref[r : r + step, :], v)
            + near_ref[r : r + step, 2 * c * part : 2 * (c + 1) * part]
        )
        for k in range(2):
            copy = pltpu.make_async_copy(
                result_ref.at[r : r + step, k * part : (k + 1) * part],
                out_hbm.at[k, r : r + step, c * part : (c + 1) * part],
                sems.at[len(copies)],
            )
            copy.start()
            copies.append(copy)
    for copy in copies:
        copy.wait()


def per_device(
    excitation, leaf_basis, self_transfer, cross_transfer, out_basis, near_tiles, near_list
):
    axis = "surf"
    count = lax.axis_size(axis)
    rows, width = excitation.shape[1:]
    rank = leaf_basis.shape[1]
    slots, _, tile, _ = near_tiles.shape
    levels = self_transfer.shape[0]
    part = width // CHUNKS
    bf16, f32 = jnp.bfloat16, jnp.float32
    listing = near_list.transpose(1, 2, 0)
    piece = pltpu.VMEM((rank, 2 * part), bf16)
    total = pltpu.VMEM((rank, 2 * part), f32)
    sent = pltpu.VMEM((2, tile, 2 * width), bf16)

    held = [
        pltpu.with_memory_space_constraint(a, pltpu.HBM)
        for a in (
            excitation,
            leaf_basis,
            self_transfer,
            cross_transfer,
            out_basis,
            near_tiles,
            listing,
        )
    ]
    first = call(
        functools.partial(first_body, axis, count),
        [piece] * CHUNKS
        + [
            pltpu.VMEM((rows, 2 * width), bf16),
            sent,
            sent,
            pltpu.VMEM((levels, rank, 2 * rank), bf16),
            pltpu.VMEM((levels, rank, 2 * rank), bf16),
            pltpu.VMEM((rows, 2 * rank), bf16),
            pltpu.VMEM(near_tiles.shape, bf16),
        ],
        [OFF_CHIP] * 7,
        held,
        8 * rank * rows * width,
        8 * rows * width,
        scratch=[
            pltpu.VMEM(excitation.shape, f32),
            pltpu.VMEM((rank, 2 * rows), bf16),
            pltpu.SMEM(listing.shape, jnp.int32),
            pltpu.SemaphoreType.DMA((8 + 4 * levels,)),
        ],
    )
    coef = first[:CHUNKS]
    xb, to_pair, to_other, self_maps, cross_maps, basis, tiles = first[CHUNKS:]
    for level in range(levels):
        swap = [(i, i ^ (1 << level)) for i in range(count)]
        partner = []
        for c in range(CHUNKS):
            partner.append(lax.ppermute(coef[c], axis, swap))
        if level == 1:
            to_pair, to_other, *coef = lax.optimization_barrier((to_pair, to_other, *coef))
            pair = lax.ppermute(to_pair, axis, [(i, i ^ 1) for i in range(count)])
            other = lax.ppermute(
                to_other, axis, [(i, (i + i % 2 * 2 - 1) % count) for i in range(count)]
            )
        own = call(
            functools.partial(own_body, level),
            [total] * CHUNKS,
            [ON_CHIP] * (CHUNKS + 1),
            (*coef, self_maps),
            8 * rank * rank * width,
            2 * rank * rank,
        )
        if level == levels - 1:
            break
        coef = []
        for c in range(CHUNKS):
            coef += call(
                functools.partial(cross_body, level),
                [piece],
                [ON_CHIP] * 3,
                (own[c], partner[c], cross_maps),
                8 * rank * rank * part,
                2 * rank * rank,
            )
    (near,) = call(
        functools.partial(near_body, axis, count),
        [pltpu.VMEM((rows, 2 * width), f32)],
        [SCALARS] + [ON_CHIP] * 4,
        (listing, tiles, xb, pair, other),
        8 * slots * tile * tile * width,
        8 * rows * width,
        scratch=[pltpu.VMEM((slots, tile, 2 * width), bf16)],
    )
    out = None
    for c in range(CHUNKS):
        before = () if out is None else (out,)
        (out,) = call(
            functools.partial(last_body, levels - 1, c),
            [jax.ShapeDtypeStruct((2, rows, width), f32)],
            [ON_CHIP] * 5 + [OFF_CHIP] * len(before),
            (own[c], partner[c], cross_maps, basis, near, *before),
            8 * rank * (rank + rows) * part,
            8 * rows * part,
            scratch=[pltpu.VMEM((rows, 2 * part), f32), pltpu.SemaphoreType.DMA((8,))],
            outs_at=[OFF_CHIP],
            aliases={5: 0} if before else {},
        )
    return out


def solution(mesh):
    placed = (
        P(None, "surf", None),
        P(None, "surf", None),
        P(None, None, "surf", None),
        P(None, None, "surf", None),
        P(None, "surf", None),
        P("surf", None, None, None),
        P(),
    )
    return jax.shard_map(
        per_device, mesh=mesh, in_specs=placed, out_specs=P(None, "surf", None), check_vma=False
    )
```

time: 85.3 us -> 28.4 us (0.33)
  matrix products: 27.9 us -> 0 us
  local copies, waits for them, and re-layouts: 26.4 us -> 0.38 us
  other arithmetic: 11.7 us -> 0 us
  between operations: 11.7 us -> 0.1 us
  Pallas kernels: 0 us -> 8.36 us
  starting transfers between devices: 6.73 us -> 13.8 us
  waiting for transfers between devices: 0.01 us -> 5.48 us
    dot_general x56 -> x0, matrix products: 27.9 us -> none  [the longest x14 8.23 us: cmat(): jnp.dot(matrix[0], vector[0], preferred_element_type=jnp.float32)]
    mul x15 -> x0, local copies, waits for them, and re-layouts: 21.4 us -> none  [per_device(): near = near + term[:, None] * hit[None, :, None, None]]
    pallas_call x0 -> x11, Pallas kernels: none -> 8.36 us  [call(): pl.pallas_call(body, out_shape=outs, in_specs=ins, out_specs=outs_at or [...]
    ppermute x5 -> x8, starting transfers between devices: 6.73 us -> 13.8 us  [the longest x6 6.94 us: per_device(): partner.append(lax.ppermute(coef[c], axis, swap))]
    ppermute x5 -> x8, waiting for transfers between devices: 0.01 us -> 5.48 us  [the longest x6 5.48 us: per_device(): partner.append(lax.ppermute(coef[c], axis, swap))]
    convert_element_type x11 -> x0, other arithmetic: 5.34 us -> none  [the longest x6 3.76 us: per_device(): hit = (block_ids == row_tile[slot]).astype(jnp.float32)]
    mul x6 -> x0, other arithmetic: 4.01 us -> none  [per_device(): term = cmat(near_tiles[slot], block) * valid[slot]]
    slice x3 -> x0, local copies, waits for them, and re-layouts: 1.99 us -> none  [the longest x1 0.66 us: per_device(): hit = (block_ids == row_tile[slot]).astype(jnp.float32)]
  transfers between devices with their start and end apart: 5 -> 8, of which waited for: 0 -> 5; matrix products, arithmetic and copies ran while one was open for 64% -> 0% of each run, Pallas kernels for 0% -> 16%
where the time goes in v2:
time: 28.4 us; the launch traced here: 28.2 us
  starting transfers between devices  13.8 us (49%)
  Pallas kernels  8.36 us (29%)
  waiting for transfers between devices  5.48 us (19%)
  local copies, waits for them, and re-layouts  0.38 us (1%)
    pallas_call x11, Pallas kernels, call(): pl.pallas_call(body, out_shape=outs, in_specs=ins, out_specs=outs_at or [...  8.36 us
    ppermute x6, starting transfers between devices, per_device(): partner.append(lax.ppermute(coef[c], axis, swap))  6.94 us
    ppermute x1, starting transfers between devices, per_device(): lax.ppermute(to_other, axis, [(i, (i + i % 2 * 2 - 1) % count) for i in r...  6.58 us
    ppermute x6, waiting for transfers between devices, per_device(): partner.append(lax.ppermute(coef[c], axis, swap))  5.48 us
  transfers between devices with their start and end apart: 8, of which 5 were waited for; matrix products, arithmetic and copies ran while one was open for 0% of the time, Pallas kernels for 16%

profile of v2, /device:TPU:0, one launch (start us, length us, event | category | flops | bytes accessed | tf_op | source)
XLA Modules:
  0.0 28.2 jit_solution(2851749184181310146)
XLA Ops:
  0.0 2.3 %shard_map.73 = (bf16[256,256]{1,0:T(8,128)(2,1)S(1)}, bf16[256,256]{1,0:T(8,128)(2,1)S(1)}, bf16[512,512]{1,0:T(8,128)(2,1)S(1)}, bf16[2,128,512]{2,1,0:T(8,128...) custom-call(f32[2,512,256]{2,1,0:T(8,128)} %refs_0_.1, ...), custom_call_target="tpu_custom_call" | custom-call | flops 268435456 | bytes 1048576 | tf_op jit(solution)/shard_map/pallas_call | solution.py:20
  2.3 0.6 %collective-permute-start = (bf16[256,256]{1,0:T(8,128)(2,1)S(1)}, bf16[256,256]{1,0:T(8,128)(2,1)S(1)}, u32[]{:S(2)}, u32[]{:S(2)}) collective-permute-start(bf16[256,256]{1,0:T(8,128)(2,1)S(1)} %get-tuple-element.26.refs_0_), channel_id=1, source_target_pairs={{0,1},{1,0},{2,3},{3,2},{4,5},{5,4},{6,7},{7,6},{8,9},{9,8},{10,11... | collective-permute-start | bytes 393224 | tf_op jit(solution)/shard_map/ppermute | solution.py:256
  2.8 0.1 collective-permute-start.1
  2.9 0.3 %shard_map.74 = (f32[256,256]{1,0:T(8,128)S(1)}, f32[256,256]{1,0:T(8,128)S(1)}) custom-call(bf16[256,256]{1,0:T(8,128)(2,1)S(1)} %get-tuple-element.26.refs_0_, bf16[256,256]{1,0:T(8,128)(2,1)S(1)} %get-tuple-element.27.refs_1_, bf16[3,256,512]{2,1,0:T(8,128)(2,1)S(1)} %get-tuple-element.28.refs_2_), custom_call_target="tpu_custom_call" | custom-call | flops 134217728 | bytes 131072 | tf_op jit(solution)/shard_map/pallas_call | solution.py:20
  3.2 0.6 %collective-permute-done.partner_ref = bf16[256,256]{1,0:T(8,128)(2,1)S(1)} collective-permute-done((bf16[256,256]{1,0:T(8,128)(2,1)S(1)}, bf16[256,256]{1,0:T(8,128)(2,1)S(1)}, u32[]{:S(2)}, u32[]{:S(2)}) %collective-permute-start) | collective-permute-done | bytes 131104 | tf_op jit(solution)/shard_map/ppermute | solution.py:256
  3.8 0.2 shard_map.75.refs_0_
  4.1 0.1 collective-permute-done.1.partner_ref
  4.2 0.2 shard_map.76.refs_1_
  4.4 0.3 %collective-permute-start.5 = (bf16[2,128,512]{2,1,0:T(8,128)(2,1)S(1)}, bf16[2,128,512]{2,1,0:T(8,128)(2,1)S(1)}, u32[]{:S(2)}, u32[]{:S(2)}) collective-permute-start(bf16[2,128,512]{2,1,0:T(8,128)(2,1)S(1)} %get-tuple-element.40), channel_id=1, source_target_pairs={{0,1},{1,0},{2,3},{3,2},{4,5},{5,4},{6,7},{7,6},{8,9},{9,8},{10,11... | collective-permute-start | bytes 786440 | tf_op jit(solution)/shard_map/ppermute | solution.py:259
  4.7 6.6 %collective-permute-start.6 = (bf16[2,128,512]{2,1,0:T(8,128)(2,1)S(1)}, bf16[2,128,512]{2,1,0:T(8,128)(2,1)S(1)}, u32[]{:S(2)}, u32[]{:S(2)}) collective-permute-start(bf16[2,128,512]{2,1,0:T(8,128)(2,1)S(1)} %get-tuple-element.41), channel_id=1, source_target_pairs={{0,31},{1,2},{2,1},{3,4},{4,3},{5,6},{6,5},{7,8},{8,7},{9,10},{10,... | collective-permute-start | bytes 786440 | tf_op jit(solution)/shard_map/ppermute | solution.py:260
  11.3 0.0 collective-permute-start.2
  11.3 2.0 %collective-permute-start.3 = (bf16[256,256]{1,0:T(8,128)(2,1)S(1)}, bf16[256,256]{1,0:T(8,128)(2,1)S(1)}, u32[]{:S(2)}, u32[]{:S(2)}) collective-permute-start(bf16[256,256]{1,0:T(8,128)(2,1)S(1)} %shard_map.76.refs_1_), channel_id=1, source_target_pairs={{0,2},{1,3},{2,0},{3,1},{4,6},{5,7},{6,4},{7,5},{8,10},{9,11},{10,... | collective-permute-start | bytes 393224 | tf_op jit(solution)/shard_map/ppermute | solution.py:256
  13.3 0.3 %shard_map.77 = (f32[256,256]{1,0:T(8,128)S(1)}, f32[256,256]{1,0:T(8,128)S(1)}) custom-call(bf16[256,256]{1,0:T(8,128)(2,1)S(1)} %shard_map.75.refs_0_, bf16[256,256]{1,0:T(8,128)(2,1)S(1)} %shard_map.76.refs_1_, bf16[3,256,512]{2,1,0:T(8,128)(2,1)S(1)} %get-tuple-element.28.refs_2_), custom_call_target="tpu_custom_call" | custom-call | flops 134217728 | bytes 131072 | tf_op jit(solution)/shard_map/pallas_call | solution.py:20
  13.7 4.0 %collective-permute-done.2.partner_ref = bf16[256,256]{1,0:T(8,128)(2,1)S(1)} collective-permute-done((bf16[256,256]{1,0:T(8,128)(2,1)S(1)}, bf16[256,256]{1,0:T(8,128)(2,1)S(1)}, u32[]{:S(2)}, u32[]{:S(2)}) %collective-permute-start.2) | collective-permute-done | bytes 131104 | tf_op jit(solution)/shard_map/ppermute | solution.py:256
  17.7 0.2 shard_map.78.refs_0_
  17.9 3.1 %collective-permute-start.7 = (bf16[256,256]{1,0:T(8,128)(2,1)S(1)}, bf16[256,256]{1,0:T(8,128)(2,1)S(1)}, u32[]{:S(2)}, u32[]{:S(2)}) collective-permute-start(bf16[256,256]{1,0:T(8,128)(2,1)S(1)} %shard_map.78.refs_0_), channel_id=1, source_target_pairs={{0,4},{1,5},{2,6},{3,7},{4,0},{5,1},{6,2},{7,3},{8,12},{9,13},{10,... | collective-permute-start | bytes 393224 | tf_op jit(solution)/shard_map/ppermute | solution.py:256
  21.1 0.0 collective-permute-done.3.partner_ref
  21.1 0.2 shard_map.79.refs_1_
  21.3 1.2 %collective-permute-start.4 = (bf16[256,256]{1,0:T(8,128)(2,1)S(1)}, bf16[256,256]{1,0:T(8,128)(2,1)S(1)}, u32[]{:S(2)}, u32[]{:S(2)}) collective-permute-start(bf16[256,256]{1,0:T(8,128)(2,1)S(1)} %shard_map.79.refs_1_), channel_id=1, source_target_pairs={{0,4},{1,5},{2,6},{3,7},{4,0},{5,1},{6,2},{7,3},{8,12},{9,13},{10,... | collective-permute-start | bytes 393224 | tf_op jit(solution)/shard_map/ppermute | solution.py:256
  22.5 0.0 copy-start
  22.5 0.3 %shard_map.80 = (f32[256,256]{1,0:T(8,128)S(1)}, f32[256,256]{1,0:T(8,128)S(1)}) custom-call(bf16[256,256]{1,0:T(8,128)(2,1)S(1)} %shard_map.78.refs_0_, bf16[256,256]{1,0:T(8,128)(2,1)S(1)} %shard_map.79.refs_1_, bf16[3,256,512]{2,1,0:T(8,128)(2,1)S(1)} %get-tuple-element.28.refs_2_), custom_call_target="tpu_custom_call" | custom-call | flops 134217728 | bytes 131072 | tf_op jit(solution)/shard_map/pallas_call | solution.py:20
  22.8 0.0 collective-permute-done.5.pair_ref
  22.8 0.0 collective-permute-done.6.other_ref
  22.8 0.4 %copy-done = s32[32,6,3]{0,2,1:T(4,128)S(1)} copy-done((s32[32,6,3]{0,2,1:T(4,128)S(1)}, s32[32,6,3]{0,2,1:T(4,128)}, u32[]{:S(2)}) %copy-start) | copy-done | bytes 2328
  23.2 1.6 %shard_map.81.refs_4_ = f32[512,512]{1,0:T(8,128)S(1)} custom-call(s32[6,3,32]{2,1,0:T(4,128)S(1)} %bitcast.2, bf16[6,2,128,128]{3,2,1,0:T(8,128)(2,1)S(1)} %get-tuple-element.38.tiles_ref, bf16[512,512]{1,0:T(8,128)(2,1)S(1)} %get-tuple-element.39.xb_ref, bf16[2,128,512]{2,1,0:T(8,128)(2,1)S(1)} %collective-permute-done.5.pair_ref, ...), custom_call_target="tpu_custom_call" | custom-call | flops 201326592 | bytes 1048576 | tf_op jit(solution)/shard_map/pallas_call | solution.py:20
  24.7 0.3 collective-permute-done.7.refs_1_
  25.0 1.4 %shard_map.82.refs_5_ = f32[2,512,256]{2,1,0:T(8,128)} custom-call(f32[256,256]{1,0:T(8,128)S(1)} %get-tuple-element.42.refs_0_, bf16[256,256]{1,0:T(8,128)(2,1)S(1)} %collective-permute-done.7.refs_1_, bf16[3,256,512]{2,1,0:T(8,128)(2,1)S(1)} %get-tuple-element.30.cross_ref.refs_2_, bf16[512,512]{1,0:T(8,128)(2,1)S(1)} %get-tuple-element.37.refs_3_, ...), custom_call_target="tpu_custom_call" | custom-call | flops 201326592 | bytes 524288 | tf_op jit(solution)/shard_map/pallas_call | solution.py:20
  26.4 0.5 %collective-permute-done.4.refs_1_ = bf16[256,256]{1,0:T(8,128)(2,1)S(1)} collective-permute-done((bf16[256,256]{1,0:T(8,128)(2,1)S(1)}, bf16[256,256]{1,0:T(8,128)(2,1)S(1)}, u32[]{:S(2)}, u32[]{:S(2)}) %collective-permute-start.4) | collective-permute-done | bytes 131104 | tf_op jit(solution)/shard_map/ppermute | solution.py:256
  26.8 1.4 %shard_map.83 = f32[2,512,256]{2,1,0:T(8,128)} custom-call(f32[256,256]{1,0:T(8,128)S(1)} %get-tuple-element.36.refs_0_, bf16[256,256]{1,0:T(8,128)(2,1)S(1)} %collective-permute-done.4.refs_1_, bf16[3,256,512]{2,1,0:T(8,128)(2,1)S(1)} %get-tuple-element.30.cross_ref.refs_2_, ...), custom_call_target="tpu_custom_call", output_to_operand_aliasing={{}: (5, {})} | custom-call | flops 201326592 | bytes 524288 | tf_op jit(solution)/shard_map/pallas_call | solution.py:20
Async XLA Ops:
  2.3 1.5 %collective-permute-start = (bf16[256,256]{1,0:T(8,128)(2,1)S(1)}, bf16[256,256]{1,0:T(8,128)(2,1)S(1)}, u32[]{:S(2)}, u32[]{:S(2)}) collective-permute-start(bf16[256,256]{1,0:T(8,128)(2,1)S(1)} %get-tuple-element.26.refs_0_), channel_id=1, source_target_pairs={{0,1},{1,0},{2,3},{3,2},{4,5},{5,4},{6,7},{7,6},{8,9},{9,8},{10,11... | collective-permute-start | bytes 393224 | tf_op jit(solution)/shard_map/ppermute | solution.py:256
  2.8 1.3 %collective-permute-start.1 = (bf16[256,256]{1,0:T(8,128)(2,1)S(1)}, bf16[256,256]{1,0:T(8,128)(2,1)S(1)}, u32[]{:S(2)}, u32[]{:S(2)}) collective-permute-start(bf16[256,256]{1,0:T(8,128)(2,1)S(1)} %get-tuple-element.27.refs_1_), channel_id=1, source_target_pairs={{0,1},{1,0},{2,3},{3,2},{4,5},{5,4},{6,7},{7,6},{8,9},{9,8},{10,11... | collective-permute-start | bytes 393224 | tf_op jit(solution)/shard_map/ppermute | solution.py:256
  4.4 18.3 %collective-permute-start.5 = (bf16[2,128,512]{2,1,0:T(8,128)(2,1)S(1)}, bf16[2,128,512]{2,1,0:T(8,128)(2,1)S(1)}, u32[]{:S(2)}, u32[]{:S(2)}) collective-permute-start(bf16[2,128,512]{2,1,0:T(8,128)(2,1)S(1)} %get-tuple-element.40), channel_id=1, source_target_pairs={{0,1},{1,0},{2,3},{3,2},{4,5},{5,4},{6,7},{7,6},{8,9},{9,8},{10,11... | collective-permute-start | bytes 786440 | tf_op jit(solution)/shard_map/ppermute | solution.py:259
  4.7 18.0 %collective-permute-start.6 = (bf16[2,128,512]{2,1,0:T(8,128)(2,1)S(1)}, bf16[2,128,512]{2,1,0:T(8,128)(2,1)S(1)}, u32[]{:S(2)}, u32[]{:S(2)}) collective-permute-start(bf16[2,128,512]{2,1,0:T(8,128)(2,1)S(1)} %get-tuple-element.41), channel_id=1, source_target_pairs={{0,31},{1,2},{2,1},{3,4},{4,3},{5,6},{6,5},{7,8},{8,7},{9,10},{10,... | collective-permute-start | bytes 786440 | tf_op jit(solution)/shard_map/ppermute | solution.py:260
  11.3 6.4 %collective-permute-start.2 = (bf16[256,256]{1,0:T(8,128)(2,1)S(1)}, bf16[256,256]{1,0:T(8,128)(2,1)S(1)}, u32[]{:S(2)}, u32[]{:S(2)}) collective-permute-start(bf16[256,256]{1,0:T(8,128)(2,1)S(1)} %shard_map.75.refs_0_), channel_id=1, source_target_pairs={{0,2},{1,3},{2,0},{3,1},{4,6},{5,7},{6,4},{7,5},{8,10},{9,11},{10,... | collective-permute-start | bytes 393224 | tf_op jit(solution)/shard_map/ppermute | solution.py:256
  11.3 9.7 %collective-permute-start.3 = (bf16[256,256]{1,0:T(8,128)(2,1)S(1)}, bf16[256,256]{1,0:T(8,128)(2,1)S(1)}, u32[]{:S(2)}, u32[]{:S(2)}) collective-permute-start(bf16[256,256]{1,0:T(8,128)(2,1)S(1)} %shard_map.76.refs_1_), channel_id=1, source_target_pairs={{0,2},{1,3},{2,0},{3,1},{4,6},{5,7},{6,4},{7,5},{8,10},{9,11},{10,... | collective-permute-start | bytes 393224 | tf_op jit(solution)/shard_map/ppermute | solution.py:256
  17.9 7.1 %collective-permute-start.7 = (bf16[256,256]{1,0:T(8,128)(2,1)S(1)}, bf16[256,256]{1,0:T(8,128)(2,1)S(1)}, u32[]{:S(2)}, u32[]{:S(2)}) collective-permute-start(bf16[256,256]{1,0:T(8,128)(2,1)S(1)} %shard_map.78.refs_0_), channel_id=1, source_target_pairs={{0,4},{1,5},{2,6},{3,7},{4,0},{5,1},{6,2},{7,3},{8,12},{9,13},{10,... | collective-permute-start | bytes 393224 | tf_op jit(solution)/shard_map/ppermute | solution.py:256
  21.3 5.5 %collective-permute-start.4 = (bf16[256,256]{1,0:T(8,128)(2,1)S(1)}, bf16[256,256]{1,0:T(8,128)(2,1)S(1)}, u32[]{:S(2)}, u32[]{:S(2)}) collective-permute-start(bf16[256,256]{1,0:T(8,128)(2,1)S(1)} %shard_map.79.refs_1_), channel_id=1, source_target_pairs={{0,4},{1,5},{2,6},{3,7},{4,0},{5,1},{6,2},{7,3},{8,12},{9,13},{10,... | collective-permute-start | bytes 393224 | tf_op jit(solution)/shard_map/ppermute | solution.py:256
  22.5 0.7 %copy-start = (s32[32,6,3]{0,2,1:T(4,128)S(1)}, s32[32,6,3]{0,2,1:T(4,128)}, u32[]{:S(2)}) copy-start(s32[32,6,3]{0,2,1:T(4,128)} %param.13) | copy-start | bytes 6916

commit v3 on v2

v3 whole, which is shorter than its diff:
```python
import functools

import jax
import jax.numpy as jnp
from jax import lax
from jax.experimental import pallas as pl
from jax.experimental.pallas import tpu as pltpu
from jax.sharding import PartitionSpec as P


CHUNKS = 2
VMEM_LIMIT = 12 * 1024 * 1024
STEPS = 4

ON_CHIP = pl.BlockSpec(memory_space=pltpu.VMEM)
OFF_CHIP = pl.BlockSpec(memory_space=pltpu.HBM)
SCALARS = pl.BlockSpec(memory_space=pltpu.SMEM)


def call(body, outs, ins, args, flops, nbytes, scratch=(), outs_at=None, aliases=None):
    return pl.pallas_call(
        body,
        out_shape=outs,
        in_specs=ins,
        out_specs=outs_at or [ON_CHIP] * len(outs),
        scratch_shapes=list(scratch),
        input_output_aliases=aliases or {},
        cost_estimate=pl.CostEstimate(
            flops=flops, bytes_accessed=nbytes, transcendentals=0
        ),
        compiler_params=pltpu.CompilerParams(vmem_limit_bytes=VMEM_LIMIT),
    )(*args)


def dot(a, b):
    return jnp.dot(a, b, preferred_element_type=jnp.float32)


def turned(v):
    half = v.shape[1] // 2
    return jnp.concatenate([-v[:, half:], v[:, :half]], axis=1)


def stacked(*vs):
    return jnp.concatenate([w for v in vs for w in (v, turned(v))], axis=0)


def flat(ref, lanes):
    return jnp.concatenate([ref[k, :, lanes] for k in range(ref.shape[0])], axis=0)


def both_sides(axis, count):
    here = lax.axis_index(axis)
    odd = lax.rem(here, 2)
    pair = here + 1 - 2 * odd
    other = lax.rem(here + count - 1 + 2 * odd, count)
    return here, pair, other


def span(list_ref, reader, owner, blocks):
    low = jnp.int32(blocks - 1)
    high = jnp.int32(0)
    for slot in range(list_ref.shape[0]):
        mine = list_ref[slot, 0, reader] == owner
        column = list_ref[slot, 2, reader]
        low = jnp.minimum(low, jnp.where(mine, column, low))
        high = jnp.maximum(high, jnp.where(mine, column, high))
    return low, high


class Fetches:
    def __init__(self, sems):
        self.sems = sems
        self.count = 0

    def start(self, source, target):
        copy = pltpu.make_async_copy(source, target, self.sems.at[self.count])
        self.count += 1
        copy.start()
        return copy

    def side_by_side(self, source, target, at=0):
        n = source.shape[-1]
        return [
            self.start(source.at[c], target.at[:, at + c * n : at + (c + 1) * n])
            for c in range(2)
        ]

    def maps(self, level, self_hbm, cross_hbm, target):
        n = self_hbm.shape[-1]
        return self.side_by_side(self_hbm.at[level], target) + self.side_by_side(
            cross_hbm.at[level], target, 2 * n
        )


def first_body(axis, count, *refs):
    x_hbm, leaf_hbm, self_hbm, cross_hbm, list_hbm = refs[:5]
    coef_refs = refs[5 : 5 + CHUNKS]
    xb_ref, pair_ref, other_ref, *map_refs = refs[5 + CHUNKS : 10 + CHUNKS]
    x_ref, leaf_ref, list_ref, sems = refs[10 + CHUNKS :]
    fetches = Fetches(sems)
    listing = fetches.start(list_hbm, list_ref)
    excitation = [fetches.start(x_hbm.at[c], x_ref.at[c]) for c in range(2)]
    leaf = fetches.side_by_side(leaf_hbm, leaf_ref)
    later = []
    for level, ref in enumerate(map_refs):
        later += fetches.maps(level, self_hbm, cross_hbm, ref)

    part = x_ref.shape[2] // CHUNKS
    for copy in excitation:
        copy.wait()
    for c in range(CHUNKS):
        for k in range(2):
            at = (2 * c + k) * part
            xb_ref[:, at : at + part] = x_ref[k, :, c * part : (c + 1) * part].astype(
                jnp.bfloat16
            )
    listing.wait()
    tile = pair_ref.shape[1]
    blocks = xb_ref.shape[0] // tile
    here, pair, other = both_sides(axis, count)
    for reader, ref in ((pair, pair_ref), (other, other_ref)):
        for k, column in enumerate(span(list_ref, reader, here, blocks)):
            rows = pl.ds(pl.multiple_of(column * tile, tile), tile)
            ref[k] = xb_ref[rows, :]
    for copy in leaf:
        copy.wait()
    for c, ref in enumerate(coef_refs):
        v = xb_ref[:, 2 * c * part : 2 * (c + 1) * part]
        ref[...] = dot(leaf_ref[...], stacked(v)).astype(ref.dtype)
    for copy in later:
        copy.wait()


def rest_body(level, self_hbm, cross_hbm, basis_hbm, tiles_hbm, map_ref, basis_ref, tiles_ref, sems):
    fetches = Fetches(sems)
    copies = fetches.maps(level, self_hbm, cross_hbm, map_ref)
    copies += fetches.side_by_side(basis_hbm, basis_ref)
    copies.append(fetches.start(tiles_hbm, tiles_ref))
    for copy in copies:
        copy.wait()


def both_body(coef_ref, partner_ref, map_ref, out_ref):
    out_ref[...] = dot(map_ref[...], stacked(coef_ref[...], partner_ref[...])).astype(
        out_ref.dtype
    )


def own_body(*refs):
    coef_refs, map_ref, out_refs = refs[:CHUNKS], refs[CHUNKS], refs[CHUNKS + 1 :]
    half = map_ref.shape[1] // 2
    for coef_ref, out_ref in zip(coef_refs, out_refs):
        out_ref[...] = dot(map_ref[:, :half], stacked(coef_ref[...]))


def cross_body(own_ref, partner_ref, map_ref, out_ref):
    half = map_ref.shape[1] // 2
    out_ref[...] = (
        own_ref[...] + dot(map_ref[:, half:], stacked(partner_ref[...]))
    ).astype(out_ref.dtype)


def near_body(axis, count, list_ref, tiles_ref, xb_ref, pair_ref, near_ref, map_ref, block_ref):
    slots, _, tile, _ = tiles_ref.shape
    blocks = xb_ref.shape[0] // tile
    here, pair, other = both_sides(axis, count)
    pair_first, _ = span(list_ref, here, pair, blocks)
    other_first, _ = span(list_ref, here, other, blocks)
    near_ref[...] = jnp.zeros_like(near_ref)
    map_ref[...] = jnp.zeros_like(map_ref)
    half = map_ref.shape[1] // 2
    for slot in range(slots):
        owner = list_ref[slot, 0, here]
        column = list_ref[slot, 2, here]
        row = list_ref[slot, 1, here]

        @pl.when(owner == here)
        def _():
            rows = pl.ds(pl.multiple_of(column * tile, tile), tile)
            block_ref[slot] = xb_ref[rows, :]

        @pl.when(owner == pair)
        def _():
            block_ref[slot] = pair_ref[jnp.where(column == pair_first, 0, 1)]

        @pl.when(jnp.logical_and(owner != here, owner != pair))
        def _():
            block_ref[slot] = jnp.zeros(block_ref.shape[1:], block_ref.dtype)

        @pl.when(jnp.logical_and(owner == other, owner != pair))
        def _():
            rows = pl.ds(pl.multiple_of(row * tile, tile), tile)
            at = jnp.where(column == other_first, 0, tile)
            for k in range(2):
                cols = pl.ds(pl.multiple_of(at + k * half, tile), tile)
                map_ref[rows, cols] = (
                    map_ref[rows, cols].astype(jnp.float32)
                    + tiles_ref[slot, k].astype(jnp.float32)
                ).astype(map_ref.dtype)

    wide = xb_ref.shape[1] // CHUNKS
    for slot in range(slots):
        row = list_ref[slot, 1, here]
        rows = pl.ds(pl.multiple_of(row * tile, tile), tile)
        for c in range(CHUNKS):
            v = block_ref[slot, :, c * wide : (c + 1) * wide]
            term = dot(tiles_ref[slot, 0], v) + dot(tiles_ref[slot, 1], turned(v))
            near_ref[rows, c * wide : (c + 1) * wide] += term


def last_body(c, *refs):
    own_ref, partner_ref, map_ref, basis_ref, near_ref = refs[:5]
    if c == 0:
        side_ref, other_ref, out_hbm, sum_ref, result_ref, sems = refs[5:]
    else:
        _, out_hbm, result_ref, sems = refs[5:]
    half = map_ref.shape[1] // 2
    v = own_ref[...] + dot(map_ref[:, half:], stacked(partner_ref[...]))
    v = stacked(v.astype(jnp.bfloat16))
    wide = v.shape[1]
    part = wide // 2
    rows = basis_ref.shape[0]
    step = rows // STEPS
    copies = []
    if c == 0:
        side = [
            stacked(flat(other_ref, slice(d * wide, (d + 1) * wide))) for d in range(CHUNKS)
        ]
    for r in range(0, rows, step):
        piece = slice(r, r + step)
        total = dot(basis_ref[piece, :], v)
        if c == 0:
            total = total + near_ref[piece, :wide] + dot(side_ref[piece, :], side[0])
        else:
            total = total + near_ref[piece, (c - 1) * wide : c * wide]
        result_ref[piece, :] = total
        for k in range(2):
            copy = pltpu.make_async_copy(
                result_ref.at[piece, k * part : (k + 1) * part],
                out_hbm.at[k, piece, c * part : (c + 1) * part],
                sems.at[len(copies)],
            )
            copy.start()
            copies.append(copy)
    if c == 0:
        for d in range(1, CHUNKS):
            lanes = slice((d - 1) * wide, d * wide)
            sum_ref[:, lanes] = near_ref[:, d * wide : (d + 1) * wide] + dot(
                side_ref[...], side[d]
            )
    for copy in copies:
        copy.wait()


def per_device(
    excitation, leaf_basis, self_transfer, cross_transfer, out_basis, near_tiles, near_list
):
    axis = "surf"
    count = lax.axis_size(axis)
    rows, width = excitation.shape[1:]
    rank = leaf_basis.shape[1]
    slots, _, tile, _ = near_tiles.shape
    levels = self_transfer.shape[0]
    part = width // CHUNKS
    bf16, f32 = jnp.bfloat16, jnp.float32
    piece = pltpu.VMEM((rank, 2 * part), bf16)
    total = pltpu.VMEM((rank, 2 * part), f32)
    sent = pltpu.VMEM((2, tile, 2 * width), bf16)
    maps = pltpu.VMEM((rank, 4 * rank), bf16)
    pairs = [(i, i ^ 1) for i in range(count)]
    others = [(i, (i + i % 2 * 2 - 1) % count) for i in range(count)]

    def held(a):
        return pltpu.with_memory_space_constraint(a, pltpu.HBM)

    def swaps(level, coef):
        found = []
        for c in range(CHUNKS):
            found.append(lax.ppermute(coef[c], axis, [(i, i ^ (1 << level)) for i in range(count)]))
        return found

    self_transfer, cross_transfer = held(self_transfer), held(cross_transfer)
    listing = near_list.transpose(1, 2, 0)
    first = call(
        functools.partial(first_body, axis, count),
        [piece] * CHUNKS + [pltpu.VMEM((rows, 2 * width), bf16), sent, sent, maps, maps],
        [OFF_CHIP] * 5,
        (held(excitation), held(leaf_basis), self_transfer, cross_transfer, held(listing)),
        8 * rank * rows * width,
        8 * rows * width,
        scratch=[
            pltpu.VMEM(excitation.shape, f32),
            pltpu.VMEM((rank, 2 * rows), bf16),
            pltpu.SMEM(listing.shape, jnp.int32),
            pltpu.SemaphoreType.DMA((13,)),
        ],
    )
    coef = first[:CHUNKS]
    xb, to_pair, to_other, maps0, maps1 = first[CHUNKS:]

    partner = swaps(0, coef)
    pair = lax.ppermute(to_pair, axis, pairs)
    coef = [
        call(
            both_body,
            [piece],
            [ON_CHIP] * 3,
            (coef[c], partner[c], maps0),
            16 * rank * rank * part,
            4 * rank * rank,
        )[0]
        for c in range(CHUNKS)
    ]

    def own_products(level_maps, coef):
        return call(
            own_body,
            [total] * CHUNKS,
            [ON_CHIP] * (CHUNKS + 1),
            (*coef, level_maps),
            8 * rank * rank * width,
            2 * rank * rank,
        )

    partner = swaps(1, coef)
    own = own_products(maps1, coef)
    to_other, *own = lax.optimization_barrier((to_other, *own))
    other = lax.ppermute(to_other, axis, others)
    coef = [
        call(
            cross_body,
            [piece],
            [ON_CHIP] * 3,
            (own[c], partner[c], maps1),
            8 * rank * rank * part,
            2 * rank * rank,
        )[0]
        for c in range(CHUNKS)
    ]
    self_last, cross_last, out_basis, near_tiles, _ = lax.optimization_barrier(
        (self_transfer, cross_transfer, out_basis, near_tiles, coef[0])
    )
    maps2, basis, tiles = call(
        functools.partial(rest_body, levels - 1),
        [maps, pltpu.VMEM((rows, 2 * rank), bf16), pltpu.VMEM(near_tiles.shape, bf16)],
        [OFF_CHIP] * 4,
        (held(self_last), held(cross_last), held(out_basis), held(near_tiles)),
        8 * rank * rank * rank,
        8 * rank * rank,
        scratch=[pltpu.SemaphoreType.DMA((7,))],
    )
    partner = swaps(2, coef)
    own = own_products(maps2, coef)
    near, side = call(
        functools.partial(near_body, axis, count),
        [pltpu.VMEM((rows, 2 * width), f32), pltpu.VMEM((rows, 4 * tile), bf16)],
        [SCALARS] + [ON_CHIP] * 3,
        (listing, tiles, xb, pair),
        8 * slots * tile * tile * width,
        8 * rows * width,
        scratch=[pltpu.VMEM((slots, tile, 2 * width), bf16)],
    )
    out = sums = None
    for c in range(CHUNKS):
        outs = [jax.ShapeDtypeStruct((2, rows, width), f32)]
        if c == 0:
            extra, ins = (side, other), [ON_CHIP] * 2
            outs.append(pltpu.VMEM((rows, 2 * part * (CHUNKS - 1)), f32))
        else:
            near, extra, ins = sums, (out,), [OFF_CHIP]
        out, *left = call(
            functools.partial(last_body, c),
            outs,
            [ON_CHIP] * 5 + ins,
            (own[c], partner[c], maps2, basis, near, *extra),
            8 * rank * (rank + rows) * part,
            8 * rows * part,
            scratch=[
                pltpu.VMEM((rows, 2 * part), f32),
                pltpu.SemaphoreType.DMA((2 * STEPS,)),
            ],
            outs_at=[OFF_CHIP] + [ON_CHIP] * (len(outs) - 1),
            aliases={} if c == 0 else {5: 0},
        )
        sums = left[0] if left else sums
    return out


def solution(mesh):
    placed = (
        P(None, "surf", None),
        P(None, "surf", None),
        P(None, None, "surf", None),
        P(None, None, "surf", None),
        P(None, "surf", None),
        P("surf", None, None, None),
        P(),
    )
    return jax.shard_map(
        per_device, mesh=mesh, in_specs=placed, out_specs=P(None, "surf", None), check_vma=False
    )
```

time: 28.4 us -> 27.9 us (0.982)
  starting transfers between devices: 13.8 us -> 11.6 us
  Pallas kernels: 8.36 us -> 9.52 us
  waiting for transfers between devices: 5.48 us -> 6.02 us
    ppermute x8, starting transfers between devices: 13.8 us -> 11.6 us  [the longest x6 7.15 us: swaps(): lax.ppermute(coef[c], axis, [(i, i ^ 1 << level) for i in range(count)])]
    pallas_call x11, Pallas kernels: 8.36 us -> 9.52 us  [call(): pl.pallas_call(body, out_shape=outs, in_specs=ins, out_specs=outs_at or [...]
    ppermute x8, waiting for transfers between devices: 5.48 us -> 6.02 us  [the longest x6 6.02 us: swaps(): lax.ppermute(coef[c], axis, [(i, i ^ 1 << level) for i in range(count)])]
  transfers between devices with their start and end apart: 8 -> 8, of which waited for: 5 -> 2; matrix products, arithmetic and copies ran while one was open for 0% -> 0% of each run, Pallas kernels for 16% -> 23%
where the time goes in v3:
time: 27.9 us; the launch traced here: 27.7 us
  starting transfers between devices  11.6 us (42%)
  Pallas kernels  9.52 us (34%)
  waiting for transfers between devices  6.02 us (22%)
  local copies, waits for them, and re-layouts  0.38 us (1%)
    pallas_call x11, Pallas kernels, call(): pl.pallas_call(body, out_shape=outs, in_specs=ins, out_specs=outs_at or [...  9.52 us
    ppermute x6, starting transfers between devices, swaps(): lax.ppermute(coef[c], axis, [(i, i ^ 1 << level) for i in range(count)])  7.15 us
    ppermute x6, waiting for transfers between devices, swaps(): lax.ppermute(coef[c], axis, [(i, i ^ 1 << level) for i in range(count)])  6.02 us
    ppermute x1, starting transfers between devices, per_device(): other = lax.ppermute(to_other, axis, others)  4.07 us
  transfers between devices with their start and end apart: 8, of which 2 were waited for; matrix products, arithmetic and copies ran while one was open for 0% of the time, Pallas kernels for 23%

profile of v3, /device:TPU:0, one launch (start us, length us, event | category | flops | bytes accessed | tf_op | source)
XLA Modules:
  0.0 27.7 jit_solution(4378766800672287298)
XLA Ops:
  0.0 1.9 %shard_map.73 = (bf16[256,256]{1,0:T(8,128)(2,1)S(1)}, bf16[256,256]{1,0:T(8,128)(2,1)S(1)}, bf16[512,512]{1,0:T(8,128)(2,1)S(1)}, bf16[2,128,512]{2,1,0:T(8,128...) custom-call(f32[2,512,256]{2,1,0:T(8,128)} %refs_0_.1, ...), custom_call_target="tpu_custom_call" | custom-call | flops 268435456 | bytes 1048576 | tf_op jit(solution)/shard_map/pallas_call | solution.py:21
  1.9 0.6 %collective-permute-start = (bf16[256,256]{1,0:T(8,128)(2,1)S(1)}, bf16[256,256]{1,0:T(8,128)(2,1)S(1)}, u32[]{:S(2)}, u32[]{:S(2)}) collective-permute-start(bf16[256,256]{1,0:T(8,128)(2,1)S(1)} %get-tuple-element.31.coef_ref), channel_id=1, source_target_pairs={{0,1},{1,0},{2,3},{3,2},{4,5},{5,4},{6,7},{7,6},{8,9},{9,8},{10,11... | collective-permute-start | bytes 393224 | tf_op jit(solution)/shard_map/ppermute | solution.py:280
  2.5 0.1 collective-permute-start.1
  2.6 0.4 %collective-permute-start.6 = (bf16[2,128,512]{2,1,0:T(8,128)(2,1)S(1)}, bf16[2,128,512]{2,1,0:T(8,128)(2,1)S(1)}, u32[]{:S(2)}, u32[]{:S(2)}) collective-permute-start(bf16[2,128,512]{2,1,0:T(8,128)(2,1)S(1)} %get-tuple-element.49), channel_id=1, source_target_pairs={{0,1},{1,0},{2,3},{3,2},{4,5},{5,4},{6,7},{7,6},{8,9},{9,8},{10,11... | collective-permute-start | bytes 786440 | tf_op jit(solution)/shard_map/ppermute | solution.py:303
  3.0 0.5 %collective-permute-done.partner_ref = bf16[256,256]{1,0:T(8,128)(2,1)S(1)} collective-permute-done((bf16[256,256]{1,0:T(8,128)(2,1)S(1)}, bf16[256,256]{1,0:T(8,128)(2,1)S(1)}, u32[]{:S(2)}, u32[]{:S(2)}) %collective-permute-start) | collective-permute-done | bytes 131104 | tf_op jit(solution)/shard_map/ppermute | solution.py:280
  3.5 0.3 %shard_map.74.refs_0_ = bf16[256,256]{1,0:T(8,128)(2,1)S(1)} custom-call(bf16[256,256]{1,0:T(8,128)(2,1)S(1)} %get-tuple-element.31.coef_ref, bf16[256,256]{1,0:T(8,128)(2,1)S(1)} %collective-permute-done.partner_ref, bf16[256,1024]{1,0:T(8,128)(2,1)S(1)} %get-tuple-element.32.map_ref), custom_call_target="tpu_custom_call" | custom-call | flops 134217728 | bytes 262144 | tf_op jit(solution)/shard_map/pallas_call | solution.py:21
  3.8 2.9 %collective-permute-start.2 = (bf16[256,256]{1,0:T(8,128)(2,1)S(1)}, bf16[256,256]{1,0:T(8,128)(2,1)S(1)}, u32[]{:S(2)}, u32[]{:S(2)}) collective-permute-start(bf16[256,256]{1,0:T(8,128)(2,1)S(1)} %shard_map.74.refs_0_), channel_id=1, source_target_pairs={{0,2},{1,3},{2,0},{3,1},{4,6},{5,7},{6,4},{7,5},{8,10},{9,11},{10,... | collective-permute-start | bytes 393224 | tf_op jit(solution)/shard_map/ppermute | solution.py:280
  6.7 0.0 collective-permute-done.1.partner_ref
  6.7 0.3 %shard_map.75.refs_1_ = bf16[256,256]{1,0:T(8,128)(2,1)S(1)} custom-call(bf16[256,256]{1,0:T(8,128)(2,1)S(1)} %get-tuple-element.33.coef_ref, bf16[256,256]{1,0:T(8,128)(2,1)S(1)} %collective-permute-done.1.partner_ref, bf16[256,1024]{1,0:T(8,128)(2,1)S(1)} %get-tuple-element.32.map_ref), custom_call_target="tpu_custom_call" | custom-call | flops 134217728 | bytes 262144 | tf_op jit(solution)/shard_map/pallas_call | solution.py:21
  7.0 0.3 %shard_map.76 = (f32[256,256]{1,0:T(8,128)S(1)}, f32[256,256]{1,0:T(8,128)S(1)}) custom-call(bf16[256,256]{1,0:T(8,128)(2,1)S(1)} %shard_map.74.refs_0_, bf16[256,256]{1,0:T(8,128)(2,1)S(1)} %shard_map.75.refs_1_, bf16[256,1024]{1,0:T(8,128)(2,1)S(1)} %get-tuple-element.34.refs_2_.map_ref), custom_call_target="tpu_custom_call" | custom-call | flops 134217728 | bytes 131072 | tf_op jit(solution)/shard_map/pallas_call | solution.py:21
  7.3 4.1 %collective-permute-start.7 = (bf16[2,128,512]{2,1,0:T(8,128)(2,1)S(1)}, bf16[2,128,512]{2,1,0:T(8,128)(2,1)S(1)}, u32[]{:S(2)}, u32[]{:S(2)}) collective-permute-start(bf16[2,128,512]{2,1,0:T(8,128)(2,1)S(1)} %get-tuple-element.52), channel_id=1, source_target_pairs={{0,31},{1,2},{2,1},{3,4},{4,3},{5,6},{6,5},{7,8},{8,7},{9,10},{10,... | collective-permute-start | bytes 786440 | tf_op jit(solution)/shard_map/ppermute | solution.py:329
  11.4 0.0 collective-permute-start.3
  11.4 0.0 collective-permute-done.2.partner_ref
  11.4 0.2 shard_map.77.refs_0_
  11.6 0.9 %collective-permute-start.5 = (bf16[256,256]{1,0:T(8,128)(2,1)S(1)}, bf16[256,256]{1,0:T(8,128)(2,1)S(1)}, u32[]{:S(2)}, u32[]{:S(2)}) collective-permute-start(bf16[256,256]{1,0:T(8,128)(2,1)S(1)} %shard_map.77.refs_0_), channel_id=1, source_target_pairs={{0,4},{1,5},{2,6},{3,7},{4,0},{5,1},{6,2},{7,3},{8,12},{9,13},{10,... | collective-permute-start | bytes 393224 | tf_op jit(solution)/shard_map/ppermute | solution.py:280
  12.6 5.5 %collective-permute-done.3.partner_ref = bf16[256,256]{1,0:T(8,128)(2,1)S(1)} collective-permute-done((bf16[256,256]{1,0:T(8,128)(2,1)S(1)}, bf16[256,256]{1,0:T(8,128)(2,1)S(1)}, u32[]{:S(2)}, u32[]{:S(2)}) %collective-permute-start.3) | collective-permute-done | bytes 131104 | tf_op jit(solution)/shard_map/ppermute | solution.py:280
  18.1 0.2 shard_map.78.refs_1_
  18.4 2.7 %collective-permute-start.4 = (bf16[256,256]{1,0:T(8,128)(2,1)S(1)}, bf16[256,256]{1,0:T(8,128)(2,1)S(1)}, u32[]{:S(2)}, u32[]{:S(2)}) collective-permute-start(bf16[256,256]{1,0:T(8,128)(2,1)S(1)} %shard_map.78.refs_1_), channel_id=1, source_target_pairs={{0,4},{1,5},{2,6},{3,7},{4,0},{5,1},{6,2},{7,3},{8,12},{9,13},{10,... | collective-permute-start | bytes 393224 | tf_op jit(solution)/shard_map/ppermute | solution.py:280
  21.0 1.5 %shard_map.79 = (bf16[256,1024]{1,0:T(8,128)(2,1)S(1)}, bf16[512,512]{1,0:T(8,128)(2,1)S(1)}, bf16[6,2,128,128]{3,2,1,0:T(8,128)(2,1)S(1)}) custom-call(bf16[3,2,256,256]{3,2,1,0:T(8,128)(2,1)} %self_hbm, bf16[3,2,256,256]{3,2,1,0:T(8,128)(2,1)} %cross_hbm, bf16[2,512,256]{2,1,0:T(8,128)(2,1)} %basis_hbm, bf16[6,2,128,128]{3,2,1,0:T(8,128)(2,1)} %tiles_hbm), custom_call_target="tpu_custom_call" | custom-call | flops 134217728 | bytes 524288 | tf_op jit(solution)/shard_map/pallas_call | solution.py:21
  22.5 0.0 copy-start
  22.5 0.3 %shard_map.80 = (f32[256,256]{1,0:T(8,128)S(1)}, f32[256,256]{1,0:T(8,128)S(1)}) custom-call(bf16[256,256]{1,0:T(8,128)(2,1)S(1)} %shard_map.77.refs_0_, bf16[256,256]{1,0:T(8,128)(2,1)S(1)} %shard_map.78.refs_1_, bf16[256,1024]{1,0:T(8,128)(2,1)S(1)} %get-tuple-element.43.refs_2_), custom_call_target="tpu_custom_call" | custom-call | flops 134217728 | bytes 131072 | tf_op jit(solution)/shard_map/pallas_call | solution.py:21
  22.8 0.0 collective-permute-done.6.pair_ref
  22.8 0.4 %copy-done = s32[32,6,3]{0,2,1:T(4,128)S(1)} copy-done((s32[32,6,3]{0,2,1:T(4,128)S(1)}, s32[32,6,3]{0,2,1:T(4,128)}, u32[]{:S(2)}) %copy-start) | copy-done | bytes 2328
  23.2 1.6 %shard_map.81 = (f32[512,512]{1,0:T(8,128)S(1)}, bf16[512,512]{1,0:T(8,128)(2,1)S(1)}) custom-call(s32[6,3,32]{2,1,0:T(4,128)S(1)} %bitcast.2, bf16[6,2,128,128]{3,2,1,0:T(8,128)(2,1)S(1)} %get-tuple-element.47.tiles_ref, bf16[512,512]{1,0:T(8,128)(2,1)S(1)} %get-tuple-element.48.xb_ref, bf16[2,128,512]{2,1,0:T(8,128)(2,1)S(1)} %collective-permute-done.6.pair_ref), custom_call_target="tpu_custom_call" | custom-call | flops 201326592 | bytes 1048576 | tf_op jit(solution)/shard_map/pallas_call | solution.py:21
  24.8 0.0 collective-permute-done.5.refs_1_
  24.8 0.0 collective-permute-done.7.refs_6_
  24.9 1.5 %shard_map.82 = (f32[2,512,256]{2,1,0:T(8,128)}, f32[512,256]{1,0:T(8,128)S(1)}) custom-call(f32[256,256]{1,0:T(8,128)S(1)} %get-tuple-element.46.refs_0_, bf16[256,256]{1,0:T(8,128)(2,1)S(1)} %collective-permute-done.5.refs_1_, bf16[256,1024]{1,0:T(8,128)(2,1)S(1)} %get-tuple-element.43.refs_2_, bf16[512,512]{1,0:T(8,128)(2,1)S(1)} %get-tuple-element.45.refs_3_, ...), custom_call_target="tpu_custom_call" | custom-call | flops 201326592 | bytes 524288 | tf_op jit(solution)/shard_map/pallas_call | solution.py:21
  26.3 0.0 collective-permute-done.4.refs_1_
  26.3 1.4 %shard_map.83 = f32[2,512,256]{2,1,0:T(8,128)} custom-call(f32[256,256]{1,0:T(8,128)S(1)} %get-tuple-element.44.refs_0_, bf16[256,256]{1,0:T(8,128)(2,1)S(1)} %collective-permute-done.4.refs_1_, bf16[256,1024]{1,0:T(8,128)(2,1)S(1)} %get-tuple-element.43.refs_2_, bf16[512,512]{1,0:T(8,128)(2,1)S(1)} %get-tuple-element.45.refs_3_, ...), custom_call_target="tpu_custom_call", output_to_operand_aliasing={{}: (5, {})} | custom-call | flops 201326592 | bytes 524288 | tf_op jit(solution)/shard_map/pallas_call | solution.py:21
Async XLA Ops:
  1.9 1.5 %collective-permute-start = (bf16[256,256]{1,0:T(8,128)(2,1)S(1)}, bf16[256,256]{1,0:T(8,128)(2,1)S(1)}, u32[]{:S(2)}, u32[]{:S(2)}) collective-permute-start(bf16[256,256]{1,0:T(8,128)(2,1)S(1)} %get-tuple-element.31.coef_ref), channel_id=1, source_target_pairs={{0,1},{1,0},{2,3},{3,2},{4,5},{5,4},{6,7},{7,6},{8,9},{9,8},{10,11... | collective-permute-start | bytes 393224 | tf_op jit(solution)/shard_map/ppermute | solution.py:280
  2.5 4.2 %collective-permute-start.1 = (bf16[256,256]{1,0:T(8,128)(2,1)S(1)}, bf16[256,256]{1,0:T(8,128)(2,1)S(1)}, u32[]{:S(2)}, u32[]{:S(2)}) collective-permute-start(bf16[256,256]{1,0:T(8,128)(2,1)S(1)} %get-tuple-element.33.coef_ref), channel_id=1, source_target_pairs={{0,1},{1,0},{2,3},{3,2},{4,5},{5,4},{6,7},{7,6},{8,9},{9,8},{10,11... | collective-permute-start | bytes 393224 | tf_op jit(solution)/shard_map/ppermute | solution.py:280
  2.6 20.2 %collective-permute-start.6 = (bf16[2,128,512]{2,1,0:T(8,128)(2,1)S(1)}, bf16[2,128,512]{2,1,0:T(8,128)(2,1)S(1)}, u32[]{:S(2)}, u32[]{:S(2)}) collective-permute-start(bf16[2,128,512]{2,1,0:T(8,128)(2,1)S(1)} %get-tuple-element.49), channel_id=1, source_target_pairs={{0,1},{1,0},{2,3},{3,2},{4,5},{5,4},{6,7},{7,6},{8,9},{9,8},{10,11... | collective-permute-start | bytes 786440 | tf_op jit(solution)/shard_map/ppermute | solution.py:303
  3.8 7.6 %collective-permute-start.2 = (bf16[256,256]{1,0:T(8,128)(2,1)S(1)}, bf16[256,256]{1,0:T(8,128)(2,1)S(1)}, u32[]{:S(2)}, u32[]{:S(2)}) collective-permute-start(bf16[256,256]{1,0:T(8,128)(2,1)S(1)} %shard_map.74.refs_0_), channel_id=1, source_target_pairs={{0,2},{1,3},{2,0},{3,1},{4,6},{5,7},{6,4},{7,5},{8,10},{9,11},{10,... | collective-permute-start | bytes 393224 | tf_op jit(solution)/shard_map/ppermute | solution.py:280
  7.3 17.5 %collective-permute-start.7 = (bf16[2,128,512]{2,1,0:T(8,128)(2,1)S(1)}, bf16[2,128,512]{2,1,0:T(8,128)(2,1)S(1)}, u32[]{:S(2)}, u32[]{:S(2)}) collective-permute-start(bf16[2,128,512]{2,1,0:T(8,128)(2,1)S(1)} %get-tuple-element.52), channel_id=1, source_target_pairs={{0,31},{1,2},{2,1},{3,4},{4,3},{5,6},{6,5},{7,8},{8,7},{9,10},{10,... | collective-permute-start | bytes 786440 | tf_op jit(solution)/shard_map/ppermute | solution.py:329
  11.4 6.7 %collective-permute-start.3 = (bf16[256,256]{1,0:T(8,128)(2,1)S(1)}, bf16[256,256]{1,0:T(8,128)(2,1)S(1)}, u32[]{:S(2)}, u32[]{:S(2)}) collective-permute-start(bf16[256,256]{1,0:T(8,128)(2,1)S(1)} %shard_map.75.refs_1_), channel_id=1, source_target_pairs={{0,2},{1,3},{2,0},{3,1},{4,6},{5,7},{6,4},{7,5},{8,10},{9,11},{10,... | collective-permute-start | bytes 393224 | tf_op jit(solution)/shard_map/ppermute | solution.py:280
  11.6 13.2 %collective-permute-start.5 = (bf16[256,256]{1,0:T(8,128)(2,1)S(1)}, bf16[256,256]{1,0:T(8,128)(2,1)S(1)}, u32[]{:S(2)}, u32[]{:S(2)}) collective-permute-start(bf16[256,256]{1,0:T(8,128)(2,1)S(1)} %shard_map.77.refs_0_), channel_id=1, source_target_pairs={{0,4},{1,5},{2,6},{3,7},{4,0},{5,1},{6,2},{7,3},{8,12},{9,13},{10,... | collective-permute-start | bytes 393224 | tf_op jit(solution)/shard_map/ppermute | solution.py:280
  18.4 8.0 %collective-permute-start.4 = (bf16[256,256]{1,0:T(8,128)(2,1)S(1)}, bf16[256,256]{1,0:T(8,128)(2,1)S(1)}, u32[]{:S(2)}, u32[]{:S(2)}) collective-permute-start(bf16[256,256]{1,0:T(8,128)(2,1)S(1)} %shard_map.78.refs_1_), channel_id=1, source_target_pairs={{0,4},{1,5},{2,6},{3,7},{4,0},{5,1},{6,2},{7,3},{8,12},{9,13},{10,... | collective-permute-start | bytes 393224 | tf_op jit(solution)/shard_map/ppermute | solution.py:280
  22.5 0.7 %copy-start = (s32[32,6,3]{0,2,1:T(4,128)S(1)}, s32[32,6,3]{0,2,1:T(4,128)}, u32[]{:S(2)}) copy-start(s32[32,6,3]{0,2,1:T(4,128)} %param.13) | copy-start | bytes 6916

commit v4 on v3

--- a/solution.py
+++ b/solution.py
@@ -45,6 +45,11 @@
     return jnp.concatenate([w for v in vs for w in (v, turned(v))], axis=0)
 
 
+def chunk_lanes(width):
+    step = 2 * width // CHUNKS
+    return [slice(c * step, (c + 1) * step) for c in range(CHUNKS)]
+
+
 def flat(ref, lanes):
     return jnp.concatenate([ref[k, :, lanes] for k in range(ref.shape[0])], axis=0)
 
@@ -106,13 +111,14 @@
     for level, ref in enumerate(map_refs):
         later += fetches.maps(level, self_hbm, cross_hbm, ref)
 
-    part = x_ref.shape[2] // CHUNKS
+    width = x_ref.shape[2]
+    half = width // CHUNKS
     for copy in excitation:
         copy.wait()
     for c in range(CHUNKS):
         for k in range(2):
-            at = (2 * c + k) * part
-            xb_ref[:, at : at + part] = x_ref[k, :, c * part : (c + 1) * part].astype(
+            at = (2 * c + k) * half
+            xb_ref[:, at : at + half] = x_ref[k, :, c * half : (c + 1) * half].astype(
                 jnp.bfloat16
             )
     listing.wait()
@@ -125,9 +131,8 @@
             ref[k] = xb_ref[rows, :]
     for copy in leaf:
         copy.wait()
-    for c, ref in enumerate(coef_refs):
-        v = xb_ref[:, 2 * c * part : 2 * (c + 1) * part]
-        ref[...] = dot(leaf_ref[...], stacked(v)).astype(ref.dtype)
+    for lanes, ref in zip(chunk_lanes(width), coef_refs):
+        ref[...] = dot(leaf_ref[...], stacked(xb_ref[:, lanes])).astype(ref.dtype)
     for copy in later:
         copy.wait()
 
@@ -199,56 +204,70 @@
                     + tiles_ref[slot, k].astype(jnp.float32)
                 ).astype(map_ref.dtype)
 
-    wide = xb_ref.shape[1] // CHUNKS
     for slot in range(slots):
         row = list_ref[slot, 1, here]
         rows = pl.ds(pl.multiple_of(row * tile, tile), tile)
-        for c in range(CHUNKS):
-            v = block_ref[slot, :, c * wide : (c + 1) * wide]
+        for lanes in chunk_lanes(xb_ref.shape[1] // 2):
+            v = block_ref[slot, :, lanes]
             term = dot(tiles_ref[slot, 0], v) + dot(tiles_ref[slot, 1], turned(v))
-            near_ref[rows, c * wide : (c + 1) * wide] += term
-
-
-def last_body(c, *refs):
-    own_ref, partner_ref, map_ref, basis_ref, near_ref = refs[:5]
-    if c == 0:
-        side_ref, other_ref, out_hbm, sum_ref, result_ref, sems = refs[5:]
-    else:
-        _, out_hbm, result_ref, sems = refs[5:]
+            near_ref[rows, lanes] += term
+
+
+def base_body(*refs):
+    coef_refs = refs[:CHUNKS]
+    map_ref, basis_ref, near_ref, base_ref, fold_ref = refs[CHUNKS:]
     half = map_ref.shape[1] // 2
-    v = own_ref[...] + dot(map_ref[:, half:], stacked(partner_ref[...]))
-    v = stacked(v.astype(jnp.bfloat16))
-    wide = v.shape[1]
-    part = wide // 2
-    rows = basis_ref.shape[0]
+    for lanes, ref in zip(chunk_lanes(near_ref.shape[1] // 2), coef_refs):
+        v = dot(map_ref[:, :half], stacked(ref[...])).astype(jnp.bfloat16)
+        base_ref[:, lanes] = near_ref[:, lanes] + dot(basis_ref[...], stacked(v))
+    fold_ref[...] = dot(basis_ref[...], stacked(map_ref[:, half:])).astype(fold_ref.dtype)
+
+
+def send_rows(result_ref, out_hbm, sems, piece, at, number):
+    half = result_ref.shape[1] // 2
+    copies = []
+    for k in range(2):
+        copy = pltpu.make_async_copy(
+            result_ref.at[piece, k * half : (k + 1) * half],
+            out_hbm.at[k, piece, at : at + half],
+            sems.at[2 * number + k],
+        )
+        copy.start()
+        copies.append(copy)
+    return copies
+
+
+def last0_body(
+    partner_ref, fold_ref, base_ref, side_ref, other_ref, out_hbm, left_ref, result_ref, sems
+):
+    rows, width = result_ref.shape
+    main, small = chunk_lanes(width)
+    v = stacked(partner_ref[...])
+    near_main, near_small = stacked(flat(other_ref, main)), stacked(flat(other_ref, small))
     step = rows // STEPS
     copies = []
-    if c == 0:
-        side = [
-            stacked(flat(other_ref, slice(d * wide, (d + 1) * wide))) for d in range(CHUNKS)
-        ]
-    for r in range(0, rows, step):
-        piece = slice(r, r + step)
-        total = dot(basis_ref[piece, :], v)
-        if c == 0:
-            total = total + near_ref[piece, :wide] + dot(side_ref[piece, :], side[0])
-        else:
-            total = total + near_ref[piece, (c - 1) * wide : c * wide]
-        result_ref[piece, :] = total
-        for k in range(2):
-            copy = pltpu.make_async_copy(
-                result_ref.at[piece, k * part : (k + 1) * part],
-                out_hbm.at[k, piece, c * part : (c + 1) * part],
-                sems.at[len(copies)],
-            )
-            copy.start()
-            copies.append(copy)
-    if c == 0:
-        for d in range(1, CHUNKS):
-            lanes = slice((d - 1) * wide, d * wide)
-            sum_ref[:, lanes] = near_ref[:, d * wide : (d + 1) * wide] + dot(
-                side_ref[...], side[d]
-            )
+    for i in range(STEPS):
+        piece = slice(i * step, (i + 1) * step)
+        result_ref[piece, :] = (
+            base_ref[piece, main]
+            + dot(fold_ref[piece, :], v)
+            + dot(side_ref[piece, :], near_main)
+        )
+        copies += send_rows(result_ref, out_hbm, sems, piece, 0, i)
+    left_ref[...] = base_ref[:, small] + dot(side_ref[...], near_small)
+    for copy in copies:
+        copy.wait()
+
+
+def last1_body(partner_ref, fold_ref, left_ref, before_hbm, out_hbm, result_ref, sems):
+    rows, width = result_ref.shape
+    v = stacked(partner_ref[...])
+    step = rows // STEPS
+    copies = []
+    for i in range(STEPS):
+        piece = slice(i * step, (i + 1) * step)
+        result_ref[piece, :] = left_ref[piece, :] + dot(fold_ref[piece, :], v)
+        copies += send_rows(result_ref, out_hbm, sems, piece, width // 2, i)
     for copy in copies:
         copy.wait()
 
@@ -262,10 +281,10 @@
     rank = leaf_basis.shape[1]
     slots, _, tile, _ = near_tiles.shape
     levels = self_transfer.shape[0]
-    part = width // CHUNKS
     bf16, f32 = jnp.bfloat16, jnp.float32
-    piece = pltpu.VMEM((rank, 2 * part), bf16)
-    total = pltpu.VMEM((rank, 2 * part), f32)
+    sizes = [lanes.stop - lanes.start for lanes in chunk_lanes(width)]
+    pieces = [pltpu.VMEM((rank, n), bf16) for n in sizes]
+    totals = [pltpu.VMEM((rank, n), f32) for n in sizes]
     sent = pltpu.VMEM((2, tile, 2 * width), bf16)
     maps = pltpu.VMEM((rank, 4 * rank), bf16)
     pairs = [(i, i ^ 1) for i in range(count)]
@@ -284,7 +303,7 @@
     listing = near_list.transpose(1, 2, 0)
     first = call(
         functools.partial(first_body, axis, count),
-        [piece] * CHUNKS + [pltpu.VMEM((rows, 2 * width), bf16), sent, sent, maps, maps],
+        pieces + [pltpu.VMEM((rows, 2 * width), bf16), sent, sent, maps, maps],
         [OFF_CHIP] * 5,
         (held(excitation), held(leaf_basis), self_transfer, cross_transfer, held(listing)),
         8 * rank * rows * width,
@@ -304,10 +323,10 @@
     coef = [
         call(
             both_body,
-            [piece],
+            [pieces[c]],
             [ON_CHIP] * 3,
             (coef[c], partner[c], maps0),
-            16 * rank * rank * part,
+            8 * rank * rank * sizes[c],
             4 * rank * rank,
         )[0]
         for c in range(CHUNKS)
@@ -316,7 +335,7 @@
     def own_products(level_maps, coef):
         return call(
             own_body,
-            [total] * CHUNKS,
+            totals,
             [ON_CHIP] * (CHUNKS + 1),
             (*coef, level_maps),
             8 * rank * rank * width,
@@ -330,16 +349,16 @@
     coef = [
         call(
             cross_body,
-            [piece],
+            [pieces[c]],
             [ON_CHIP] * 3,
             (own[c], partner[c], maps1),
-            8 * rank * rank * part,
+            4 * rank * rank * sizes[c],
             2 * rank * rank,
         )[0]
         for c in range(CHUNKS)
     ]
     self_last, cross_last, out_basis, near_tiles, _ = lax.optimization_barrier(
-        (self_transfer, cross_transfer, out_basis, near_tiles, coef[0])
+        (self_transfer, cross_transfer, out_basis, near_tiles, own[0])
     )
     maps2, basis, tiles = call(
         functools.partial(rest_body, levels - 1),
@@ -351,7 +370,6 @@
         scratch=[pltpu.SemaphoreType.DMA((7,))],
     )
     partner = swaps(2, coef)
-    own = own_products(maps2, coef)
     near, side = call(
         functools.partial(near_body, axis, count),
         [pltpu.VMEM((rows, 2 * width), f32), pltpu.VMEM((rows, 4 * tile), bf16)],
@@ -361,30 +379,37 @@
         8 * rows * width,
         scratch=[pltpu.VMEM((slots, tile, 2 * width), bf16)],
     )
-    out = sums = None
-    for c in range(CHUNKS):
-        outs = [jax.ShapeDtypeStruct((2, rows, width), f32)]
-        if c == 0:
-            extra, ins = (side, other), [ON_CHIP] * 2
-            outs.append(pltpu.VMEM((rows, 2 * part * (CHUNKS - 1)), f32))
-        else:
-            near, extra, ins = sums, (out,), [OFF_CHIP]
-        out, *left = call(
-            functools.partial(last_body, c),
-            outs,
-            [ON_CHIP] * 5 + ins,
-            (own[c], partner[c], maps2, basis, near, *extra),
-            8 * rank * (rank + rows) * part,
-            8 * rows * part,
-            scratch=[
-                pltpu.VMEM((rows, 2 * part), f32),
-                pltpu.SemaphoreType.DMA((2 * STEPS,)),
-            ],
-            outs_at=[OFF_CHIP] + [ON_CHIP] * (len(outs) - 1),
-            aliases={} if c == 0 else {5: 0},
-        )
-        sums = left[0] if left else sums
-    return out
+    base, fold = call(
+        base_body,
+        [pltpu.VMEM((rows, 2 * width), f32), pltpu.VMEM((rows, 2 * rank), bf16)],
+        [ON_CHIP] * (CHUNKS + 3),
+        (*coef, maps2, basis, near),
+        8 * rows * rank * (rank + width),
+        8 * rows * width,
+    )
+    whole = jax.ShapeDtypeStruct((2, rows, width), f32)
+    scratch = [pltpu.VMEM((rows, width), f32), pltpu.SemaphoreType.DMA((2 * STEPS,))]
+    out, left = call(
+        last0_body,
+        [whole, pltpu.VMEM((rows, width), f32)],
+        [ON_CHIP] * 5,
+        (partner[0], fold, base, side, other),
+        8 * rows * (rank + tile) * width,
+        8 * rows * width,
+        scratch=scratch,
+        outs_at=[OFF_CHIP, ON_CHIP],
+    )
+    return call(
+        last1_body,
+        [whole],
+        [ON_CHIP] * 3 + [OFF_CHIP],
+        (partner[1], fold, left, out),
+        2 * rows * rank * width,
+        4 * rows * width,
+        scratch=scratch,
+        outs_at=[OFF_CHIP],
+        aliases={3: 0},
+    )[0]
 
 
 def solution(mesh):

time: 27.9 us -> 27.8 us (level)
  local copies, waits for them, and re-layouts: 0.38 us -> 0.01 us
  Pallas kernels: 9.52 us -> 9.8 us
    unnamed x2, local copies, waits for them, and re-layouts: 0.38 us -> 0.01 us
  transfers between devices with their start and end apart: 8 -> 8, of which waited for: 2 -> 2; matrix products, arithmetic and copies ran while one was open for 0% -> 0% of each run, Pallas kernels for 23% -> 25%
where the time goes in v4:
time: 27.8 us; the launch traced here: 27.6 us
  starting transfers between devices  11.6 us (42%)
  Pallas kernels  9.8 us (35%)
  waiting for transfers between devices  6.02 us (22%)
    pallas_call x11, Pallas kernels, call(): pl.pallas_call(body, out_shape=outs, in_specs=ins, out_specs=outs_at or [...  9.8 us
    ppermute x6, starting transfers between devices, swaps(): lax.ppermute(coef[c], axis, [(i, i ^ 1 << level) for i in range(count)])  7.15 us
    ppermute x6, waiting for transfers between devices, swaps(): lax.ppermute(coef[c], axis, [(i, i ^ 1 << level) for i in range(count)])  6.02 us
    ppermute x1, starting transfers between devices, per_device(): other = lax.ppermute(to_other, axis, others)  4.07 us
  transfers between devices with their start and end apart: 8, of which 2 were waited for; matrix products, arithmetic and copies ran while one was open for 0% of the time, Pallas kernels for 25%

profile of v4, /device:TPU:0, one launch (start us, length us, event | category | flops | bytes accessed | tf_op | source)
XLA Modules:
  0.0 27.6 jit_solution(10377135834448899519)
XLA Ops:
  0.0 1.9 %shard_map.73 = (bf16[256,256]{1,0:T(8,128)(2,1)S(1)}, bf16[256,256]{1,0:T(8,128)(2,1)S(1)}, bf16[512,512]{1,0:T(8,128)(2,1)S(1)}, bf16[2,128,512]{2,1,0:T(8,128...) custom-call(f32[2,512,256]{2,1,0:T(8,128)} %refs_0_.1, ...), custom_call_target="tpu_custom_call" | custom-call | flops 268435456 | bytes 1048576 | tf_op jit(solution)/shard_map/pallas_call | solution.py:21
  1.9 0.6 %collective-permute-start = (bf16[256,256]{1,0:T(8,128)(2,1)S(1)}, bf16[256,256]{1,0:T(8,128)(2,1)S(1)}, u32[]{:S(2)}, u32[]{:S(2)}) collective-permute-start(bf16[256,256]{1,0:T(8,128)(2,1)S(1)} %get-tuple-element.31.coef_ref), channel_id=1, source_target_pairs={{0,1},{1,0},{2,3},{3,2},{4,5},{5,4},{6,7},{7,6},{8,9},{9,8},{10,11... | collective-permute-start | bytes 393224 | tf_op jit(solution)/shard_map/ppermute | solution.py:299
  2.5 0.1 collective-permute-start.1
  2.6 0.4 %collective-permute-start.5 = (bf16[2,128,512]{2,1,0:T(8,128)(2,1)S(1)}, bf16[2,128,512]{2,1,0:T(8,128)(2,1)S(1)}, u32[]{:S(2)}, u32[]{:S(2)}) collective-permute-start(bf16[2,128,512]{2,1,0:T(8,128)(2,1)S(1)} %get-tuple-element.47), channel_id=1, source_target_pairs={{0,1},{1,0},{2,3},{3,2},{4,5},{5,4},{6,7},{7,6},{8,9},{9,8},{10,11... | collective-permute-start | bytes 786440 | tf_op jit(solution)/shard_map/ppermute | solution.py:322
  3.0 0.5 %collective-permute-done.partner_ref = bf16[256,256]{1,0:T(8,128)(2,1)S(1)} collective-permute-done((bf16[256,256]{1,0:T(8,128)(2,1)S(1)}, bf16[256,256]{1,0:T(8,128)(2,1)S(1)}, u32[]{:S(2)}, u32[]{:S(2)}) %collective-permute-start) | collective-permute-done | bytes 131104 | tf_op jit(solution)/shard_map/ppermute | solution.py:299
  3.5 0.3 %shard_map.74.refs_0_ = bf16[256,256]{1,0:T(8,128)(2,1)S(1)} custom-call(bf16[256,256]{1,0:T(8,128)(2,1)S(1)} %get-tuple-element.31.coef_ref, bf16[256,256]{1,0:T(8,128)(2,1)S(1)} %collective-permute-done.partner_ref, bf16[256,1024]{1,0:T(8,128)(2,1)S(1)} %get-tuple-element.32.map_ref), custom_call_target="tpu_custom_call" | custom-call | flops 134217728 | bytes 262144 | tf_op jit(solution)/shard_map/pallas_call | solution.py:21
  3.8 2.9 %collective-permute-start.4 = (bf16[256,256]{1,0:T(8,128)(2,1)S(1)}, bf16[256,256]{1,0:T(8,128)(2,1)S(1)}, u32[]{:S(2)}, u32[]{:S(2)}) collective-permute-start(bf16[256,256]{1,0:T(8,128)(2,1)S(1)} %shard_map.74.refs_0_), channel_id=1, source_target_pairs={{0,2},{1,3},{2,0},{3,1},{4,6},{5,7},{6,4},{7,5},{8,10},{9,11},{10,... | collective-permute-start | bytes 393224 | tf_op jit(solution)/shard_map/ppermute | solution.py:299
  6.7 0.0 collective-permute-done.1.partner_ref
  6.7 0.3 %shard_map.75.refs_1_ = bf16[256,256]{1,0:T(8,128)(2,1)S(1)} custom-call(bf16[256,256]{1,0:T(8,128)(2,1)S(1)} %get-tuple-element.33.coef_ref, bf16[256,256]{1,0:T(8,128)(2,1)S(1)} %collective-permute-done.1.partner_ref, bf16[256,1024]{1,0:T(8,128)(2,1)S(1)} %get-tuple-element.32.map_ref), custom_call_target="tpu_custom_call" | custom-call | flops 134217728 | bytes 262144 | tf_op jit(solution)/shard_map/pallas_call | solution.py:21
  7.0 0.3 %shard_map.76 = (f32[256,256]{1,0:T(8,128)S(1)}, f32[256,256]{1,0:T(8,128)S(1)}) custom-call(bf16[256,256]{1,0:T(8,128)(2,1)S(1)} %shard_map.74.refs_0_, bf16[256,256]{1,0:T(8,128)(2,1)S(1)} %shard_map.75.refs_1_, bf16[256,1024]{1,0:T(8,128)(2,1)S(1)} %get-tuple-element.34.refs_2_.map_ref), custom_call_target="tpu_custom_call" | custom-call | flops 134217728 | bytes 131072 | tf_op jit(solution)/shard_map/pallas_call | solution.py:21
  7.3 4.1 %collective-permute-start.7 = (bf16[2,128,512]{2,1,0:T(8,128)(2,1)S(1)}, bf16[2,128,512]{2,1,0:T(8,128)(2,1)S(1)}, u32[]{:S(2)}, u32[]{:S(2)}) collective-permute-start(bf16[2,128,512]{2,1,0:T(8,128)(2,1)S(1)} %get-tuple-element.52), channel_id=1, source_target_pairs={{0,31},{1,2},{2,1},{3,4},{4,3},{5,6},{6,5},{7,8},{8,7},{9,10},{10,... | collective-permute-start | bytes 786440 | tf_op jit(solution)/shard_map/ppermute | solution.py:348
  11.4 0.0 collective-permute-start.2
  11.4 0.0 collective-permute-done.4.partner_ref
  11.4 0.2 shard_map.78.refs_0_
  11.6 0.9 %collective-permute-start.6 = (bf16[256,256]{1,0:T(8,128)(2,1)S(1)}, bf16[256,256]{1,0:T(8,128)(2,1)S(1)}, u32[]{:S(2)}, u32[]{:S(2)}) collective-permute-start(bf16[256,256]{1,0:T(8,128)(2,1)S(1)} %shard_map.78.refs_0_), channel_id=1, source_target_pairs={{0,4},{1,5},{2,6},{3,7},{4,0},{5,1},{6,2},{7,3},{8,12},{9,13},{10,... | collective-permute-start | bytes 393224 | tf_op jit(solution)/shard_map/ppermute | solution.py:299
  12.6 5.5 %collective-permute-done.2.partner_ref = bf16[256,256]{1,0:T(8,128)(2,1)S(1)} collective-permute-done((bf16[256,256]{1,0:T(8,128)(2,1)S(1)}, bf16[256,256]{1,0:T(8,128)(2,1)S(1)}, u32[]{:S(2)}, u32[]{:S(2)}) %collective-permute-start.2) | collective-permute-done | bytes 131104 | tf_op jit(solution)/shard_map/ppermute | solution.py:299
  18.1 0.2 shard_map.77.refs_1_
  18.4 2.7 %collective-permute-start.3 = (bf16[256,256]{1,0:T(8,128)(2,1)S(1)}, bf16[256,256]{1,0:T(8,128)(2,1)S(1)}, u32[]{:S(2)}, u32[]{:S(2)}) collective-permute-start(bf16[256,256]{1,0:T(8,128)(2,1)S(1)} %shard_map.77.refs_1_), channel_id=1, source_target_pairs={{0,4},{1,5},{2,6},{3,7},{4,0},{5,1},{6,2},{7,3},{8,12},{9,13},{10,... | collective-permute-start | bytes 393224 | tf_op jit(solution)/shard_map/ppermute | solution.py:299
  21.0 0.0 copy-start
  21.0 1.5 %shard_map.79 = (bf16[256,1024]{1,0:T(8,128)(2,1)S(1)}, bf16[512,512]{1,0:T(8,128)(2,1)S(1)}, bf16[6,2,128,128]{3,2,1,0:T(8,128)(2,1)S(1)}) custom-call(bf16[3,2,256,256]{3,2,1,0:T(8,128)(2,1)} %self_hbm, bf16[3,2,256,256]{3,2,1,0:T(8,128)(2,1)} %cross_hbm, bf16[2,512,256]{2,1,0:T(8,128)(2,1)} %basis_hbm, bf16[6,2,128,128]{3,2,1,0:T(8,128)(2,1)} %tiles_hbm), custom_call_target="tpu_custom_call" | custom-call | flops 134217728 | bytes 524288 | tf_op jit(solution)/shard_map/pallas_call | solution.py:21
  22.5 0.0 collective-permute-done.5.pair_ref
  22.5 0.0 copy-done
  22.5 1.6 %shard_map.80 = (f32[512,512]{1,0:T(8,128)S(1)}, bf16[512,512]{1,0:T(8,128)(2,1)S(1)}) custom-call(s32[6,3,32]{2,1,0:T(4,128)S(1)} %bitcast.2, bf16[6,2,128,128]{3,2,1,0:T(8,128)(2,1)S(1)} %get-tuple-element.45.tiles_ref, bf16[512,512]{1,0:T(8,128)(2,1)S(1)} %get-tuple-element.46.xb_ref, bf16[2,128,512]{2,1,0:T(8,128)(2,1)S(1)} %collective-permute-done.5.pair_ref), custom_call_target="tpu_custom_call" | custom-call | flops 201326592 | bytes 1048576 | tf_op jit(solution)/shard_map/pallas_call | solution.py:21
  24.2 1.1 %shard_map.81 = (f32[512,512]{1,0:T(8,128)S(1)}, bf16[512,512]{1,0:T(8,128)(2,1)S(1)}) custom-call(bf16[256,256]{1,0:T(8,128)(2,1)S(1)} %shard_map.78.refs_0_, bf16[256,256]{1,0:T(8,128)(2,1)S(1)} %shard_map.77.refs_1_, bf16[256,1024]{1,0:T(8,128)(2,1)S(1)} %get-tuple-element.43.refs_2_, bf16[512,512]{1,0:T(8,128)(2,1)S(1)} %get-tuple-element.44.refs_3_, ...), custom_call_target="tpu_custom_call" | custom-call | flops 536870912 | bytes 1048576 | tf_op jit(solution)/shard_map/pallas_call | solution.py:21
  25.2 0.0 collective-permute-done.6.partner_ref
  25.3 0.0 collective-permute-done.7.other_ref
  25.3 1.2 %shard_map.82 = (f32[2,512,256]{2,1,0:T(8,128)}, f32[512,256]{1,0:T(8,128)S(1)}) custom-call(bf16[256,256]{1,0:T(8,128)(2,1)S(1)} %collective-permute-done.6.partner_ref, bf16[512,512]{1,0:T(8,128)(2,1)S(1)} %get-tuple-element.49.fold_ref, f32[512,512]{1,0:T(8,128)S(1)} %get-tuple-element.50.base_ref, bf16[512,512]{1,0:T(8,128)(2,1)S(1)} %get-tuple-element.51.side_ref, ...), custom_call_target="tpu_custom_call" | custom-call | flops 402653184 | bytes 1048576 | tf_op jit(solution)/shard_map/pallas_call | solution.py:21
  26.5 0.0 collective-permute-done.3.partner_ref
  26.5 1.1 %shard_map.83 = f32[2,512,256]{2,1,0:T(8,128)} custom-call(bf16[256,256]{1,0:T(8,128)(2,1)S(1)} %collective-permute-done.3.partner_ref, bf16[512,512]{1,0:T(8,128)(2,1)S(1)} %get-tuple-element.49.fold_ref, f32[512,256]{1,0:T(8,128)S(1)} %get-tuple-element.53.left_ref, f32[2,512,256]{2,1,0:T(8,128)} %get-tuple-element.54.before_hbm), custom_call_target="tpu_custom_call", output_to_operand_aliasing={{}: (3, {})} | custom-call | flops 67108864 | bytes 524288 | tf_op jit(solution)/shard_map/pallas_call | solution.py:21
Async XLA Ops:
  1.9 1.5 %collective-permute-start = (bf16[256,256]{1,0:T(8,128)(2,1)S(1)}, bf16[256,256]{1,0:T(8,128)(2,1)S(1)}, u32[]{:S(2)}, u32[]{:S(2)}) collective-permute-start(bf16[256,256]{1,0:T(8,128)(2,1)S(1)} %get-tuple-element.31.coef_ref), channel_id=1, source_target_pairs={{0,1},{1,0},{2,3},{3,2},{4,5},{5,4},{6,7},{7,6},{8,9},{9,8},{10,11... | collective-permute-start | bytes 393224 | tf_op jit(solution)/shard_map/ppermute | solution.py:299
  2.5 4.2 %collective-permute-start.1 = (bf16[256,256]{1,0:T(8,128)(2,1)S(1)}, bf16[256,256]{1,0:T(8,128)(2,1)S(1)}, u32[]{:S(2)}, u32[]{:S(2)}) collective-permute-start(bf16[256,256]{1,0:T(8,128)(2,1)S(1)} %get-tuple-element.33.coef_ref), channel_id=1, source_target_pairs={{0,1},{1,0},{2,3},{3,2},{4,5},{5,4},{6,7},{7,6},{8,9},{9,8},{10,11... | collective-permute-start | bytes 393224 | tf_op jit(solution)/shard_map/ppermute | solution.py:299
  2.6 19.9 %collective-permute-start.5 = (bf16[2,128,512]{2,1,0:T(8,128)(2,1)S(1)}, bf16[2,128,512]{2,1,0:T(8,128)(2,1)S(1)}, u32[]{:S(2)}, u32[]{:S(2)}) collective-permute-start(bf16[2,128,512]{2,1,0:T(8,128)(2,1)S(1)} %get-tuple-element.47), channel_id=1, source_target_pairs={{0,1},{1,0},{2,3},{3,2},{4,5},{5,4},{6,7},{7,6},{8,9},{9,8},{10,11... | collective-permute-start | bytes 786440 | tf_op jit(solution)/shard_map/ppermute | solution.py:322
  3.8 7.6 %collective-permute-start.4 = (bf16[256,256]{1,0:T(8,128)(2,1)S(1)}, bf16[256,256]{1,0:T(8,128)(2,1)S(1)}, u32[]{:S(2)}, u32[]{:S(2)}) collective-permute-start(bf16[256,256]{1,0:T(8,128)(2,1)S(1)} %shard_map.74.refs_0_), channel_id=1, source_target_pairs={{0,2},{1,3},{2,0},{3,1},{4,6},{5,7},{6,4},{7,5},{8,10},{9,11},{10,... | collective-permute-start | bytes 393224 | tf_op jit(solution)/shard_map/ppermute | solution.py:299
  7.3 17.9 %collective-permute-start.7 = (bf16[2,128,512]{2,1,0:T(8,128)(2,1)S(1)}, bf16[2,128,512]{2,1,0:T(8,128)(2,1)S(1)}, u32[]{:S(2)}, u32[]{:S(2)}) collective-permute-start(bf16[2,128,512]{2,1,0:T(8,128)(2,1)S(1)} %get-tuple-element.52), channel_id=1, source_target_pairs={{0,31},{1,2},{2,1},{3,4},{4,3},{5,6},{6,5},{7,8},{8,7},{9,10},{10,... | collective-permute-start | bytes 786440 | tf_op jit(solution)/shard_map/ppermute | solution.py:348
  11.4 6.7 %collective-permute-start.2 = (bf16[256,256]{1,0:T(8,128)(2,1)S(1)}, bf16[256,256]{1,0:T(8,128)(2,1)S(1)}, u32[]{:S(2)}, u32[]{:S(2)}) collective-permute-start(bf16[256,256]{1,0:T(8,128)(2,1)S(1)} %shard_map.75.refs_1_), channel_id=1, source_target_pairs={{0,2},{1,3},{2,0},{3,1},{4,6},{5,7},{6,4},{7,5},{8,10},{9,11},{10,... | collective-permute-start | bytes 393224 | tf_op jit(solution)/shard_map/ppermute | solution.py:299
  11.6 13.6 %collective-permute-start.6 = (bf16[256,256]{1,0:T(8,128)(2,1)S(1)}, bf16[256,256]{1,0:T(8,128)(2,1)S(1)}, u32[]{:S(2)}, u32[]{:S(2)}) collective-permute-start(bf16[256,256]{1,0:T(8,128)(2,1)S(1)} %shard_map.78.refs_0_), channel_id=1, source_target_pairs={{0,4},{1,5},{2,6},{3,7},{4,0},{5,1},{6,2},{7,3},{8,12},{9,13},{10,... | collective-permute-start | bytes 393224 | tf_op jit(solution)/shard_map/ppermute | solution.py:299
  18.4 8.1 %collective-permute-start.3 = (bf16[256,256]{1,0:T(8,128)(2,1)S(1)}, bf16[256,256]{1,0:T(8,128)(2,1)S(1)}, u32[]{:S(2)}, u32[]{:S(2)}) collective-permute-start(bf16[256,256]{1,0:T(8,128)(2,1)S(1)} %shard_map.77.refs_1_), channel_id=1, source_target_pairs={{0,4},{1,5},{2,6},{3,7},{4,0},{5,1},{6,2},{7,3},{8,12},{9,13},{10,... | collective-permute-start | bytes 393224 | tf_op jit(solution)/shard_map/ppermute | solution.py:299
  21.0 1.5 %copy-start = (s32[32,6,3]{0,2,1:T(4,128)S(1)}, s32[32,6,3]{0,2,1:T(4,128)}, u32[]{:S(2)}) copy-start(s32[32,6,3]{0,2,1:T(4,128)} %param.13) | copy-start | bytes 6916

commit v5 on v4

--- a/solution.py
+++ b/solution.py
@@ -137,19 +137,20 @@
         copy.wait()
 
 
-def rest_body(level, self_hbm, cross_hbm, basis_hbm, tiles_hbm, map_ref, basis_ref, tiles_ref, sems):
-    fetches = Fetches(sems)
-    copies = fetches.maps(level, self_hbm, cross_hbm, map_ref)
-    copies += fetches.side_by_side(basis_hbm, basis_ref)
-    copies.append(fetches.start(tiles_hbm, tiles_ref))
-    for copy in copies:
-        copy.wait()
-
-
-def both_body(coef_ref, partner_ref, map_ref, out_ref):
-    out_ref[...] = dot(map_ref[...], stacked(coef_ref[...], partner_ref[...])).astype(
-        out_ref.dtype
-    )
+def rest_body(axis, turn, level, *refs):
+    self_hbm, cross_hbm, basis_hbm, tiles_hbm = refs[:4]
+    map_ref, basis_ref, tiles_ref, sems = refs[-4:]
+    here = lax.axis_index(axis)
+    early = jnp.logical_and(lax.rem(here, 2) == 0, here > 0)
+
+    @pl.when(early if turn == 0 else jnp.logical_not(early))
+    def _():
+        fetches = Fetches(sems)
+        copies = fetches.maps(level, self_hbm, cross_hbm, map_ref)
+        copies += fetches.side_by_side(basis_hbm, basis_ref)
+        copies.append(fetches.start(tiles_hbm, tiles_ref))
+        for copy in copies:
+            copy.wait()
 
 
 def own_body(*refs):
@@ -299,6 +300,31 @@
             found.append(lax.ppermute(coef[c], axis, [(i, i ^ (1 << level)) for i in range(count)]))
         return found
 
+    def own_products(level_maps, coef):
+        return call(
+            own_body,
+            totals,
+            [ON_CHIP] * (CHUNKS + 1),
+            (*coef, level_maps),
+            8 * rank * rank * width,
+            2 * rank * rank,
+        )
+
+    def rest(turn, after, before=()):
+        late = lax.optimization_barrier(
+            (self_transfer, cross_transfer, out_basis, near_tiles, after)
+        )
+        return call(
+            functools.partial(rest_body, axis, turn, levels - 1),
+            [maps, pltpu.VMEM((rows, 2 * rank), bf16), pltpu.VMEM(near_tiles.shape, bf16)],
+            [OFF_CHIP] * 4 + [ON_CHIP] * len(before),
+            (*[held(a) for a in late[:4]], *before),
+            8 * rank * rank * rank,
+            8 * rank * rank,
+            scratch=[pltpu.SemaphoreType.DMA((7,))],
+            aliases={4 + k: k for k in range(len(before))},
+        )
+
     self_transfer, cross_transfer = held(self_transfer), held(cross_transfer)
     listing = near_list.transpose(1, 2, 0)
     first = call(
@@ -320,27 +346,18 @@
 
     partner = swaps(0, coef)
     pair = lax.ppermute(to_pair, axis, pairs)
+    own = own_products(maps0, coef)
     coef = [
         call(
-            both_body,
+            cross_body,
             [pieces[c]],
             [ON_CHIP] * 3,
-            (coef[c], partner[c], maps0),
+            (own[c], partner[c], maps0),
             8 * rank * rank * sizes[c],
             4 * rank * rank,
         )[0]
         for c in range(CHUNKS)
     ]
-
-    def own_products(level_maps, coef):
-        return call(
-            own_body,
-            totals,
-            [ON_CHIP] * (CHUNKS + 1),
-            (*coef, level_maps),
-            8 * rank * rank * width,
-            2 * rank * rank,
-        )
 
     partner = swaps(1, coef)
     own = own_products(maps1, coef)
@@ -357,18 +374,7 @@
         )[0]
         for c in range(CHUNKS)
     ]
-    self_last, cross_last, out_basis, near_tiles, _ = lax.optimization_barrier(
-        (self_transfer, cross_transfer, out_basis, near_tiles, own[0])
-    )
-    maps2, basis, tiles = call(
-        functools.partial(rest_body, levels - 1),
-        [maps, pltpu.VMEM((rows, 2 * rank), bf16), pltpu.VMEM(near_tiles.shape, bf16)],
-        [OFF_CHIP] * 4,
-        (held(self_last), held(cross_last), held(out_basis), held(near_tiles)),
-        8 * rank * rank * rank,
-        8 * rank * rank,
-        scratch=[pltpu.SemaphoreType.DMA((7,))],
-    )
+    maps2, basis, tiles = rest(1, coef[0], rest(0, own[0]))
     partner = swaps(2, coef)
     near, side = call(
         functools.partial(near_body, axis, count),

time: 27.8 us -> 27.8 us (level)
    pallas_call x11 -> x13, Pallas kernels: 9.8 us -> 10 us  [call(): pl.pallas_call(body, out_shape=outs, in_specs=ins, out_specs=outs_at or [...]
where the time goes in v5:
time: 27.8 us; the launch traced here: 27.6 us
  starting transfers between devices  11.6 us (42%)
  Pallas kernels  10 us (36%)
  waiting for transfers between devices  5.8 us (21%)
    pallas_call x13, Pallas kernels, call(): pl.pallas_call(body, out_shape=outs, in_specs=ins, out_specs=outs_at or [...  10 us
    ppermute x6, starting transfers between devices, swaps(): lax.ppermute(coef[c], axis, [(i, i ^ 1 << level) for i in range(count)])  7.14 us
    ppermute x6, waiting for transfers between devices, swaps(): lax.ppermute(coef[c], axis, [(i, i ^ 1 << level) for i in range(count)])  5.79 us
    ppermute x1, starting transfers between devices, per_device(): other = lax.ppermute(to_other, axis, others)  4.06 us
  transfers between devices with their start and end apart: 8, of which 2 were waited for; matrix products, arithmetic and copies ran while one was open for 0% of the time, Pallas kernels for 25%

profile of v5, /device:TPU:0, one launch (start us, length us, event | category | flops | bytes accessed | tf_op | source)
XLA Modules:
  0.0 27.6 jit_solution(10604683060546100341)
XLA Ops:
  0.0 1.9 %shard_map.73 = (bf16[256,256]{1,0:T(8,128)(2,1)S(1)}, bf16[256,256]{1,0:T(8,128)(2,1)S(1)}, bf16[512,512]{1,0:T(8,128)(2,1)S(1)}, bf16[2,128,512]{2,1,0:T(8,128...) custom-call(f32[2,512,256]{2,1,0:T(8,128)} %refs_0_.1, ...), custom_call_target="tpu_custom_call" | custom-call | flops 268435456 | bytes 1048576 | tf_op jit(solution)/shard_map/pallas_call | solution.py:21
  1.9 0.6 %collective-permute-start = (bf16[256,256]{1,0:T(8,128)(2,1)S(1)}, bf16[256,256]{1,0:T(8,128)(2,1)S(1)}, u32[]{:S(2)}, u32[]{:S(2)}) collective-permute-start(bf16[256,256]{1,0:T(8,128)(2,1)S(1)} %get-tuple-element.40.refs_0_), channel_id=1, source_target_pairs={{0,1},{1,0},{2,3},{3,2},{4,5},{5,4},{6,7},{7,6},{8,9},{9,8},{10,11... | collective-permute-start | bytes 393224 | tf_op jit(solution)/shard_map/ppermute | solution.py:300
  2.5 0.1 collective-permute-start.1
  2.6 0.4 %collective-permute-start.5 = (bf16[2,128,512]{2,1,0:T(8,128)(2,1)S(1)}, bf16[2,128,512]{2,1,0:T(8,128)(2,1)S(1)}, u32[]{:S(2)}, u32[]{:S(2)}) collective-permute-start(bf16[2,128,512]{2,1,0:T(8,128)(2,1)S(1)} %get-tuple-element.65), channel_id=1, source_target_pairs={{0,1},{1,0},{2,3},{3,2},{4,5},{5,4},{6,7},{7,6},{8,9},{9,8},{10,11... | collective-permute-start | bytes 786440 | tf_op jit(solution)/shard_map/ppermute | solution.py:348
  3.0 0.3 %shard_map.74 = (f32[256,256]{1,0:T(8,128)S(1)}, f32[256,256]{1,0:T(8,128)S(1)}) custom-call(bf16[256,256]{1,0:T(8,128)(2,1)S(1)} %get-tuple-element.40.refs_0_, bf16[256,256]{1,0:T(8,128)(2,1)S(1)} %get-tuple-element.41.refs_1_, bf16[256,1024]{1,0:T(8,128)(2,1)S(1)} %get-tuple-element.42.refs_2_.map_ref), custom_call_target="tpu_custom_call" | custom-call | flops 134217728 | bytes 131072 | tf_op jit(solution)/shard_map/pallas_call | solution.py:21
  3.3 0.2 collective-permute-done.partner_ref
  3.5 0.2 shard_map.75.refs_0_
  3.7 2.9 %collective-permute-start.4 = (bf16[256,256]{1,0:T(8,128)(2,1)S(1)}, bf16[256,256]{1,0:T(8,128)(2,1)S(1)}, u32[]{:S(2)}, u32[]{:S(2)}) collective-permute-start(bf16[256,256]{1,0:T(8,128)(2,1)S(1)} %shard_map.75.refs_0_), channel_id=1, source_target_pairs={{0,2},{1,3},{2,0},{3,1},{4,6},{5,7},{6,4},{7,5},{8,10},{9,11},{10,... | collective-permute-start | bytes 393224 | tf_op jit(solution)/shard_map/ppermute | solution.py:300
  6.6 0.0 collective-permute-done.1.partner_ref
  6.6 0.2 shard_map.76.refs_1_
  6.9 0.3 %shard_map.77 = (f32[256,256]{1,0:T(8,128)S(1)}, f32[256,256]{1,0:T(8,128)S(1)}) custom-call(bf16[256,256]{1,0:T(8,128)(2,1)S(1)} %shard_map.75.refs_0_, bf16[256,256]{1,0:T(8,128)(2,1)S(1)} %shard_map.76.refs_1_, bf16[256,1024]{1,0:T(8,128)(2,1)S(1)} %get-tuple-element.45.refs_2_.map_ref), custom_call_target="tpu_custom_call" | custom-call | flops 134217728 | bytes 131072 | tf_op jit(solution)/shard_map/pallas_call | solution.py:21
  7.2 4.1 %collective-permute-start.7 = (bf16[2,128,512]{2,1,0:T(8,128)(2,1)S(1)}, bf16[2,128,512]{2,1,0:T(8,128)(2,1)S(1)}, u32[]{:S(2)}, u32[]{:S(2)}) collective-permute-start(bf16[2,128,512]{2,1,0:T(8,128)(2,1)S(1)} %get-tuple-element.70), channel_id=1, source_target_pairs={{0,31},{1,2},{2,1},{3,4},{4,3},{5,6},{6,5},{7,8},{8,7},{9,10},{10,... | collective-permute-start | bytes 786440 | tf_op jit(solution)/shard_map/ppermute | solution.py:365
  11.2 0.0 collective-permute-start.2
  11.2 0.0 collective-permute-done.4.partner_ref
  11.2 0.2 shard_map.79.refs_0_
  11.5 1.0 %collective-permute-start.6 = (bf16[256,256]{1,0:T(8,128)(2,1)S(1)}, bf16[256,256]{1,0:T(8,128)(2,1)S(1)}, u32[]{:S(2)}, u32[]{:S(2)}) collective-permute-start(bf16[256,256]{1,0:T(8,128)(2,1)S(1)} %shard_map.79.refs_0_), channel_id=1, source_target_pairs={{0,4},{1,5},{2,6},{3,7},{4,0},{5,1},{6,2},{7,3},{8,12},{9,13},{10,... | collective-permute-start | bytes 393224 | tf_op jit(solution)/shard_map/ppermute | solution.py:300
  12.5 5.6 %collective-permute-done.2.partner_ref = bf16[256,256]{1,0:T(8,128)(2,1)S(1)} collective-permute-done((bf16[256,256]{1,0:T(8,128)(2,1)S(1)}, bf16[256,256]{1,0:T(8,128)(2,1)S(1)}, u32[]{:S(2)}, u32[]{:S(2)}) %collective-permute-start.2) | collective-permute-done | bytes 131104 | tf_op jit(solution)/shard_map/ppermute | solution.py:300
  18.1 0.2 shard_map.78.refs_1_
  18.4 2.6 %collective-permute-start.3 = (bf16[256,256]{1,0:T(8,128)(2,1)S(1)}, bf16[256,256]{1,0:T(8,128)(2,1)S(1)}, u32[]{:S(2)}, u32[]{:S(2)}) collective-permute-start(bf16[256,256]{1,0:T(8,128)(2,1)S(1)} %shard_map.78.refs_1_), channel_id=1, source_target_pairs={{0,4},{1,5},{2,6},{3,7},{4,0},{5,1},{6,2},{7,3},{8,12},{9,13},{10,... | collective-permute-start | bytes 393224 | tf_op jit(solution)/shard_map/ppermute | solution.py:300
  20.9 0.1 shard_map.80
  21.0 0.0 copy-start
  21.0 1.5 %shard_map.81 = (bf16[256,1024]{1,0:T(8,128)(2,1)S(1)}, bf16[512,512]{1,0:T(8,128)(2,1)S(1)}, bf16[6,2,128,128]{3,2,1,0:T(8,128)(2,1)S(1)}) custom-call(bf16[3,2,256,256]{3,2,1,0:T(8,128)(2,1)} %refs_0_.3, bf16[3,2,256,256]{3,2,1,0:T(8,128)(2,1)} %refs_1_.3, ...), custom_call_target="tpu_custom_call", output_to_operand_aliasing={{0}: (4, {}), {1}: (5, {}), {2}: (6, {})} | custom-call | flops 134217728 | bytes 524288 | tf_op jit(solution)/shard_map/pallas_call | solution.py:21
  22.5 0.0 collective-permute-done.5.pair_ref
  22.5 0.0 copy-done
  22.5 1.6 %shard_map.82 = (f32[512,512]{1,0:T(8,128)S(1)}, bf16[512,512]{1,0:T(8,128)(2,1)S(1)}) custom-call(s32[6,3,32]{2,1,0:T(4,128)S(1)} %bitcast.2, bf16[6,2,128,128]{3,2,1,0:T(8,128)(2,1)S(1)} %get-tuple-element.63.tiles_ref, bf16[512,512]{1,0:T(8,128)(2,1)S(1)} %get-tuple-element.64.xb_ref, bf16[2,128,512]{2,1,0:T(8,128)(2,1)S(1)} %collective-permute-done.5.pair_ref), custom_call_target="tpu_custom_call" | custom-call | flops 201326592 | bytes 1048576 | tf_op jit(solution)/shard_map/pallas_call | solution.py:21
  24.2 1.1 %shard_map.83 = (f32[512,512]{1,0:T(8,128)S(1)}, bf16[512,512]{1,0:T(8,128)(2,1)S(1)}) custom-call(bf16[256,256]{1,0:T(8,128)(2,1)S(1)} %shard_map.79.refs_0_, bf16[256,256]{1,0:T(8,128)(2,1)S(1)} %shard_map.78.refs_1_, bf16[256,1024]{1,0:T(8,128)(2,1)S(1)} %get-tuple-element.61.refs_2_, bf16[512,512]{1,0:T(8,128)(2,1)S(1)} %get-tuple-element.62.refs_3_, ...), custom_call_target="tpu_custom_call" | custom-call | flops 536870912 | bytes 1048576 | tf_op jit(solution)/shard_map/pallas_call | solution.py:21
  25.3 0.0 collective-permute-done.6.partner_ref
  25.3 0.0 collective-permute-done.7.other_ref
  25.3 1.2 %shard_map.84 = (f32[2,512,256]{2,1,0:T(8,128)}, f32[512,256]{1,0:T(8,128)S(1)}) custom-call(bf16[256,256]{1,0:T(8,128)(2,1)S(1)} %collective-permute-done.6.partner_ref, bf16[512,512]{1,0:T(8,128)(2,1)S(1)} %get-tuple-element.67.fold_ref, f32[512,512]{1,0:T(8,128)S(1)} %get-tuple-element.68.base_ref, bf16[512,512]{1,0:T(8,128)(2,1)S(1)} %get-tuple-element.69.side_ref, ...), custom_call_target="tpu_custom_call" | custom-call | flops 402653184 | bytes 1048576 | tf_op jit(solution)/shard_map/pallas_call | solution.py:21
  26.5 0.0 collective-permute-done.3.partner_ref
  26.5 1.1 %shard_map.85 = f32[2,512,256]{2,1,0:T(8,128)} custom-call(bf16[256,256]{1,0:T(8,128)(2,1)S(1)} %collective-permute-done.3.partner_ref, bf16[512,512]{1,0:T(8,128)(2,1)S(1)} %get-tuple-element.67.fold_ref, f32[512,256]{1,0:T(8,128)S(1)} %get-tuple-element.71.left_ref, f32[2,512,256]{2,1,0:T(8,128)} %get-tuple-element.72.before_hbm), custom_call_target="tpu_custom_call", output_to_operand_aliasing={{}: (3, {})} | custom-call | flops 67108864 | bytes 524288 | tf_op jit(solution)/shard_map/pallas_call | solution.py:21
Async XLA Ops:
  1.9 1.5 %collective-permute-start = (bf16[256,256]{1,0:T(8,128)(2,1)S(1)}, bf16[256,256]{1,0:T(8,128)(2,1)S(1)}, u32[]{:S(2)}, u32[]{:S(2)}) collective-permute-start(bf16[256,256]{1,0:T(8,128)(2,1)S(1)} %get-tuple-element.40.refs_0_), channel_id=1, source_target_pairs={{0,1},{1,0},{2,3},{3,2},{4,5},{5,4},{6,7},{7,6},{8,9},{9,8},{10,11... | collective-permute-start | bytes 393224 | tf_op jit(solution)/shard_map/ppermute | solution.py:300
  2.5 4.1 %collective-permute-start.1 = (bf16[256,256]{1,0:T(8,128)(2,1)S(1)}, bf16[256,256]{1,0:T(8,128)(2,1)S(1)}, u32[]{:S(2)}, u32[]{:S(2)}) collective-permute-start(bf16[256,256]{1,0:T(8,128)(2,1)S(1)} %get-tuple-element.41.refs_1_), channel_id=1, source_target_pairs={{0,1},{1,0},{2,3},{3,2},{4,5},{5,4},{6,7},{7,6},{8,9},{9,8},{10,11... | collective-permute-start | bytes 393224 | tf_op jit(solution)/shard_map/ppermute | solution.py:300
  2.6 19.9 %collective-permute-start.5 = (bf16[2,128,512]{2,1,0:T(8,128)(2,1)S(1)}, bf16[2,128,512]{2,1,0:T(8,128)(2,1)S(1)}, u32[]{:S(2)}, u32[]{:S(2)}) collective-permute-start(bf16[2,128,512]{2,1,0:T(8,128)(2,1)S(1)} %get-tuple-element.65), channel_id=1, source_target_pairs={{0,1},{1,0},{2,3},{3,2},{4,5},{5,4},{6,7},{7,6},{8,9},{9,8},{10,11... | collective-permute-start | bytes 786440 | tf_op jit(solution)/shard_map/ppermute | solution.py:348
  3.7 7.5 %collective-permute-start.4 = (bf16[256,256]{1,0:T(8,128)(2,1)S(1)}, bf16[256,256]{1,0:T(8,128)(2,1)S(1)}, u32[]{:S(2)}, u32[]{:S(2)}) collective-permute-start(bf16[256,256]{1,0:T(8,128)(2,1)S(1)} %shard_map.75.refs_0_), channel_id=1, source_target_pairs={{0,2},{1,3},{2,0},{3,1},{4,6},{5,7},{6,4},{7,5},{8,10},{9,11},{10,... | collective-permute-start | bytes 393224 | tf_op jit(solution)/shard_map/ppermute | solution.py:300
  7.2 18.1 %collective-permute-start.7 = (bf16[2,128,512]{2,1,0:T(8,128)(2,1)S(1)}, bf16[2,128,512]{2,1,0:T(8,128)(2,1)S(1)}, u32[]{:S(2)}, u32[]{:S(2)}) collective-permute-start(bf16[2,128,512]{2,1,0:T(8,128)(2,1)S(1)} %get-tuple-element.70), channel_id=1, source_target_pairs={{0,31},{1,2},{2,1},{3,4},{4,3},{5,6},{6,5},{7,8},{8,7},{9,10},{10,... | collective-permute-start | bytes 786440 | tf_op jit(solution)/shard_map/ppermute | solution.py:365
  11.2 6.9 %collective-permute-start.2 = (bf16[256,256]{1,0:T(8,128)(2,1)S(1)}, bf16[256,256]{1,0:T(8,128)(2,1)S(1)}, u32[]{:S(2)}, u32[]{:S(2)}) collective-permute-start(bf16[256,256]{1,0:T(8,128)(2,1)S(1)} %shard_map.76.refs_1_), channel_id=1, source_target_pairs={{0,2},{1,3},{2,0},{3,1},{4,6},{5,7},{6,4},{7,5},{8,10},{9,11},{10,... | collective-permute-start | bytes 393224 | tf_op jit(solution)/shard_map/ppermute | solution.py:300
  11.5 13.8 %collective-permute-start.6 = (bf16[256,256]{1,0:T(8,128)(2,1)S(1)}, bf16[256,256]{1,0:T(8,128)(2,1)S(1)}, u32[]{:S(2)}, u32[]{:S(2)}) collective-permute-start(bf16[256,256]{1,0:T(8,128)(2,1)S(1)} %shard_map.79.refs_0_), channel_id=1, source_target_pairs={{0,4},{1,5},{2,6},{3,7},{4,0},{5,1},{6,2},{7,3},{8,12},{9,13},{10,... | collective-permute-start | bytes 393224 | tf_op jit(solution)/shard_map/ppermute | solution.py:300
  18.4 8.2 %collective-permute-start.3 = (bf16[256,256]{1,0:T(8,128)(2,1)S(1)}, bf16[256,256]{1,0:T(8,128)(2,1)S(1)}, u32[]{:S(2)}, u32[]{:S(2)}) collective-permute-start(bf16[256,256]{1,0:T(8,128)(2,1)S(1)} %shard_map.78.refs_1_), channel_id=1, source_target_pairs={{0,4},{1,5},{2,6},{3,7},{4,0},{5,1},{6,2},{7,3},{8,12},{9,13},{10,... | collective-permute-start | bytes 393224 | tf_op jit(solution)/shard_map/ppermute | solution.py:300
  21.0 1.5 %copy-start = (s32[32,6,3]{0,2,1:T(4,128)S(1)}, s32[32,6,3]{0,2,1:T(4,128)}, u32[]{:S(2)}) copy-start(s32[32,6,3]{0,2,1:T(4,128)} %param.13) | copy-start | bytes 6916

commit v6 on v5

--- a/solution.py
+++ b/solution.py
@@ -143,11 +143,15 @@
     here = lax.axis_index(axis)
     early = jnp.logical_and(lax.rem(here, 2) == 0, here > 0)
 
+    fetches = Fetches(sems)
+
     @pl.when(early if turn == 0 else jnp.logical_not(early))
     def _():
-        fetches = Fetches(sems)
-        copies = fetches.maps(level, self_hbm, cross_hbm, map_ref)
-        copies += fetches.side_by_side(basis_hbm, basis_ref)
+        for copy in fetches.maps(level, self_hbm, cross_hbm, map_ref):
+            copy.wait()
+
+    if turn:
+        copies = fetches.side_by_side(basis_hbm, basis_ref)
         copies.append(fetches.start(tiles_hbm, tiles_ref))
         for copy in copies:
             copy.wait()
@@ -361,7 +365,8 @@
 
     partner = swaps(1, coef)
     own = own_products(maps1, coef)
-    to_other, *own = lax.optimization_barrier((to_other, *own))
+    loaded = rest(0, own[0])
+    to_other, *loaded = lax.optimization_barrier((to_other, *loaded))
     other = lax.ppermute(to_other, axis, others)
     coef = [
         call(
@@ -374,7 +379,7 @@
         )[0]
         for c in range(CHUNKS)
     ]
-    maps2, basis, tiles = rest(1, coef[0], rest(0, own[0]))
+    maps2, basis, tiles = rest(1, coef[0], loaded)
     partner = swaps(2, coef)
     near, side = call(
         functools.partial(near_body, axis, count),

time: 27.8 us -> 28.6 us (1.029)
  Pallas kernels: 10 us -> 10.9 us
  waiting for transfers between devices: 5.8 us -> 5.39 us
  starting transfers between devices: 11.6 us -> 11.9 us
    pallas_call x13, Pallas kernels: 10 us -> 10.9 us  [call(): pl.pallas_call(body, out_shape=outs, in_specs=ins, out_specs=outs_at or [...]
    ppermute x6, waiting for transfers between devices: 5.79 us -> 5.39 us  [swaps(): lax.ppermute(coef[c], axis, [(i, i ^ 1 << level) for i in range(count)])]
    ppermute x6, starting transfers between devices: 7.14 us -> 7.44 us  [swaps(): lax.ppermute(coef[c], axis, [(i, i ^ 1 << level) for i in range(count)])]
  transfers between devices with their start and end apart: 8 -> 8, of which waited for: 2 -> 2; matrix products, arithmetic and copies ran while one was open for 0% -> 0% of each run, Pallas kernels for 25% -> 28%
where the time goes in v6:
time: 28.6 us; the launch traced here: 28.4 us
  starting transfers between devices  11.9 us (42%)
  Pallas kernels  10.9 us (38%)
  waiting for transfers between devices  5.39 us (19%)
    pallas_call x13, Pallas kernels, call(): pl.pallas_call(body, out_shape=outs, in_specs=ins, out_specs=outs_at or [...  10.9 us
    ppermute x6, starting transfers between devices, swaps(): lax.ppermute(coef[c], axis, [(i, i ^ 1 << level) for i in range(count)])  7.44 us
    ppermute x6, waiting for transfers between devices, swaps(): lax.ppermute(coef[c], axis, [(i, i ^ 1 << level) for i in range(count)])  5.39 us
    ppermute x1, starting transfers between devices, per_device(): other = lax.ppermute(to_other, axis, others)  4.06 us
  transfers between devices with their start and end apart: 8, of which 2 were waited for; matrix products, arithmetic and copies ran while one was open for 0% of the time, Pallas kernels for 28%

profile of v6, /device:TPU:0, one launch (start us, length us, event | category | flops | bytes accessed | tf_op | source)
XLA Modules:
  0.0 28.4 jit_solution(8093502889876478657)
XLA Ops:
  0.0 1.9 %shard_map.73 = (bf16[256,256]{1,0:T(8,128)(2,1)S(1)}, bf16[256,256]{1,0:T(8,128)(2,1)S(1)}, bf16[512,512]{1,0:T(8,128)(2,1)S(1)}, bf16[2,128,512]{2,1,0:T(8,128...) custom-call(f32[2,512,256]{2,1,0:T(8,128)} %refs_0_.1, ...), custom_call_target="tpu_custom_call" | custom-call | flops 268435456 | bytes 1048576 | tf_op jit(solution)/shard_map/pallas_call | solution.py:21
  1.9 0.6 %collective-permute-start = (bf16[256,256]{1,0:T(8,128)(2,1)S(1)}, bf16[256,256]{1,0:T(8,128)(2,1)S(1)}, u32[]{:S(2)}, u32[]{:S(2)}) collective-permute-start(bf16[256,256]{1,0:T(8,128)(2,1)S(1)} %get-tuple-element.40.refs_0_), channel_id=1, source_target_pairs={{0,1},{1,0},{2,3},{3,2},{4,5},{5,4},{6,7},{7,6},{8,9},{9,8},{10,11... | collective-permute-start | bytes 393224 | tf_op jit(solution)/shard_map/ppermute | solution.py:304
  2.5 0.1 collective-permute-start.1
  2.6 0.4 %collective-permute-start.5 = (bf16[2,128,512]{2,1,0:T(8,128)(2,1)S(1)}, bf16[2,128,512]{2,1,0:T(8,128)(2,1)S(1)}, u32[]{:S(2)}, u32[]{:S(2)}) collective-permute-start(bf16[2,128,512]{2,1,0:T(8,128)(2,1)S(1)} %get-tuple-element.67), channel_id=1, source_target_pairs={{0,1},{1,0},{2,3},{3,2},{4,5},{5,4},{6,7},{7,6},{8,9},{9,8},{10,11... | collective-permute-start | bytes 786440 | tf_op jit(solution)/shard_map/ppermute | solution.py:352
  3.0 0.3 %shard_map.74 = (f32[256,256]{1,0:T(8,128)S(1)}, f32[256,256]{1,0:T(8,128)S(1)}) custom-call(bf16[256,256]{1,0:T(8,128)(2,1)S(1)} %get-tuple-element.40.refs_0_, bf16[256,256]{1,0:T(8,128)(2,1)S(1)} %get-tuple-element.41.refs_1_, bf16[256,1024]{1,0:T(8,128)(2,1)S(1)} %get-tuple-element.42.refs_2_.map_ref), custom_call_target="tpu_custom_call" | custom-call | flops 134217728 | bytes 131072 | tf_op jit(solution)/shard_map/pallas_call | solution.py:21
  3.3 0.2 collective-permute-done.partner_ref
  3.5 0.2 shard_map.75.refs_0_
  3.7 2.9 %collective-permute-start.4 = (bf16[256,256]{1,0:T(8,128)(2,1)S(1)}, bf16[256,256]{1,0:T(8,128)(2,1)S(1)}, u32[]{:S(2)}, u32[]{:S(2)}) collective-permute-start(bf16[256,256]{1,0:T(8,128)(2,1)S(1)} %shard_map.75.refs_0_), channel_id=1, source_target_pairs={{0,2},{1,3},{2,0},{3,1},{4,6},{5,7},{6,4},{7,5},{8,10},{9,11},{10,... | collective-permute-start | bytes 393224 | tf_op jit(solution)/shard_map/ppermute | solution.py:304
  6.6 0.0 collective-permute-done.1.partner_ref
  6.6 0.2 shard_map.76.refs_1_
  6.9 0.3 %shard_map.77 = (f32[256,256]{1,0:T(8,128)S(1)}, f32[256,256]{1,0:T(8,128)S(1)}) custom-call(bf16[256,256]{1,0:T(8,128)(2,1)S(1)} %shard_map.75.refs_0_, bf16[256,256]{1,0:T(8,128)(2,1)S(1)} %shard_map.76.refs_1_, bf16[256,1024]{1,0:T(8,128)(2,1)S(1)} %get-tuple-element.45.refs_2_.map_ref), custom_call_target="tpu_custom_call" | custom-call | flops 134217728 | bytes 131072 | tf_op jit(solution)/shard_map/pallas_call | solution.py:21
  7.2 0.1 shard_map.80
  7.3 4.1 %collective-permute-start.7 = (bf16[2,128,512]{2,1,0:T(8,128)(2,1)S(1)}, bf16[2,128,512]{2,1,0:T(8,128)(2,1)S(1)}, u32[]{:S(2)}, u32[]{:S(2)}) collective-permute-start(bf16[2,128,512]{2,1,0:T(8,128)(2,1)S(1)} %get-tuple-element.72), channel_id=1, source_target_pairs={{0,31},{1,2},{2,1},{3,4},{4,3},{5,6},{6,5},{7,8},{8,7},{9,10},{10,... | collective-permute-start | bytes 786440 | tf_op jit(solution)/shard_map/ppermute | solution.py:370
  11.3 0.0 collective-permute-start.2
  11.3 0.0 collective-permute-done.4.partner_ref
  11.3 0.2 shard_map.79.refs_0_
  11.6 0.9 %collective-permute-start.6 = (bf16[256,256]{1,0:T(8,128)(2,1)S(1)}, bf16[256,256]{1,0:T(8,128)(2,1)S(1)}, u32[]{:S(2)}, u32[]{:S(2)}) collective-permute-start(bf16[256,256]{1,0:T(8,128)(2,1)S(1)} %shard_map.79.refs_0_), channel_id=1, source_target_pairs={{0,4},{1,5},{2,6},{3,7},{4,0},{5,1},{6,2},{7,3},{8,12},{9,13},{10,... | collective-permute-start | bytes 393224 | tf_op jit(solution)/shard_map/ppermute | solution.py:304
  12.5 5.2 %collective-permute-done.2.partner_ref = bf16[256,256]{1,0:T(8,128)(2,1)S(1)} collective-permute-done((bf16[256,256]{1,0:T(8,128)(2,1)S(1)}, bf16[256,256]{1,0:T(8,128)(2,1)S(1)}, u32[]{:S(2)}, u32[]{:S(2)}) %collective-permute-start.2) | collective-permute-done | bytes 131104 | tf_op jit(solution)/shard_map/ppermute | solution.py:304
  17.7 0.2 shard_map.78.refs_1_
  18.0 3.0 %collective-permute-start.3 = (bf16[256,256]{1,0:T(8,128)(2,1)S(1)}, bf16[256,256]{1,0:T(8,128)(2,1)S(1)}, u32[]{:S(2)}, u32[]{:S(2)}) collective-permute-start(bf16[256,256]{1,0:T(8,128)(2,1)S(1)} %shard_map.78.refs_1_), channel_id=1, source_target_pairs={{0,4},{1,5},{2,6},{3,7},{4,0},{5,1},{6,2},{7,3},{8,12},{9,13},{10,... | collective-permute-start | bytes 393224 | tf_op jit(solution)/shard_map/ppermute | solution.py:304
  20.9 0.0 copy-start
  20.9 2.3 %shard_map.81 = (bf16[256,1024]{1,0:T(8,128)(2,1)S(1)}, bf16[512,512]{1,0:T(8,128)(2,1)S(1)}, bf16[6,2,128,128]{3,2,1,0:T(8,128)(2,1)S(1)}) custom-call(bf16[3,2,256,256]{3,2,1,0:T(8,128)(2,1)} %refs_0_.3, bf16[3,2,256,256]{3,2,1,0:T(8,128)(2,1)} %refs_1_.3, ...), custom_call_target="tpu_custom_call", output_to_operand_aliasing={{0}: (4, {}), {1}: (5, {}), {2}: (6, {})} | custom-call | flops 134217728 | bytes 524288 | tf_op jit(solution)/shard_map/pallas_call | solution.py:21
  23.3 0.0 collective-permute-done.5.pair_ref
  23.3 0.0 copy-done
  23.3 1.6 %shard_map.82 = (f32[512,512]{1,0:T(8,128)S(1)}, bf16[512,512]{1,0:T(8,128)(2,1)S(1)}) custom-call(s32[6,3,32]{2,1,0:T(4,128)S(1)} %bitcast.2, bf16[6,2,128,128]{3,2,1,0:T(8,128)(2,1)S(1)} %get-tuple-element.65.tiles_ref, bf16[512,512]{1,0:T(8,128)(2,1)S(1)} %get-tuple-element.66.xb_ref, bf16[2,128,512]{2,1,0:T(8,128)(2,1)S(1)} %collective-permute-done.5.pair_ref), custom_call_target="tpu_custom_call" | custom-call | flops 201326592 | bytes 1048576 | tf_op jit(solution)/shard_map/pallas_call | solution.py:21
  24.9 1.1 %shard_map.83 = (f32[512,512]{1,0:T(8,128)S(1)}, bf16[512,512]{1,0:T(8,128)(2,1)S(1)}) custom-call(bf16[256,256]{1,0:T(8,128)(2,1)S(1)} %shard_map.79.refs_0_, bf16[256,256]{1,0:T(8,128)(2,1)S(1)} %shard_map.78.refs_1_, bf16[256,1024]{1,0:T(8,128)(2,1)S(1)} %get-tuple-element.63.refs_2_, bf16[512,512]{1,0:T(8,128)(2,1)S(1)} %get-tuple-element.64.refs_3_, ...), custom_call_target="tpu_custom_call" | custom-call | flops 536870912 | bytes 1048576 | tf_op jit(solution)/shard_map/pallas_call | solution.py:21
  26.0 0.0 collective-permute-done.6.partner_ref
  26.0 0.0 collective-permute-done.7.other_ref
  26.1 1.2 %shard_map.84 = (f32[2,512,256]{2,1,0:T(8,128)}, f32[512,256]{1,0:T(8,128)S(1)}) custom-call(bf16[256,256]{1,0:T(8,128)(2,1)S(1)} %collective-permute-done.6.partner_ref, bf16[512,512]{1,0:T(8,128)(2,1)S(1)} %get-tuple-element.69.fold_ref, f32[512,512]{1,0:T(8,128)S(1)} %get-tuple-element.70.base_ref, bf16[512,512]{1,0:T(8,128)(2,1)S(1)} %get-tuple-element.71.side_ref, ...), custom_call_target="tpu_custom_call" | custom-call | flops 402653184 | bytes 1048576 | tf_op jit(solution)/shard_map/pallas_call | solution.py:21
  27.3 0.0 collective-permute-done.3.partner_ref
  27.3 1.1 %shard_map.85 = f32[2,512,256]{2,1,0:T(8,128)} custom-call(bf16[256,256]{1,0:T(8,128)(2,1)S(1)} %collective-permute-done.3.partner_ref, bf16[512,512]{1,0:T(8,128)(2,1)S(1)} %get-tuple-element.69.fold_ref, f32[512,256]{1,0:T(8,128)S(1)} %get-tuple-element.73.left_ref, f32[2,512,256]{2,1,0:T(8,128)} %get-tuple-element.74.before_hbm), custom_call_target="tpu_custom_call", output_to_operand_aliasing={{}: (3, {})} | custom-call | flops 67108864 | bytes 524288 | tf_op jit(solution)/shard_map/pallas_call | solution.py:21
Async XLA Ops:
  1.9 1.5 %collective-permute-start = (bf16[256,256]{1,0:T(8,128)(2,1)S(1)}, bf16[256,256]{1,0:T(8,128)(2,1)S(1)}, u32[]{:S(2)}, u32[]{:S(2)}) collective-permute-start(bf16[256,256]{1,0:T(8,128)(2,1)S(1)} %get-tuple-element.40.refs_0_), channel_id=1, source_target_pairs={{0,1},{1,0},{2,3},{3,2},{4,5},{5,4},{6,7},{7,6},{8,9},{9,8},{10,11... | collective-permute-start | bytes 393224 | tf_op jit(solution)/shard_map/ppermute | solution.py:304
  2.5 4.1 %collective-permute-start.1 = (bf16[256,256]{1,0:T(8,128)(2,1)S(1)}, bf16[256,256]{1,0:T(8,128)(2,1)S(1)}, u32[]{:S(2)}, u32[]{:S(2)}) collective-permute-start(bf16[256,256]{1,0:T(8,128)(2,1)S(1)} %get-tuple-element.41.refs_1_), channel_id=1, source_target_pairs={{0,1},{1,0},{2,3},{3,2},{4,5},{5,4},{6,7},{7,6},{8,9},{9,8},{10,11... | collective-permute-start | bytes 393224 | tf_op jit(solution)/shard_map/ppermute | solution.py:304
  2.6 20.7 %collective-permute-start.5 = (bf16[2,128,512]{2,1,0:T(8,128)(2,1)S(1)}, bf16[2,128,512]{2,1,0:T(8,128)(2,1)S(1)}, u32[]{:S(2)}, u32[]{:S(2)}) collective-permute-start(bf16[2,128,512]{2,1,0:T(8,128)(2,1)S(1)} %get-tuple-element.67), channel_id=1, source_target_pairs={{0,1},{1,0},{2,3},{3,2},{4,5},{5,4},{6,7},{7,6},{8,9},{9,8},{10,11... | collective-permute-start | bytes 786440 | tf_op jit(solution)/shard_map/ppermute | solution.py:352
  3.7 7.6 %collective-permute-start.4 = (bf16[256,256]{1,0:T(8,128)(2,1)S(1)}, bf16[256,256]{1,0:T(8,128)(2,1)S(1)}, u32[]{:S(2)}, u32[]{:S(2)}) collective-permute-start(bf16[256,256]{1,0:T(8,128)(2,1)S(1)} %shard_map.75.refs_0_), channel_id=1, source_target_pairs={{0,2},{1,3},{2,0},{3,1},{4,6},{5,7},{6,4},{7,5},{8,10},{9,11},{10,... | collective-permute-start | bytes 393224 | tf_op jit(solution)/shard_map/ppermute | solution.py:304
  7.3 18.8 %collective-permute-start.7 = (bf16[2,128,512]{2,1,0:T(8,128)(2,1)S(1)}, bf16[2,128,512]{2,1,0:T(8,128)(2,1)S(1)}, u32[]{:S(2)}, u32[]{:S(2)}) collective-permute-start(bf16[2,128,512]{2,1,0:T(8,128)(2,1)S(1)} %get-tuple-element.72), channel_id=1, source_target_pairs={{0,31},{1,2},{2,1},{3,4},{4,3},{5,6},{6,5},{7,8},{8,7},{9,10},{10,... | collective-permute-start | bytes 786440 | tf_op jit(solution)/shard_map/ppermute | solution.py:370
  11.3 6.4 %collective-permute-start.2 = (bf16[256,256]{1,0:T(8,128)(2,1)S(1)}, bf16[256,256]{1,0:T(8,128)(2,1)S(1)}, u32[]{:S(2)}, u32[]{:S(2)}) collective-permute-start(bf16[256,256]{1,0:T(8,128)(2,1)S(1)} %shard_map.76.refs_1_), channel_id=1, source_target_pairs={{0,2},{1,3},{2,0},{3,1},{4,6},{5,7},{6,4},{7,5},{8,10},{9,11},{10,... | collective-permute-start | bytes 393224 | tf_op jit(solution)/shard_map/ppermute | solution.py:304
  11.6 14.4 %collective-permute-start.6 = (bf16[256,256]{1,0:T(8,128)(2,1)S(1)}, bf16[256,256]{1,0:T(8,128)(2,1)S(1)}, u32[]{:S(2)}, u32[]{:S(2)}) collective-permute-start(bf16[256,256]{1,0:T(8,128)(2,1)S(1)} %shard_map.79.refs_0_), channel_id=1, source_target_pairs={{0,4},{1,5},{2,6},{3,7},{4,0},{5,1},{6,2},{7,3},{8,12},{9,13},{10,... | collective-permute-start | bytes 393224 | tf_op jit(solution)/shard_map/ppermute | solution.py:304
  18.0 9.3 %collective-permute-start.3 = (bf16[256,256]{1,0:T(8,128)(2,1)S(1)}, bf16[256,256]{1,0:T(8,128)(2,1)S(1)}, u32[]{:S(2)}, u32[]{:S(2)}) collective-permute-start(bf16[256,256]{1,0:T(8,128)(2,1)S(1)} %shard_map.78.refs_1_), channel_id=1, source_target_pairs={{0,4},{1,5},{2,6},{3,7},{4,0},{5,1},{6,2},{7,3},{8,12},{9,13},{10,... | collective-permute-start | bytes 393224 | tf_op jit(solution)/shard_map/ppermute | solution.py:304
  20.9 2.3 %copy-start = (s32[32,6,3]{0,2,1:T(4,128)S(1)}, s32[32,6,3]{0,2,1:T(4,128)}, u32[]{:S(2)}) copy-start(s32[32,6,3]{0,2,1:T(4,128)} %param.13) | copy-start | bytes 6916
